TPU v7x, 32 devices: a whole 2x2x4 slice. The times are simulated.
32 devices in a mesh: dp: 2 (over x), tp: 4 (over z), cp: 4 (over y, core).
Axes of the slice: x: 2, y: 2, z: 4, core: 2. Of those that a mesh axis runs over, the one named last changes fastest.
Arguments:
- x: bfloat16 [8192, 4096], P(('dp', 'cp')), parts along dimension 0
- doc_id: int32 [8192], P(('dp', 'cp')), parts along dimension 0
- pos_in_doc: int32 [8192], P(('dp', 'cp')), parts along dimension 0
- norm_gain: float32 [4096], replicated
- w_q: bfloat16 [4096, 4096], P(None, 'tp')
- w_k: bfloat16 [4096, 1024], P(None, 'tp')
- w_v: bfloat16 [4096, 1024], P(None, 'tp')
- w_o: bfloat16 [4096, 4096], P('tp')
- inv_freq: float32 [64], replicated
Outputs:
- output 1: bfloat16 [8192, 4096], P(('dp', 'cp')), parts along dimension 0
- output 2: bfloat16 [8192, 8, 128], P(('dp', 'cp'), 'tp'), parts along dimension 0
- output 3: bfloat16 [8192, 8, 128], P(('dp', 'cp'), 'tp'), parts along dimension 0
There are 2 independent parts. A program takes and returns all parts, laid end to end along the dimension named above; an argument that names none is the same for every part.
All inputs are finite; a program needn't handle non-finite values.
Results may differ from a plain program's by a relative error of at most 0.00397746.
Values are sent between devices in bfloat16 or wider.
A program may use at most 1 GiB of HBM per device.

v0:
```python
import jax
import jax.numpy as jnp
from jax import lax
from jax.sharding import PartitionSpec as P

QUERY_ROWS = 128


def rms_norm(x_in, norm_gain):
    x_f32 = x_in.astype(jnp.float32)
    inv_rms = lax.rsqrt(jnp.mean(x_f32 * x_f32, axis=-1, keepdims=True) + 1e-5)
    return (x_f32 * inv_rms * norm_gain).astype(jnp.bfloat16)


def apply_rope(vectors, cos_t, sin_t):
    half_dim = vectors.shape[-1] // 2
    lower_half = vectors[..., :half_dim].astype(jnp.float32)
    upper_half = vectors[..., half_dim:].astype(jnp.float32)
    turned = jnp.concatenate([lower_half * cos_t - upper_half * sin_t, upper_half * cos_t + lower_half * sin_t], axis=-1)
    return turned.astype(jnp.bfloat16)


def project(x_in, pos_in_doc, norm_gain, w_q, w_k, w_v, inv_freq):
    num_rows = x_in.shape[0]
    head_dim = 2 * inv_freq.shape[0]
    kv_heads = w_k.shape[1] // head_dim
    group_size = w_q.shape[1] // (head_dim * kv_heads)
    normed = rms_norm(x_in, norm_gain)
    q_new = jnp.dot(normed, w_q, preferred_element_type=jnp.float32).astype(jnp.bfloat16).reshape(num_rows, kv_heads, group_size, head_dim)
    k_new = jnp.dot(normed, w_k, preferred_element_type=jnp.float32).astype(jnp.bfloat16).reshape(num_rows, kv_heads, head_dim)
    v_new = jnp.dot(normed, w_v, preferred_element_type=jnp.float32).astype(jnp.bfloat16).reshape(num_rows, kv_heads, head_dim)
    rope_angle = pos_in_doc.astype(jnp.float32)[:, None] * inv_freq[None, :]
    cos_t = jnp.cos(rope_angle)
    sin_t = jnp.sin(rope_angle)
    q_rot = apply_rope(q_new, cos_t[:, None, None, :], sin_t[:, None, None, :])
    k_rot = apply_rope(k_new, cos_t[:, None, :], sin_t[:, None, :])
    return q_rot, k_rot, v_new


def global_index(stored_pos, local_rows, cp_size):
    piece_len = local_rows // 2
    owner = stored_pos // local_rows
    within = stored_pos % local_rows
    piece_id = jnp.where(within < piece_len, owner, 2 * cp_size - 1 - owner)
    return piece_id * piece_len + within % piece_len


def attention(q_rot, key_rows, val_rows, q_doc, q_idx, key_doc, key_idx):
    local_rows, kv_heads, group_size, head_dim = q_rot.shape
    blocks = local_rows // QUERY_ROWS
    score_scale = head_dim ** -0.5

    def attend(block_args):
        q_blk, doc_blk, idx_blk = block_args
        scores = jnp.einsum('qngd,knd->ngqk', q_blk, key_rows, preferred_element_type=jnp.float32) * score_scale
        visible = (doc_blk[:, None] == key_doc[None, :]) & (key_idx[None, :] <= idx_blk[:, None])
        scores = jnp.where(visible, scores, -1e30)
        attn_probs = jax.nn.softmax(scores, axis=-1).astype(jnp.bfloat16)
        return jnp.einsum('ngqk,knd->qngd', attn_probs, val_rows, preferred_element_type=jnp.float32).astype(jnp.bfloat16)

    attn_out = lax.map(attend, (q_rot.reshape(blocks, QUERY_ROWS, kv_heads, group_size, head_dim), q_doc.reshape(blocks, QUERY_ROWS), q_idx.reshape(blocks, QUERY_ROWS)))
    return attn_out.reshape(local_rows, kv_heads * group_size * head_dim)


def solution(mesh):
    cp_size = mesh.shape['cp']

    def local_step(x_in, doc_id, pos_in_doc, norm_gain, w_q, w_k, w_v, w_o, inv_freq):
        local_rows = x_in.shape[0]
        tokens = local_rows * cp_size
        q_rot, k_rot, v_new = project(x_in, pos_in_doc, norm_gain, w_q, w_k, w_v, inv_freq)
        k_all = lax.all_gather(k_rot, 'cp', tiled=True)
        v_all = lax.all_gather(v_new, 'cp', tiled=True)
        doc_all = lax.all_gather(doc_id, 'cp', tiled=True)
        cp_index = lax.axis_index('cp')
        q_idx = global_index(cp_index * local_rows + jnp.arange(local_rows), local_rows, cp_size)
        key_idx = global_index(jnp.arange(tokens), local_rows, cp_size)
        attn_out = attention(q_rot, k_all, v_all, doc_id, q_idx, doc_all, key_idx)
        part_sum = jnp.dot(attn_out, w_o, preferred_element_type=jnp.float32)
        full_sum = lax.psum(part_sum, 'tp')
        y_out = (x_in.astype(jnp.float32) + full_sum).astype(jnp.bfloat16)
        return y_out, k_rot, v_new

    row_spec = P(('dp', 'cp'))
    in_specs = (P(('dp', 'cp'), None), row_spec, row_spec, P(), P(None, 'tp'), P(None, 'tp'), P(None, 'tp'), P('tp', None), P())
    out_specs = (P(('dp', 'cp'), None), P(('dp', 'cp'), 'tp', None), P(('dp', 'cp'), 'tp', None))
    return jax.shard_map(local_step, mesh=mesh, in_specs=in_specs, out_specs=out_specs, check_vma=False)
```

profile of v0, /device:TPU:0, one launch (start us, length us, event | category | flops | bytes accessed | tf_op | source)
XLA Modules:
  0.0 832.3 jit_solution(5108190485976897050)
XLA Ops:
  8.1 5.5 fusion.57
  14.7 2.9 convolution_convert_fusion.2
  17.8 1.1 copy.37
  19.0 6.7 convolution_convert_fusion.1
  26.9 14.0 %convolution_convert_fusion = bf16[1024,1024]{0,1:T(8,128)(2,1)S(1)} fusion(bf16[4096,1024]{1,0:T(8,128)(2,1)} %param.15, bf16[1024,4096]{1,0:T(8,128)(2,1)} %param.11, f32[4096]{0:T(1024)S(1)} %copy-done.7, f32[1024]{0:T(1024)S(1)} %add_rsqrt_fusion), kind=kOutput, calls=%fused_computation.71 | convolution fusion | flops 8607760384 | bytes 18894848 | tf_op jit(solution)/shard_map/dot_general | solution.py:29
  42.5 2.6 copy.39
  45.1 6.4 all_gather.9
  51.5 3.2 copy.40
  54.7 13.9 %all-gather.5.cloned.1.call-done = bf16[4096,2,128]{2,0,1:T(8,128)(2,1)} async-done(((bf16[1024,2,128]{2,0,1:T(8,128)(2,1)}), bf16[4096,2,128]{2,0,1:T(8,128)(2,1)}) %all-gather.5.cloned.1.call-update) | async-done | bytes 2097168 | tf_op jit(solution)/shard_map/all_gather | solution.py:73
  68.6 167.6 %while.11 = (s32[]{:T(128)}, bf16[8,128,2,4,128]{4,1,3,2,0:T(8,128)(2,1)}, s32[8,128]{1,0:T(8,128)S(1)}, s32[4096]{0:T(1024)S(1)}, s32[8,128]{1,0:T(8,128)S(1)},...) while((s32[]{:T(128)}, ...), condition=%wide.region_4.5_spmd.clone, body=%wide.region_1.4_spmd.clone.sunk | while | flops 2174472192 | bytes 39382128 | solution.py:61
  69.1 11.0 %fusion.106 = (f32[2,4,128]{2,1,0:T(4,128)S(1)}, f32[2,4,128,4096]{3,2,1,0:T(8,128)}) fusion(pred[128,4096]{1,0:T(8,128)(4,1)S(1)} %compare_and_fusion.2, bf16[4096,2,128]{2,0,1:T(8,128)(2,1)} %get-tuple-element.220, bf16[8,128,2,4,128]{4,1,3,2,0:T(8,128)(2,1)} %get-tuple-element.219, s32[]{:T(128)S(6)} %copy.56), kind=kOutput, calls=%fused_computation.103.clone.1 | convolution fusion | flops 1090523136 | bytes 19664900 | tf_op jit(solution)/shard_map/while/body/eval_jaxpr/sub | solution.py:58
  80.1 9.4 %fusion.107 = bf16[8,128,2,4,128]{4,1,3,2,0:T(8,128)(2,1)} fusion(bf16[8,128,2,4,128]{4,1,3,2,0:T(8,128)(2,1)} %get-tuple-element.206, s32[]{:T(128)S(6)} %copy.56, bf16[4096,2,128]{2,0,1:T(8,128)(2,1)} %get-tuple-element.221, f32[2,4,128,4096]{3,2,1,0:T(8,128)} %get-tuple-element.194, f32[2,4,128]{2,1,0:T(4,128)S(1)} %get-tuple-element.195), kind=kOutput, calls=%fused_computation.20.clone.1 | convolution fusion | flops 1082261504 | bytes 19140612 | tf_op jit(solution)/shard_map/while/body/eval_jaxpr/ngqk,knd->qngd/dot_general | solution.py:59
  90.1 11.0 %fusion.106 = (f32[2,4,128]{2,1,0:T(4,128)S(1)}, f32[2,4,128,4096]{3,2,1,0:T(8,128)}) fusion(pred[128,4096]{1,0:T(8,128)(4,1)S(1)} %compare_and_fusion.2, bf16[4096,2,128]{2,0,1:T(8,128)(2,1)} %get-tuple-element.220, bf16[8,128,2,4,128]{4,1,3,2,0:T(8,128)(2,1)} %get-tuple-element.219, s32[]{:T(128)S(6)} %copy.56), kind=kOutput, calls=%fused_computation.103.clone.1 | convolution fusion | flops 1090523136 | bytes 19664900 | tf_op jit(solution)/shard_map/while/body/eval_jaxpr/sub | solution.py:58
  101.1 9.4 %fusion.107 = bf16[8,128,2,4,128]{4,1,3,2,0:T(8,128)(2,1)} fusion(bf16[8,128,2,4,128]{4,1,3,2,0:T(8,128)(2,1)} %get-tuple-element.206, s32[]{:T(128)S(6)} %copy.56, bf16[4096,2,128]{2,0,1:T(8,128)(2,1)} %get-tuple-element.221, f32[2,4,128,4096]{3,2,1,0:T(8,128)} %get-tuple-element.194, f32[2,4,128]{2,1,0:T(4,128)S(1)} %get-tuple-element.195), kind=kOutput, calls=%fused_computation.20.clone.1 | convolution fusion | flops 1082261504 | bytes 19140612 | tf_op jit(solution)/shard_map/while/body/eval_jaxpr/ngqk,knd->qngd/dot_general | solution.py:59
  111.0 11.0 %fusion.106 = (f32[2,4,128]{2,1,0:T(4,128)S(1)}, f32[2,4,128,4096]{3,2,1,0:T(8,128)}) fusion(pred[128,4096]{1,0:T(8,128)(4,1)S(1)} %compare_and_fusion.2, bf16[4096,2,128]{2,0,1:T(8,128)(2,1)} %get-tuple-element.220, bf16[8,128,2,4,128]{4,1,3,2,0:T(8,128)(2,1)} %get-tuple-element.219, s32[]{:T(128)S(6)} %copy.56), kind=kOutput, calls=%fused_computation.103.clone.1 | convolution fusion | flops 1090523136 | bytes 19664900 | tf_op jit(solution)/shard_map/while/body/eval_jaxpr/sub | solution.py:58
  122.0 9.4 %fusion.107 = bf16[8,128,2,4,128]{4,1,3,2,0:T(8,128)(2,1)} fusion(bf16[8,128,2,4,128]{4,1,3,2,0:T(8,128)(2,1)} %get-tuple-element.206, s32[]{:T(128)S(6)} %copy.56, bf16[4096,2,128]{2,0,1:T(8,128)(2,1)} %get-tuple-element.221, f32[2,4,128,4096]{3,2,1,0:T(8,128)} %get-tuple-element.194, f32[2,4,128]{2,1,0:T(4,128)S(1)} %get-tuple-element.195), kind=kOutput, calls=%fused_computation.20.clone.1 | convolution fusion | flops 1082261504 | bytes 19140612 | tf_op jit(solution)/shard_map/while/body/eval_jaxpr/ngqk,knd->qngd/dot_general | solution.py:59
  132.0 11.0 %fusion.106 = (f32[2,4,128]{2,1,0:T(4,128)S(1)}, f32[2,4,128,4096]{3,2,1,0:T(8,128)}) fusion(pred[128,4096]{1,0:T(8,128)(4,1)S(1)} %compare_and_fusion.2, bf16[4096,2,128]{2,0,1:T(8,128)(2,1)} %get-tuple-element.220, bf16[8,128,2,4,128]{4,1,3,2,0:T(8,128)(2,1)} %get-tuple-element.219, s32[]{:T(128)S(6)} %copy.56), kind=kOutput, calls=%fused_computation.103.clone.1 | convolution fusion | flops 1090523136 | bytes 19664900 | tf_op jit(solution)/shard_map/while/body/eval_jaxpr/sub | solution.py:58
  143.0 9.4 %fusion.107 = bf16[8,128,2,4,128]{4,1,3,2,0:T(8,128)(2,1)} fusion(bf16[8,128,2,4,128]{4,1,3,2,0:T(8,128)(2,1)} %get-tuple-element.206, s32[]{:T(128)S(6)} %copy.56, bf16[4096,2,128]{2,0,1:T(8,128)(2,1)} %get-tuple-element.221, f32[2,4,128,4096]{3,2,1,0:T(8,128)} %get-tuple-element.194, f32[2,4,128]{2,1,0:T(4,128)S(1)} %get-tuple-element.195), kind=kOutput, calls=%fused_computation.20.clone.1 | convolution fusion | flops 1082261504 | bytes 19140612 | tf_op jit(solution)/shard_map/while/body/eval_jaxpr/ngqk,knd->qngd/dot_general | solution.py:59
  152.9 11.0 %fusion.106 = (f32[2,4,128]{2,1,0:T(4,128)S(1)}, f32[2,4,128,4096]{3,2,1,0:T(8,128)}) fusion(pred[128,4096]{1,0:T(8,128)(4,1)S(1)} %compare_and_fusion.2, bf16[4096,2,128]{2,0,1:T(8,128)(2,1)} %get-tuple-element.220, bf16[8,128,2,4,128]{4,1,3,2,0:T(8,128)(2,1)} %get-tuple-element.219, s32[]{:T(128)S(6)} %copy.56), kind=kOutput, calls=%fused_computation.103.clone.1 | convolution fusion | flops 1090523136 | bytes 19664900 | tf_op jit(solution)/shard_map/while/body/eval_jaxpr/sub | solution.py:58
  163.9 9.4 %fusion.107 = bf16[8,128,2,4,128]{4,1,3,2,0:T(8,128)(2,1)} fusion(bf16[8,128,2,4,128]{4,1,3,2,0:T(8,128)(2,1)} %get-tuple-element.206, s32[]{:T(128)S(6)} %copy.56, bf16[4096,2,128]{2,0,1:T(8,128)(2,1)} %get-tuple-element.221, f32[2,4,128,4096]{3,2,1,0:T(8,128)} %get-tuple-element.194, f32[2,4,128]{2,1,0:T(4,128)S(1)} %get-tuple-element.195), kind=kOutput, calls=%fused_computation.20.clone.1 | convolution fusion | flops 1082261504 | bytes 19140612 | tf_op jit(solution)/shard_map/while/body/eval_jaxpr/ngqk,knd->qngd/dot_general | solution.py:59
  173.9 11.0 %fusion.106 = (f32[2,4,128]{2,1,0:T(4,128)S(1)}, f32[2,4,128,4096]{3,2,1,0:T(8,128)}) fusion(pred[128,4096]{1,0:T(8,128)(4,1)S(1)} %compare_and_fusion.2, bf16[4096,2,128]{2,0,1:T(8,128)(2,1)} %get-tuple-element.220, bf16[8,128,2,4,128]{4,1,3,2,0:T(8,128)(2,1)} %get-tuple-element.219, s32[]{:T(128)S(6)} %copy.56), kind=kOutput, calls=%fused_computation.103.clone.1 | convolution fusion | flops 1090523136 | bytes 19664900 | tf_op jit(solution)/shard_map/while/body/eval_jaxpr/sub | solution.py:58
  184.9 9.4 %fusion.107 = bf16[8,128,2,4,128]{4,1,3,2,0:T(8,128)(2,1)} fusion(bf16[8,128,2,4,128]{4,1,3,2,0:T(8,128)(2,1)} %get-tuple-element.206, s32[]{:T(128)S(6)} %copy.56, bf16[4096,2,128]{2,0,1:T(8,128)(2,1)} %get-tuple-element.221, f32[2,4,128,4096]{3,2,1,0:T(8,128)} %get-tuple-element.194, f32[2,4,128]{2,1,0:T(4,128)S(1)} %get-tuple-element.195), kind=kOutput, calls=%fused_computation.20.clone.1 | convolution fusion | flops 1082261504 | bytes 19140612 | tf_op jit(solution)/shard_map/while/body/eval_jaxpr/ngqk,knd->qngd/dot_general | solution.py:59
  194.8 11.0 %fusion.106 = (f32[2,4,128]{2,1,0:T(4,128)S(1)}, f32[2,4,128,4096]{3,2,1,0:T(8,128)}) fusion(pred[128,4096]{1,0:T(8,128)(4,1)S(1)} %compare_and_fusion.2, bf16[4096,2,128]{2,0,1:T(8,128)(2,1)} %get-tuple-element.220, bf16[8,128,2,4,128]{4,1,3,2,0:T(8,128)(2,1)} %get-tuple-element.219, s32[]{:T(128)S(6)} %copy.56), kind=kOutput, calls=%fused_computation.103.clone.1 | convolution fusion | flops 1090523136 | bytes 19664900 | tf_op jit(solution)/shard_map/while/body/eval_jaxpr/sub | solution.py:58
  205.8 9.4 %fusion.107 = bf16[8,128,2,4,128]{4,1,3,2,0:T(8,128)(2,1)} fusion(bf16[8,128,2,4,128]{4,1,3,2,0:T(8,128)(2,1)} %get-tuple-element.206, s32[]{:T(128)S(6)} %copy.56, bf16[4096,2,128]{2,0,1:T(8,128)(2,1)} %get-tuple-element.221, f32[2,4,128,4096]{3,2,1,0:T(8,128)} %get-tuple-element.194, f32[2,4,128]{2,1,0:T(4,128)S(1)} %get-tuple-element.195), kind=kOutput, calls=%fused_computation.20.clone.1 | convolution fusion | flops 1082261504 | bytes 19140612 | tf_op jit(solution)/shard_map/while/body/eval_jaxpr/ngqk,knd->qngd/dot_general | solution.py:59
  215.8 11.0 %fusion.106 = (f32[2,4,128]{2,1,0:T(4,128)S(1)}, f32[2,4,128,4096]{3,2,1,0:T(8,128)}) fusion(pred[128,4096]{1,0:T(8,128)(4,1)S(1)} %compare_and_fusion.2, bf16[4096,2,128]{2,0,1:T(8,128)(2,1)} %get-tuple-element.220, bf16[8,128,2,4,128]{4,1,3,2,0:T(8,128)(2,1)} %get-tuple-element.219, s32[]{:T(128)S(6)} %copy.56), kind=kOutput, calls=%fused_computation.103.clone.1 | convolution fusion | flops 1090523136 | bytes 19664900 | tf_op jit(solution)/shard_map/while/body/eval_jaxpr/sub | solution.py:58
  226.8 9.4 %fusion.107 = bf16[8,128,2,4,128]{4,1,3,2,0:T(8,128)(2,1)} fusion(bf16[8,128,2,4,128]{4,1,3,2,0:T(8,128)(2,1)} %get-tuple-element.206, s32[]{:T(128)S(6)} %copy.56, bf16[4096,2,128]{2,0,1:T(8,128)(2,1)} %get-tuple-element.221, f32[2,4,128,4096]{3,2,1,0:T(8,128)} %get-tuple-element.194, f32[2,4,128]{2,1,0:T(4,128)S(1)} %get-tuple-element.195), kind=kOutput, calls=%fused_computation.20.clone.1 | convolution fusion | flops 1082261504 | bytes 19140612 | tf_op jit(solution)/shard_map/while/body/eval_jaxpr/ngqk,knd->qngd/dot_general | solution.py:59
  236.2 3.1 copy.41
  239.3 14.6 %fusion.65 = f32[1024,4096]{1,0:T(8,128)} fusion(bf16[1024,4096]{1,0:T(8,128)(2,1)} %param.18, bf16[128,8,8,128]{3,2,1,0:T(8,128)(2,1)S(1)} %bitcast.104), kind=kOutput, calls=%fused_computation.67 | convolution fusion | flops 8589934592 | bytes 27262976 | tf_op jit(solution)/shard_map/dot_general | solution.py:79
  253.9 1.0 copy-done.4
  254.9 1.1 copy.43
  256.0 557.6 %all-reduce.2.cloned.1.call-done = f32[1024,4096]{1,0:T(8,128)} async-done(((f32[1024,4096]{1,0:T(8,128)}), f32[1024,4096]{1,0:T(8,128)}) %all-reduce.2.cloned.1.call-update) | async-done | bytes 16777232 | tf_op jit(solution)/shard_map/psum | solution.py:80
  813.6 12.2 %fusion.60 = bf16[1024,4096]{1,0:T(8,128)(2,1)} fusion(f32[1024,4096]{1,0:T(8,128)} %all-reduce.2.cloned.1.call-done, bf16[1024,4096]{1,0:T(8,128)(2,1)} %param.11), kind=kLoop, calls=%fused_computation.58 | loop fusion | flops 12582912 | bytes 33554432 | tf_op jit(solution)/shard_map/convert_element_type | solution.py:81
  (58 shorter events, 8.9 us)
Async XLA Ops:
  7.2 7.5 copy-start
  7.2 6.5 copy-start.6
  7.2 7.5 copy-start.7
  7.2 44.3 %all-gather.3.cloned.1.call-start = ((), (), s32[]{:S(2)}) async-start(), calls=%async_computation | async-start | bytes 2621440 | tf_op jit(solution)/shard_map/all_gather | solution.py:72
  7.2 7.4 copy-start.2
  18.9 49.7 %all-gather.5.cloned.1.call-start = ((), (), s32[]{:S(2)}) async-start(), calls=%async_computation.1 | async-start | bytes 2621440 | tf_op jit(solution)/shard_map/all_gather | solution.py:73
  25.6 15.3 %copy-start.3 = (bf16[1024,256]{0,1:T(8,128)(2,1)}, bf16[1024,256]{0,1:T(8,128)(2,1)S(1)}, u32[]{:S(2)}) copy-start(bf16[1024,256]{0,1:T(8,128)(2,1)S(1)} %convolution_convert_fusion.1) | copy-start | bytes 1572868
  26.7 786.9 %all-reduce.2.cloned.1.call-start = ((), (), s32[]{:S(2)}) async-start(), calls=%async_computation.2 | async-start | bytes 33554432 | tf_op jit(solution)/shard_map/psum | solution.py:80
  41.0 4.1 copy-start.5
  253.9 1.0 copy-start.4
  813.6 12.2 %copy-start.1 = (bf16[4096,256]{1,0:T(8,128)(2,1)S(1)}, bf16[4096,256]{1,0:T(8,128)(2,1)}, u32[]{:S(2)}) copy-start(bf16[4096,256]{1,0:T(8,128)(2,1)} %param.16) | copy-start | bytes 6291460
Sparse Core Ops, SparseCore 0:
  19.0 25.0 all-gather.2
  46.3 22.3 all-gather.4
  254.0 559.5 all-reduce.1
where the time goes:
time: 833 us; the launch traced here: 832 us
  waiting for transfers between devices  572 us (69%)
  matrix products  202 us (24%)
  other arithmetic  24.5 us (3%)
  between operations  13.9 us (2%)
  local copies, waits for them, and re-layouts  13.7 us (2%)
    psum x1, waiting for transfers between devices, local_step(): full_sum = lax.psum(part_sum, 'tp')  558 us
    sub x8, matrix products, attend(): attn_probs = jax.nn.softmax(scores, axis=-1).astype(jnp.bfloat16)  88 us
    dot_general x8, matrix products, attend(): jnp.einsum('ngqk,knd->qngd', attn_probs, val_rows, preferred_element_type...  75.5 us
  transfers between devices with their start and end apart: 3, of which 2 were waited for; matrix products, arithmetic and copies ran while one was open for 4% of the time, Pallas kernels for 0%

commit v1 on v0

v1 whole, which is shorter than its diff:
```python
import functools

import jax
import jax.numpy as jnp
from jax import lax
from jax.experimental import pallas as pl
from jax.experimental.pallas import tpu as pltpu
from jax.sharding import PartitionSpec as P

MESH = pl.DeviceIdType.MESH
HBM = pltpu.HBM
VMEM = pltpu.VMEM
HEAD = 128
Q_TILE = 128
F32 = jnp.float32
BF16 = jnp.bfloat16


def rope(vec, cos_t, sin_t):
    vec = vec.astype(F32)
    return (vec * cos_t + pltpu.roll(vec, HEAD // 2, 1) * sin_t).astype(BF16)


def kv_kernel(x_ref, gain_ref, wk_ref, wv_ref, cos_ref, sin_ref, h_ref, kv_ref):
    rows, width = x_ref.shape
    step = 16

    def norm_rows(i, _):
        at = pl.ds(pl.multiple_of(i * step, step), step)
        xf = x_ref[at, :].astype(F32)
        inv = lax.rsqrt(jnp.sum(xf * xf, axis=-1, keepdims=True) * (1.0 / width) + 1e-5)
        h_ref[at, :] = (xf * inv * gain_ref[...]).astype(BF16)
        return 0

    lax.fori_loop(0, rows // step, norm_rows, 0)
    h = h_ref[...]
    k_new = jnp.dot(h, wk_ref[...], preferred_element_type=F32).astype(BF16)
    v_new = jnp.dot(h, wv_ref[...], preferred_element_type=F32).astype(BF16)
    cols = k_new.shape[1]
    for j in range(cols // HEAD):
        at = slice(j * HEAD, (j + 1) * HEAD)
        kv_ref[:, at] = rope(k_new[:, at], cos_ref[...], sin_ref[...])
    kv_ref[:, cols:] = v_new


def norm_kv(x, gain, w_k, w_v, cos_t, sin_t):
    rows, width = x.shape
    cols = w_k.shape[1]
    tile = 256
    const = lambda i: (0, 0)
    byrow = lambda i: (i, 0)
    return pl.pallas_call(
        kv_kernel,
        grid=(rows // tile,),
        in_specs=[
            pl.BlockSpec((tile, width), byrow),
            pl.BlockSpec((1, width), const),
            pl.BlockSpec((width, cols), const),
            pl.BlockSpec((width, cols), const),
            pl.BlockSpec((tile, HEAD), byrow),
            pl.BlockSpec((tile, HEAD), byrow),
        ],
        out_specs=[pl.BlockSpec((tile, width), byrow), pl.BlockSpec((tile, 2 * cols), byrow)],
        out_shape=[jax.ShapeDtypeStruct((rows, width), BF16), jax.ShapeDtypeStruct((rows, 2 * cols), BF16)],
        compiler_params=pltpu.CompilerParams(vmem_limit_bytes=32 << 20),
        cost_estimate=pl.CostEstimate(flops=4 * rows * width * cols, bytes_accessed=21 << 20, transcendentals=0),
        name="norm_kv",
    )(x, gain.reshape(1, width), w_k, w_v, cos_t, sin_t)


def q_kernel(h_ref, wq_ref, cos_ref, sin_ref, q_ref):
    q_new = jnp.dot(h_ref[...], wq_ref[...], preferred_element_type=F32).astype(BF16)
    for j in range(q_new.shape[1] // HEAD):
        at = slice(j * HEAD, (j + 1) * HEAD)
        q_ref[:, at] = rope(q_new[:, at], cos_ref[...], sin_ref[...])


def q_proj(h, w_q, cos_t, sin_t):
    rows, width = h.shape
    cols = w_q.shape[1]
    tile = 256
    const = lambda i: (0, 0)
    return pl.pallas_call(
        q_kernel,
        grid=(cols // tile,),
        in_specs=[
            pl.BlockSpec((rows, width), const),
            pl.BlockSpec((width, tile), lambda i: (0, i)),
            pl.BlockSpec((rows, HEAD), const),
            pl.BlockSpec((rows, HEAD), const),
        ],
        out_specs=pl.BlockSpec((rows, tile), lambda i: (0, i)),
        out_shape=jax.ShapeDtypeStruct((rows, cols), BF16),
        compiler_params=pltpu.CompilerParams(vmem_limit_bytes=40 << 20),
        cost_estimate=pl.CostEstimate(flops=2 * rows * width * cols, bytes_accessed=18 << 20, transcendentals=0),
        name="q_proj",
    )(h, w_q, cos_t, sin_t)


def attn_kernel(n_cp, group, gidx_ref, low_ref, place_ref, q_ref, tok_ref, pos_ref, kv0, kv1, kv2, kv3, o_ref, kv_ref, sems):
    head, blk = pl.program_id(0), pl.program_id(1)
    piece = kv0.shape[0] // 2
    kv_cols = kv0.shape[1] // 2

    @pl.when((head == 0) & (blk == 0))
    def _():
        copies = []
        for r, src in enumerate((kv0, kv1, kv2, kv3)):
            for half in range(2):
                at = pl.multiple_of(place_ref[2 * r + half], piece)
                copies.append(pltpu.make_async_copy(src.at[pl.ds(half * piece, piece)], kv_ref.at[pl.ds(at, piece)], sems.at[2 * r + half]))
        for c in copies:
            c.start()
        for c in copies:
            c.wait()

    q_rows = q_ref.shape[0]
    q = jnp.concatenate([q_ref[:, g * HEAD:(g + 1) * HEAD] for g in range(group)], axis=0)
    g0 = gidx_ref[blk]
    tok = jnp.concatenate([tok_ref[...]] * group, axis=0)
    first = tok - jnp.concatenate([pos_ref[...]] * group, axis=0)
    scale = HEAD ** -0.5
    k_at = pl.ds(pl.multiple_of(head * HEAD, HEAD), HEAD)
    v_at = pl.ds(pl.multiple_of(kv_cols + head * HEAD, HEAD), HEAD)

    def scores(start, width):
        keys = kv_ref[pl.ds(pl.multiple_of(start, Q_TILE), width), k_at]
        s = lax.dot_general(q, keys, (((1,), (1,)), ((), ())), preferred_element_type=F32) * scale
        u = start + lax.broadcasted_iota(jnp.int32, (1, width), 1)
        return jnp.where((u >= first) & (u <= tok), s, -1e30)

    def values(start, width):
        return kv_ref[pl.ds(pl.multiple_of(start, Q_TILE), width), v_at]

    near = jnp.maximum(g0 - Q_TILE, 0)
    s = scores(near, 2 * Q_TILE)
    m = jnp.max(s, axis=-1, keepdims=True)
    p = jnp.exp(s - m)
    total = jnp.sum(p, axis=-1, keepdims=True)
    acc = jnp.dot(p.astype(BF16), values(near, 2 * Q_TILE), preferred_element_type=F32)

    def far(i, carry):
        m, total, acc = carry
        start = i * Q_TILE
        s = scores(start, Q_TILE)
        m_new = jnp.maximum(m, jnp.max(s, axis=-1, keepdims=True))
        old = jnp.exp(m - m_new)
        p = jnp.exp(s - m_new)
        total = total * old + jnp.sum(p, axis=-1, keepdims=True)
        acc = acc * old + jnp.dot(p.astype(BF16), values(start, Q_TILE), preferred_element_type=F32)
        return m_new, total, acc

    m, total, acc = lax.fori_loop(low_ref[blk], near // Q_TILE, far, (m, total, acc))
    out = (acc / total).astype(BF16)
    for g in range(group):
        o_ref[:, g * HEAD:(g + 1) * HEAD] = out[g * q_rows:(g + 1) * q_rows]


def attention(q, kvs, tok, pos, cp):
    rows, q_cols = q.shape
    n_cp = len(kvs)
    kv_cols = kvs[0].shape[1] // 2
    heads = kv_cols // HEAD
    group = q_cols // kv_cols
    piece = rows // 2
    gidx = tok[::Q_TILE]
    low = (gidx - pos[::Q_TILE]) // Q_TILE
    owners = [cp ^ r for r in range(n_cp)]
    place = jnp.stack([w for o in owners for w in (o * piece, (2 * n_cp - 1 - o) * piece)]).astype(jnp.int32)
    q_map = lambda h, i, *_: (i, h)
    row_map = lambda h, i, *_: (i, 0)
    return pl.pallas_call(
        functools.partial(attn_kernel, n_cp, group),
        grid_spec=pltpu.PrefetchScalarGridSpec(
            num_scalar_prefetch=3,
            grid=(heads, rows // Q_TILE),
            in_specs=[
                pl.BlockSpec((Q_TILE, group * HEAD), q_map),
                pl.BlockSpec((Q_TILE, 1), row_map),
                pl.BlockSpec((Q_TILE, 1), row_map),
            ] + [pl.BlockSpec(memory_space=HBM)] * n_cp,
            out_specs=pl.BlockSpec((Q_TILE, group * HEAD), q_map),
            scratch_shapes=[VMEM((n_cp * rows, 2 * kv_cols), BF16), pltpu.SemaphoreType.DMA((2 * n_cp,))],
        ),
        out_shape=jax.ShapeDtypeStruct((rows, q_cols), BF16),
        compiler_params=pltpu.CompilerParams(vmem_limit_bytes=32 << 20),
        cost_estimate=pl.CostEstimate(flops=5 << 30, bytes_accessed=8 << 20, transcendentals=0),
        name="attn",
    )(gidx, low, place, q, tok[:, None], pos[:, None], *kvs)


def out_kernel(o_ref, fl_ref, fr_ref, fl2_ref, fr2_ref, wown_ref, x_ref, y_ref,
               wbuf, wtile, xtile, obuf, acc, ytile,
               load_sem, tile_sem, y_sem, wsend, wrecv, w3_send, w3_recv, own_send, fwd_send, o_recv):
    rows, kdim = o_ref.shape
    width = x_ref.shape[1]
    slice_rows = fl_ref.shape[0]
    half = slice_rows // 2
    chunks = 4
    c_rows = rows // chunks
    n_tile = 512
    y_cols = ytile.shape[2]
    dp, z, cp = lax.axis_index("dp"), lax.axis_index("tp"), lax.axis_index("cp")
    is_end = (z == 0) | (z == 3)
    is_mid = (z == 1) | (z == 2)
    core = {"cp": cp + 1 - 2 * lax.rem(cp, 2)}
    ynb = {"cp": lax.rem(cp + 2, 4)}
    xnb = {"dp": 1 - dp}
    left = {"tp": jnp.maximum(z - 1, 0)}
    right = {"tp": jnp.minimum(z + 1, 3)}
    p_own = dp * 4 + cp
    p_x = (1 - dp) * 4 + cp
    p_y = dp * 4 + lax.rem(cp + 2, 4)
    p_d = (1 - dp) * 4 + lax.rem(cp + 2, 4)
    p_core = dp * 4 + cp + 1 - 2 * lax.rem(cp, 2)
    low_side = z < 2
    s1 = jnp.where(low_side, 1 - z, 5 - z)
    s2 = jnp.where(low_side, 2, 1)
    s3 = jnp.where(low_side, 3, 0)

    def remote(src, dst, ssem, rsem, dev):
        return pltpu.make_async_remote_copy(src_ref=src, dst_ref=dst, send_sem=ssem, recv_sem=rsem, device_id=dev, device_id_type=MESH)

    barrier = pltpu.get_barrier_semaphore()
    for dev in (core, ynb, xnb):
        pl.semaphore_signal(barrier, inc=1, device_id=dev, device_id_type=MESH)

    @pl.when(z > 0)
    def _():
        pl.semaphore_signal(barrier, inc=1, device_id=left, device_id_type=MESH)

    @pl.when(z < 3)
    def _():
        pl.semaphore_signal(barrier, inc=1, device_id=right, device_id_type=MESH)

    def w_at(j, p, start=0, n=None):
        n = slice_rows if n is None else n
        return wbuf.at[j, pl.ds(pl.multiple_of(p * slice_rows + start, half), n)]

    def load_w(src, j):
        return pltpu.make_async_copy(src, w_at(j, p_own), load_sem.at[j])

    sources = ((fr_ref, fr2_ref, None), (fl_ref, fr_ref, fr2_ref), (fr_ref, fl_ref, fl2_ref), (fl_ref, fl2_ref, None))
    o_load = pltpu.make_async_copy(o_ref, obuf.at[z], load_sem.at[3])
    o_load.start()
    for zz in range(4):
        @pl.when(z == zz)
        def _(zz=zz):
            for j in range(3):
                if sources[zz][j] is not None:
                    load_w(sources[zz][j], j).start()

    @pl.when(is_end)
    def _():
        pl.semaphore_wait(barrier, 4)

    @pl.when(is_mid)
    def _():
        pl.semaphore_wait(barrier, 5)

    def w_copy(j, kind):
        dev = (xnb, ynb, core, ynb, xnb, core, core, core, core)[kind]
        src = (w_at(j, p_own), w_at(j, p_own), w_at(j, p_own), w_at(j, p_x, 0, half), w_at(j, p_y, half, half),
               w_at(j, p_x), w_at(j, p_y), w_at(j, p_d, 0, half), w_at(j, p_d, half, half))[kind]
        return remote(src, src, wsend.at[j, kind], wrecv.at[j, kind], dev)

    def core_p(p):
        return p + 1 - 2 * lax.rem(p, 2)

    def w_wait(j, kind):
        dst = (w_at(j, p_x), w_at(j, p_y), w_at(j, p_core), w_at(j, p_d, 0, half), w_at(j, p_d, half, half),
               w_at(j, core_p(p_x)), w_at(j, core_p(p_y)), w_at(j, core_p(p_d), 0, half), w_at(j, core_p(p_d), half, half))[kind]
        remote(dst, dst, wsend.at[j, kind], wrecv.at[j, kind], core).wait_recv()

    def spread_own(j):
        for kind in (0, 1, 2):
            w_copy(j, kind).start()

    def spread_relay(j):
        w_wait(j, 0)
        w_copy(j, 3).start()
        w_copy(j, 5).start()
        w_wait(j, 1)
        w_copy(j, 4).start()
        w_copy(j, 6).start()

    def spread_diag(j):
        w_wait(j, 3)
        w_copy(j, 7).start()
        w_wait(j, 4)
        w_copy(j, 8).start()

    def spread_done(j):
        for kind in (2, 5, 6, 7, 8):
            w_wait(j, kind)

    def o_at(s, c):
        return obuf.at[s, pl.ds(pl.multiple_of(c * c_rows, c_rows), c_rows)]

    def o_own(c, side):
        return remote(o_at(z, c), o_at(z, c), own_send.at[side, c], o_recv.at[z, c], (left, right)[side])

    def o_fwd(s, c, side):
        return remote(o_at(s, c), o_at(s, c), fwd_send.at[s, c], o_recv.at[s, c], (left, right)[side])

    def o_wait(s, c):
        remote(o_at(s, c), o_at(s, c), fwd_send.at[s, c], o_recv.at[s, c], left).wait_recv()

    def o_pass(s, c):
        o_wait(s, c)

        @pl.when(s < z)
        def _():
            o_fwd(s, c, 1).start()

        @pl.when(s > z)
        def _():
            o_fwd(s, c, 0).start()

    w3 = remote(w_at(2, p_own), w_at(2, p_own), w3_send, w3_recv, {"tp": jnp.where(z == 1, 0, 3)})

    @pl.when(is_mid)
    def _():
        load_w(fl_ref, 2).wait()
        w3.start()

    o_load.wait()
    for c in range(chunks):
        @pl.when(z > 0)
        def _(c=c):
            o_own(c, 0).start()

        @pl.when(z < 3)
        def _(c=c):
            o_own(c, 1).start()

    for j in range(2):
        load_w(fl_ref, j).wait()
        spread_own(j)

    def tile_loads(n, slot):
        at = pl.ds(pl.multiple_of(n * n_tile, n_tile), n_tile)
        return (pltpu.make_async_copy(wown_ref.at[:, at], wtile.at[slot], tile_sem.at[0, slot]),
                pltpu.make_async_copy(x_ref.at[:, at], xtile.at[slot], tile_sem.at[1, slot]))

    n_steps = width // n_tile
    for cpy in tile_loads(0, 0):
        cpy.start()

    def own_step(n, _):
        slot = lax.rem(n, 2)

        @pl.when(n + 1 < n_steps)
        def _():
            for cpy in tile_loads(n + 1, 1 - slot):
                cpy.start()

        for cpy in tile_loads(n, slot):
            cpy.wait()
        at = pl.ds(pl.multiple_of(n * n_tile, n_tile), n_tile)
        acc[:, at] = xtile[slot].astype(F32) + jnp.dot(obuf[z], wtile[slot], preferred_element_type=F32)
        return 0

    lax.fori_loop(0, n_steps, own_step, 0)

    def add_shard(j, s):
        def step(n, _):
            at = pl.ds(pl.multiple_of(n * n_tile, n_tile), n_tile)
            acc[:, at] += jnp.dot(obuf[s], wbuf[j, :, at], preferred_element_type=F32)
            return 0

        lax.fori_loop(0, n_steps, step, 0)

    spread_relay(0)
    spread_relay(1)

    @pl.when(is_end)
    def _():
        remote(w_at(2, p_own), w_at(2, p_own), w3_send, w3_recv, left).wait_recv()

    spread_own(2)

    @pl.when(is_mid)
    def _():
        for c in range(chunks):
            o_pass(s1, c)
            o_pass(s2, c)

    spread_diag(0)
    spread_done(0)

    @pl.when(is_end)
    def _():
        for c in range(chunks):
            o_wait(s1, c)

    add_shard(0, s1)
    spread_diag(1)
    spread_done(1)

    @pl.when(is_mid)
    def _():
        for c in range(chunks):
            o_pass(s3, c)

    spread_relay(2)

    @pl.when(is_end)
    def _():
        for c in range(chunks):
            o_wait(s2, c)

    add_shard(1, s2)
    spread_diag(2)
    spread_done(2)

    y_steps = width // y_cols

    def y_copy(i):
        slot = lax.rem(i, 2)
        r_at = pl.ds(pl.multiple_of((i // y_steps) * c_rows, c_rows), c_rows)
        n_at = pl.ds(pl.multiple_of(lax.rem(i, y_steps) * y_cols, y_cols), y_cols)
        return pltpu.make_async_copy(ytile.at[slot], y_ref.at[r_at, n_at], y_sem.at[slot])

    def last_step(i, _):
        c = i // y_steps

        @pl.when(is_end & (lax.rem(i, y_steps) == 0))
        def _():
            o_wait(s3, c)

        @pl.when(i >= 2)
        def _():
            y_copy(i - 2).wait()

        r_at = pl.ds(pl.multiple_of(c * c_rows, c_rows), c_rows)
        n_at = pl.ds(pl.multiple_of(lax.rem(i, y_steps) * y_cols, y_cols), y_cols)
        ytile[lax.rem(i, 2)] = (acc[r_at, n_at] + jnp.dot(obuf[s3, r_at, :], wbuf[2, :, n_at], preferred_element_type=F32)).astype(BF16)
        y_copy(i).start()
        return 0

    total = chunks * y_steps
    lax.fori_loop(0, total, last_step, 0)
    y_copy(total - 2).wait()
    y_copy(total - 1).wait()

    for j in range(3):
        for kind in range(9):
            w_copy(j, kind).wait_send()
    for c in range(chunks):
        @pl.when(z > 0)
        def _(c=c):
            o_own(c, 0).wait_send()

        @pl.when(z < 3)
        def _(c=c):
            o_own(c, 1).wait_send()

    @pl.when(is_mid)
    def _():
        w3.wait_send()
        for c in range(chunks):
            for s in (s1, s2, s3):
                o_fwd(s, c, 0).wait_send()


def out_proj(o, fl, fr, fl2, fr2, w_own, x):
    rows, kdim = o.shape
    width = x.shape[1]
    dma = pltpu.SemaphoreType.DMA
    return pl.pallas_call(
        out_kernel,
        in_specs=[pl.BlockSpec(memory_space=HBM)] * 7,
        out_specs=pl.BlockSpec(memory_space=HBM),
        out_shape=jax.ShapeDtypeStruct((rows, width), BF16),
        scratch_shapes=[
            VMEM((3, kdim, width), BF16),
            VMEM((2, kdim, 512), BF16),
            VMEM((2, rows, 512), BF16),
            VMEM((4, rows, kdim), BF16),
            VMEM((rows, width), F32),
            VMEM((2, rows // 4, 1024), BF16),
            dma((4,)), dma((2, 2)), dma((2,)), dma((3, 9)), dma((3, 9)), dma, dma,
            dma((2, 4)), dma((4, 4)), dma((4, 4)),
        ],
        compiler_params=pltpu.CompilerParams(collective_id=1, has_side_effects=True, vmem_limit_bytes=62 << 20),
        name="out_proj",
    )(o, fl, fr, fl2, fr2, w_own, x)


def solution(mesh):
    def local_step(x_in, doc_id, pos_in_doc, norm_gain, w_q, w_k, w_v, w_o, inv_freq):
        rows = x_in.shape[0]
        piece = rows // 2
        dp, cp = lax.axis_index("dp"), lax.axis_index("cp")
        n_cp = 4
        slice_rows = w_o.shape[0] // 8
        w_slice = lax.dynamic_slice(w_o, ((dp * 4 + cp) * slice_rows, 0), (slice_rows, w_o.shape[1]))
        fl = lax.ppermute(w_slice, "tp", [(0, 1), (1, 2), (2, 3)])
        fr = lax.ppermute(w_slice, "tp", [(1, 0), (2, 1), (3, 2)])

        angle = pos_in_doc.astype(F32)[:, None] * inv_freq[None, :]
        cos_h, sin_h = jnp.cos(angle), jnp.sin(angle)
        cos_t = jnp.concatenate([cos_h, cos_h], axis=-1)
        sin_t = jnp.concatenate([-sin_h, sin_h], axis=-1)
        h, kv = norm_kv(x_in, norm_gain, w_k, w_v, cos_t, sin_t)
        kv_y = lax.ppermute(kv, "cp", [(0, 2), (1, 3), (2, 0), (3, 1)])
        kv_c = lax.ppermute(kv, "cp", [(0, 1), (1, 0), (2, 3), (3, 2)])
        q = q_proj(h, w_q, cos_t, sin_t)
        fl2 = lax.ppermute(fl, "tp", [(1, 2), (2, 3)])
        fr2 = lax.ppermute(fr, "tp", [(1, 0), (2, 1)])
        kv_yc = lax.ppermute(kv_y, "cp", [(0, 1), (1, 0), (2, 3), (3, 2)])

        loc = jnp.arange(rows)
        tok = jnp.where(loc < piece, cp * piece + loc, (2 * n_cp - 1 - cp) * piece + loc - piece).astype(jnp.int32)
        o = attention(q, [kv, kv_c, kv_y, kv_yc], tok, pos_in_doc, cp)
        y = out_proj(o, fl, fr, fl2, fr2, w_o, x_in)
        cols = w_k.shape[1]
        k_out = kv[:, :cols].reshape(rows, cols // HEAD, HEAD)
        v_out = kv[:, cols:].reshape(rows, cols // HEAD, HEAD)
        return y, k_out, v_out

    row_spec = P(("dp", "cp"))
    in_specs = (P(("dp", "cp"), None), row_spec, row_spec, P(), P(None, "tp"), P(None, "tp"), P(None, "tp"), P("tp", None), P())
    out_specs = (P(("dp", "cp"), None), P(("dp", "cp"), "tp", None), P(("dp", "cp"), "tp", None))
    return jax.shard_map(local_step, mesh=mesh, in_specs=in_specs, out_specs=out_specs, check_vma=False)
```

time: 833 us -> 270 us (0.32)
  waiting for transfers between devices: 572 us -> 17.7 us
  Pallas kernels: 0 us -> 208 us
  matrix products: 202 us -> 0 us
  other arithmetic: 24.5 us -> 3.64 us
  local copies, waits for them, and re-layouts: 13.7 us -> 27.6 us
  between operations: 13.9 us -> 0.79 us
  starting transfers between devices: 0.3 us -> 11.8 us
    psum x1 -> x0, waiting for transfers between devices: 558 us -> none  [local_step(): full_sum = lax.psum(part_sum, 'tp')]
    pallas_call x0 -> x4, Pallas kernels: none -> 208 us  [the longest x1 167 us: out_proj(): pl.pallas_call(out_kernel, in_specs=[pl.BlockSpec(memory_space=HBM)] * 7,...]
    dot_general x12 -> x0, matrix products: 114 us -> none  [the longest x8 75.5 us: attend(): jnp.einsum('ngqk,knd->qngd', attn_probs, val_rows, preferred_element_type...]
    sub x8 -> x0, matrix products: 88 us -> none  [attend(): attn_probs = jax.nn.softmax(scores, axis=-1).astype(jnp.bfloat16)]
    ppermute x0 -> x7, waiting for transfers between devices: none -> 17.7 us  [the longest x1 13.9 us: local_step(): kv_y = lax.ppermute(kv, 'cp', [(0, 2), (1, 3), (2, 0), (3, 1)])]
    all_gather x2 -> x0, waiting for transfers between devices: 13.9 us -> none  [the longest x1 13.9 us: local_step(): v_all = lax.all_gather(v_new, 'cp', tiled=True)]
    convert_element_type x2 -> x1, other arithmetic: 13 us -> 0.69 us  [local_step(): angle = pos_in_doc.astype(F32)[:, None] * inv_freq[None, :]]
    ppermute x0 -> x7, starting transfers between devices: none -> 11.8 us  [the longest x1 4.53 us: local_step(): fl = lax.ppermute(w_slice, 'tp', [(0, 1), (1, 2), (2, 3)])]
  transfers between devices with their start and end apart: 3 -> 7, of which waited for: 2 -> 3; matrix products, arithmetic and copies ran while one was open for 4% -> 3% of each run, Pallas kernels for 0% -> 9%
where the time goes in v1:
time: 270 us; the launch traced here: 269 us
  Pallas kernels  208 us (77%)
  local copies, waits for them, and re-layouts  27.6 us (10%)
  waiting for transfers between devices  17.7 us (7%)
  starting transfers between devices  11.8 us (4%)
  other arithmetic  3.64 us (1%)
    pallas_call x1, Pallas kernels, out_proj(): pl.pallas_call(out_kernel, in_specs=[pl.BlockSpec(memory_space=HBM)] * 7,...  167 us
    unnamed x15, local copies, waits for them, and re-layouts  19.9 us
    pallas_call x1, Pallas kernels, norm_kv(): pl.pallas_call(kv_kernel, grid=(rows // tile,), in_specs=[pl.BlockSpec((t...  16.4 us
    ppermute x1, waiting for transfers between devices, local_step(): kv_y = lax.ppermute(kv, 'cp', [(0, 2), (1, 3), (2, 0), (3, 1)])  13.9 us
    pallas_call x1, Pallas kernels, attention(): pl.pallas_call(functools.partial(attn_kernel, n_cp, group), grid_spec=plt...  12.3 us
    pallas_call x1, Pallas kernels, q_proj(): pl.pallas_call(q_kernel, grid=(cols // tile,), in_specs=[pl.BlockSpec((ro...  11.6 us
  transfers between devices with their start and end apart: 7, of which 3 were waited for; matrix products, arithmetic and copies ran while one was open for 3% of the time, Pallas kernels for 9%

profile of v1, /device:TPU:0, one launch (start us, length us, event | category | flops | bytes accessed | tf_op | source)
XLA Modules:
  0.0 269.0 jit_solution(9546078763143131728)
XLA Ops:
  0.6 0.7 convert_element_type.3
  1.3 2.6 fusion
  3.9 0.3 pad_maximum_fusion
  4.2 1.6 copy-done.1
  5.8 1.6 copy-done.2
  7.4 0.7 copy-done.3
  8.1 16.4 %norm_kv.1 = (bf16[1024,4096]{1,0:T(8,128)(2,1)S(1)}, bf16[1024,512]{1,0:T(8,128)(2,1)S(1)}) custom-call(bf16[1024,4096]{1,0:T(8,128)(2,1)} %x_ref.3, f32[1,4096]{1,0:T(1,128)S(1)} %bitcast.10, bf16[4096,256]{1,0:T(8,128)(2,1)S(1)} %copy-done.1, bf16[4096,256]{1,0:T(8,128)(2,1)S(1)} %copy-done.2, f32[1024,128]{1,0:T(8,128)S(1)} %get-tuple-element.12.cos_ref, ...), custom_call_target="tpu_custom_call" | custom-call | flops 4294967296 | bytes 22020096 | tf_op jit(solution)/shard_map/norm_kv/pallas_call | solution.py:52
  24.5 0.0 copy-start.4
  24.5 3.4 %copy-done.4 = bf16[1024,4096]{1,0:T(8,128)(2,1)} copy-done((bf16[1024,4096]{1,0:T(8,128)(2,1)}, bf16[1024,4096]{1,0:T(8,128)(2,1)S(1)}, u32[]{:S(2)}) %copy-start.4) | copy-done | bytes 8388632
  27.9 3.0 %collective-permute-start.1 = (bf16[1024,512]{1,0:T(8,128)(2,1)S(1)}, bf16[1024,512]{1,0:T(8,128)(2,1)}, u32[]{:S(2)}, u32[]{:S(2)}) collective-permute-start(bf16[1024,512]{1,0:T(8,128)(2,1)S(1)} %get-tuple-element.6.kv0), channel_id=1, source_target_pairs={{0,2},{1,3},{2,0},{3,1},{4,6},{5,7},{6,4},{7,5},{8,10},{9,11},{10,... | collective-permute-start | bytes 3145736 | tf_op jit(solution)/shard_map/ppermute | solution.py:507
  31.0 2.3 constant_dynamic-slice_fusion
  33.2 4.5 %collective-permute-start.3 = (bf16[128,4096]{1,0:T(8,128)(2,1)}, bf16[128,4096]{1,0:T(8,128)(2,1)}, u32[]{:S(2)}, u32[]{:S(2)}) collective-permute-start(bf16[128,4096]{1,0:T(8,128)(2,1)} %constant_dynamic-slice_fusion), channel_id=1, source_target_pairs={{0,4},{4,8},{8,12},{1,5},{5,9},{9,13},{2,6},{6,10},{10,14},{3,7},{... | collective-permute-start | bytes 3145736 | tf_op jit(solution)/shard_map/ppermute | solution.py:499
  37.8 1.3 collective-permute-start.4
  39.1 0.1 collective-permute-start
  39.2 1.0 fusion.1
  40.2 13.9 %collective-permute-done.1.kv2 = bf16[1024,512]{1,0:T(8,128)(2,1)} collective-permute-done((bf16[1024,512]{1,0:T(8,128)(2,1)S(1)}, bf16[1024,512]{1,0:T(8,128)(2,1)}, u32[]{:S(2)}, u32[]{:S(2)}) %collective-permute-start.1) | collective-permute-done | bytes 1048608 | tf_op jit(solution)/shard_map/ppermute | solution.py:507
  54.1 0.1 slice.13
  54.2 0.1 slice.12.gidx_ref
  54.3 0.2 copy.11.pos_ref
  54.5 2.0 reshape.43
  56.5 2.0 reshape.44
  58.5 0.1 stack.35.place_ref
  58.6 0.2 collective-permute-done.3.fl_ref
  58.8 1.6 collective-permute-start.5
  60.5 3.5 %collective-permute-done.4.fr_ref = bf16[128,4096]{1,0:T(8,128)(2,1)} collective-permute-done((bf16[128,4096]{1,0:T(8,128)(2,1)}, bf16[128,4096]{1,0:T(8,128)(2,1)}, u32[]{:S(2)}, u32[]{:S(2)}) %collective-permute-start.4) | collective-permute-done | bytes 1048608 | tf_op jit(solution)/shard_map/ppermute | solution.py:500
  64.0 1.3 collective-permute-start.6
  65.3 3.4 %copy-done.5 = bf16[1024,4096]{1,0:T(8,128)(2,1)S(1)} copy-done((bf16[1024,4096]{1,0:T(8,128)(2,1)S(1)}, bf16[1024,4096]{1,0:T(8,128)(2,1)}, u32[]{:S(2)}) %copy-start.5) | copy-done | bytes 8388632
  68.7 11.6 %q_proj.1.q_ref = bf16[1024,1024]{1,0:T(8,128)(2,1)S(1)} custom-call(bf16[1024,4096]{1,0:T(8,128)(2,1)S(1)} %copy-done.5, bf16[4096,1024]{1,0:T(8,128)(2,1)} %wq_ref.1, f32[1024,128]{1,0:T(8,128)S(1)} %get-tuple-element.12.cos_ref, f32[1024,128]{1,0:T(8,128)S(1)} %get-tuple-element.13.sin_ref), custom_call_target="tpu_custom_call" | custom-call | flops 8589934592 | bytes 18874368 | tf_op jit(solution)/shard_map/q_proj/pallas_call | solution.py:83
  80.3 12.3 %attn.1.o_ref = bf16[1024,1024]{1,0:T(8,128)(2,1)S(1)} custom-call(s32[8]{0:T(128)S(1)} %slice.12.gidx_ref, s32[8]{0:T(128)S(1)} %and_select_fusion.low_ref, s32[8]{0:T(128)S(1)} %stack.35.place_ref, bf16[1024,1024]{1,0:T(8,128)(2,1)S(1)} %q_proj.1.q_ref, s32[1024,1]{1,0:T(8,128)S(1)} %add_select_fusion.tok_ref, s32[1024,1]{1,0:T(8,128)S(1)} %copy.11.pos_ref, ...), custom_call_target="tpu_custom_call" | custom-call | flops 5368709120 | bytes 8388608 | tf_op jit(solution)/shard_map/attn/pallas_call | solution.py:172
  92.6 1.3 copy-done
  93.9 167.2 %out_proj.1 = bf16[1024,4096]{1,0:T(8,128)(2,1)} custom-call(bf16[1024,1024]{1,0:T(8,128)(2,1)} %copy-done, bf16[128,4096]{1,0:T(8,128)(2,1)} %collective-permute-done.3.fl_ref, bf16[128,4096]{1,0:T(8,128)(2,1)} %collective-permute-done.4.fr_ref, bf16[128,4096]{1,0:T(8,128)(2,1)} %collective-permute-done.5.fl2_ref, ...), custom_call_target="tpu_custom_call" | custom-call | tf_op jit(solution)/shard_map/out_proj/pallas_call | solution.py:471
  261.2 7.9 %copy.13 = bf16[1024,4096]{1,0:T(8,128)(2,1)} copy(bf16[1024,4096]{1,0:T(8,128)(2,1)} %out_proj.1) | data formatting | bytes 16777216
  (15 shorter events, 0.1 us)
Async XLA Ops:
  4.2 1.6 copy-start.1
  5.8 1.6 copy-start.2
  7.4 0.7 copy-start.3
  8.1 46.0 %copy-start.6 = (s32[1024]{0:T(1024)S(1)}, s32[1024]{0:T(1024)}, u32[]{:S(2)}) copy-start(s32[1024]{0:T(1024)} %param.10) | copy-start | bytes 12292
  24.5 3.4 %copy-start.4 = (bf16[1024,4096]{1,0:T(8,128)(2,1)}, bf16[1024,4096]{1,0:T(8,128)(2,1)S(1)}, u32[]{:S(2)}) copy-start(bf16[1024,4096]{1,0:T(8,128)(2,1)S(1)} %get-tuple-element.5.h_ref) | copy-start | bytes 25165828
  27.9 26.2 %collective-permute-start.1 = (bf16[1024,512]{1,0:T(8,128)(2,1)S(1)}, bf16[1024,512]{1,0:T(8,128)(2,1)}, u32[]{:S(2)}, u32[]{:S(2)}) collective-permute-start(bf16[1024,512]{1,0:T(8,128)(2,1)S(1)} %get-tuple-element.6.kv0), channel_id=1, source_target_pairs={{0,2},{1,3},{2,0},{3,1},{4,6},{5,7},{6,4},{7,5},{8,10},{9,11},{10,... | collective-permute-start | bytes 3145736 | tf_op jit(solution)/shard_map/ppermute | solution.py:507
  33.2 25.6 %collective-permute-start.3 = (bf16[128,4096]{1,0:T(8,128)(2,1)}, bf16[128,4096]{1,0:T(8,128)(2,1)}, u32[]{:S(2)}, u32[]{:S(2)}) collective-permute-start(bf16[128,4096]{1,0:T(8,128)(2,1)} %constant_dynamic-slice_fusion), channel_id=1, source_target_pairs={{0,4},{4,8},{8,12},{1,5},{5,9},{9,13},{2,6},{6,10},{10,14},{3,7},{... | collective-permute-start | bytes 3145736 | tf_op jit(solution)/shard_map/ppermute | solution.py:499
  37.8 26.2 %collective-permute-start.4 = (bf16[128,4096]{1,0:T(8,128)(2,1)}, bf16[128,4096]{1,0:T(8,128)(2,1)}, u32[]{:S(2)}, u32[]{:S(2)}) collective-permute-start(bf16[128,4096]{1,0:T(8,128)(2,1)} %constant_dynamic-slice_fusion), channel_id=1, source_target_pairs={{4,0},{8,4},{12,8},{5,1},{9,5},{13,9},{6,2},{10,6},{14,10},{7,3},{... | collective-permute-start | bytes 3145736 | tf_op jit(solution)/shard_map/ppermute | solution.py:500
  39.1 41.2 %collective-permute-start = (bf16[1024,512]{1,0:T(8,128)(2,1)S(1)}, bf16[1024,512]{1,0:T(8,128)(2,1)}, u32[]{:S(2)}, u32[]{:S(2)}) collective-permute-start(bf16[1024,512]{1,0:T(8,128)(2,1)S(1)} %get-tuple-element.6.kv0), channel_id=1, source_target_pairs={{0,1},{1,0},{2,3},{3,2},{4,5},{5,4},{6,7},{7,6},{8,9},{9,8},{10,11... | collective-permute-start | bytes 3145736 | tf_op jit(solution)/shard_map/ppermute | solution.py:508
  54.1 26.1 %collective-permute-start.2 = (bf16[1024,512]{1,0:T(8,128)(2,1)}, bf16[1024,512]{1,0:T(8,128)(2,1)}, u32[]{:S(2)}, u32[]{:S(2)}) collective-permute-start(bf16[1024,512]{1,0:T(8,128)(2,1)} %collective-permute-done.1.kv2), channel_id=1, source_target_pairs={{0,1},{1,0},{2,3},{3,2},{4,5},{5,4},{6,7},{7,6},{8,9},{9,8},{10,11... | collective-permute-start | bytes 3145736 | tf_op jit(solution)/shard_map/ppermute | solution.py:512
  58.8 35.1 %collective-permute-start.5 = (bf16[128,4096]{1,0:T(8,128)(2,1)}, bf16[128,4096]{1,0:T(8,128)(2,1)}, u32[]{:S(2)}, u32[]{:S(2)}) collective-permute-start(bf16[128,4096]{1,0:T(8,128)(2,1)} %collective-permute-done.3.fl_ref), channel_id=1, source_target_pairs={{4,8},{8,12},{5,9},{9,13},{6,10},{10,14},{7,11},{11,15},{20,24},{2... | collective-permute-start | bytes 3145736 | tf_op jit(solution)/shard_map/ppermute | solution.py:510
  64.0 29.9 %collective-permute-start.6 = (bf16[128,4096]{1,0:T(8,128)(2,1)}, bf16[128,4096]{1,0:T(8,128)(2,1)}, u32[]{:S(2)}, u32[]{:S(2)}) collective-permute-start(bf16[128,4096]{1,0:T(8,128)(2,1)} %collective-permute-done.4.fr_ref), channel_id=1, source_target_pairs={{4,0},{8,4},{5,1},{9,5},{6,2},{10,6},{7,3},{11,7},{20,16},{24,20},... | collective-permute-start | bytes 3145736 | tf_op jit(solution)/shard_map/ppermute | solution.py:511
  65.3 3.4 %copy-start.5 = (bf16[1024,4096]{1,0:T(8,128)(2,1)S(1)}, bf16[1024,4096]{1,0:T(8,128)(2,1)}, u32[]{:S(2)}) copy-start(bf16[1024,4096]{1,0:T(8,128)(2,1)} %copy-done.4) | copy-start | bytes 25165828
  92.6 1.3 copy-start

commit v2 on v1

v2 whole, which is shorter than its diff:
```python
import functools

import jax
import jax.numpy as jnp
from jax import lax
from jax.experimental import pallas as pl
from jax.experimental.pallas import tpu as pltpu
from jax.sharding import PartitionSpec as P

MESH = pl.DeviceIdType.MESH
HBM = pltpu.HBM
VMEM = pltpu.VMEM
HEAD = 128
Q_TILE = 128
F32 = jnp.float32
BF16 = jnp.bfloat16


def rope(vec, cos_t, sin_t):
    vec = vec.astype(F32)
    return (vec * cos_t + pltpu.roll(vec, HEAD // 2, 1) * sin_t).astype(BF16)


def proj_kernel(x_ref, gain_ref, wk_ref, wv_ref, wq_ref, wo_ref, cos_ref, sin_ref,
                q_ref, kvg_ref, fla_ref, flb_ref, fra_ref, frb_ref, fl2_ref, fr2_ref,
                xbuf, hbuf, invbuf, wkbuf, wvbuf, wqbuf, kvbuf, qbuf,
                x_sem, w_sem, wq_sem, kvl_sem, q_sem, kv_send, kv_recv, r1_send, r1_recv, r2_send, r2_recv):
    chunks, q_tiles = 4, 4
    rows, width = hbuf.shape
    c_rows = rows // chunks
    piece = rows // 2
    cols = wkbuf.shape[1]
    q_cols = wqbuf.shape[2]
    half = fla_ref.shape[0]
    n_cp = 4
    dp, z, cp = lax.axis_index("dp"), lax.axis_index("tp"), lax.axis_index("cp")
    core_cp = cp + 1 - 2 * lax.rem(cp, 2)
    y_cp = lax.rem(cp + 2, 4)
    core, ynb = {"cp": core_cp}, {"cp": y_cp}
    left = {"tp": jnp.maximum(z - 1, 0)}
    right = {"tp": jnp.minimum(z + 1, 3)}
    is_mid = (z == 1) | (z == 2)

    def remote(src, dst, ssem, rsem, dev):
        return pltpu.make_async_remote_copy(src_ref=src, dst_ref=dst, send_sem=ssem, recv_sem=rsem, device_id=dev, device_id_type=MESH)

    barrier = pltpu.get_barrier_semaphore()
    for dev in (core, ynb):
        pl.semaphore_signal(barrier, inc=1, device_id=dev, device_id_type=MESH)

    @pl.when(z > 0)
    def _():
        pl.semaphore_signal(barrier, inc=1, device_id=left, device_id_type=MESH)

    @pl.when(z < 3)
    def _():
        pl.semaphore_signal(barrier, inc=1, device_id=right, device_id_type=MESH)

    def x_load(c):
        return pltpu.make_async_copy(x_ref.at[pl.ds(c * c_rows, c_rows)], xbuf.at[c], x_sem.at[c])

    def wq_load(t):
        return pltpu.make_async_copy(wq_ref.at[:, pl.ds(t * q_cols, q_cols)], wqbuf.at[t], wq_sem.at[t])

    wk_load = pltpu.make_async_copy(wk_ref, wkbuf, w_sem.at[0])
    wv_load = pltpu.make_async_copy(wv_ref, wvbuf, w_sem.at[1])
    x_load(0).start()
    wk_load.start()
    wv_load.start()
    for c in range(1, chunks):
        x_load(c).start()
    for t in range(q_tiles):
        wq_load(t).start()

    @pl.when(is_mid)
    def _():
        pl.semaphore_wait(barrier, 4)

    @pl.when(jnp.logical_not(is_mid))
    def _():
        pl.semaphore_wait(barrier, 3)

    p_own = dp * 4 + cp

    def r1(side, part):
        src = wo_ref.at[pl.ds(pl.multiple_of((p_own * 2 + part) * half, half), half)]
        dst = ((fra_ref, frb_ref), (fla_ref, flb_ref))[side][part]
        return remote(src, dst, r1_send.at[side, part], r1_recv.at[side, part], (left, right)[side])

    def r2(side):
        src = (fra_ref, fla_ref)[side]
        dst = (fr2_ref, fl2_ref)[side]
        return remote(src, dst, r2_send.at[side], r2_recv.at[side], (left, right)[side])

    for part in range(2):
        @pl.when(z > 0)
        def _(part=part):
            r1(0, part).start()

        @pl.when(z < 3)
        def _(part=part):
            r1(1, part).start()

    def kv_at(owner, c):
        start = jnp.where(c < chunks // 2, owner, 2 * n_cp - 1 - owner) * piece + (c % (chunks // 2)) * c_rows
        return kvg_ref.at[pl.ds(pl.multiple_of(start, c_rows), c_rows)]

    def kv_local(c):
        return pltpu.make_async_copy(kvbuf.at[pl.ds(c * c_rows, c_rows)], kv_at(cp, c), kvl_sem.at[c])

    def kv_copy(kind, c):
        at = kv_at((cp, cp, y_cp)[kind], c)
        return remote(at, at, kv_send.at[kind, c], kv_recv.at[kind, c], (ynb, core, core)[kind])

    def kv_wait(kind, c):
        at = kv_at((y_cp, core_cp, lax.rem(core_cp + 2, 4))[kind], c)
        remote(at, at, kv_send.at[kind, c], kv_recv.at[kind, c], core).wait_recv()

    def kv_out(c):
        kv_local(c).wait()
        kv_copy(0, c).start()
        kv_copy(1, c).start()

    step = 16

    def full(t):
        return jnp.concatenate([t, t], axis=-1)

    def turn(vec, r_at):
        cos_h, sin_h = cos_ref[r_at, :], sin_ref[r_at, :]
        return rope(vec, full(cos_h), jnp.concatenate([-sin_h, sin_h], axis=-1))

    for c in range(chunks):
        x_load(c).wait()

        def square_rows(i, _, c=c):
            at = pl.ds(pl.multiple_of(i * step, step), step)
            xf = xbuf[c, at, :].astype(F32)
            mean = jnp.sum(xf * xf, axis=-1, keepdims=True) * (1.0 / width)
            invbuf[at, :] = jnp.broadcast_to(lax.rsqrt(mean + 1e-5), (step, HEAD))
            return 0

        def norm_rows(i, _, c=c):
            at = pl.ds(pl.multiple_of(i * step, step), step)
            to = pl.ds(pl.multiple_of(c * c_rows + i * step, step), step)
            inv = invbuf[at, 0:1]
            hbuf[to, :] = (xbuf[c, at, :].astype(F32) * inv * gain_ref[...]).astype(BF16)
            return 0

        lax.fori_loop(0, c_rows // step, square_rows, 0, unroll=4)
        lax.fori_loop(0, c_rows // step, norm_rows, 0, unroll=2)
        if c == 0:
            wk_load.wait()
            wv_load.wait()
        r_at = pl.ds(c * c_rows, c_rows)
        h = hbuf[r_at, :]
        k_new = jnp.dot(h, wkbuf[...], preferred_element_type=F32).astype(BF16)
        v_new = jnp.dot(h, wvbuf[...], preferred_element_type=F32).astype(BF16)
        for j in range(cols // HEAD):
            kvbuf[r_at, j * HEAD:(j + 1) * HEAD] = turn(k_new[:, j * HEAD:(j + 1) * HEAD], r_at)
        kvbuf[r_at, cols:] = v_new
        kv_local(c).start()
        if c > 0:
            kv_out(c - 1)

    @pl.when(z > 0)
    def _():
        r1(1, 0).wait_recv()

    @pl.when(z < 3)
    def _():
        r1(0, 0).wait_recv()

    @pl.when(is_mid)
    def _():
        r2(0).start()
        r2(1).start()

    def q_out(t):
        return pltpu.make_async_copy(qbuf.at[t], q_ref.at[:, pl.ds(t * q_cols, q_cols)], q_sem.at[t])

    def q_tile(t):
        wq_load(t).wait()
        q_new = jnp.dot(hbuf[...], wqbuf[t], preferred_element_type=F32).astype(BF16)
        everything = pl.ds(0, rows)
        for j in range(q_cols // HEAD):
            qbuf[t, :, j * HEAD:(j + 1) * HEAD] = turn(q_new[:, j * HEAD:(j + 1) * HEAD], everything)
        q_out(t).start()

    q_tile(0)
    kv_out(chunks - 1)
    q_tile(1)
    for c in range(2):
        kv_wait(0, c)
        kv_copy(2, c).start()
    q_tile(2)
    q_tile(3)
    for c in range(2, chunks):
        kv_wait(0, c)
        kv_copy(2, c).start()
    for c in range(chunks):
        kv_wait(1, c)
        kv_wait(2, c)
    for t in range(q_tiles):
        q_out(t).wait()

    @pl.when(z > 0)
    def _():
        r1(1, 1).wait_recv()
        for part in range(2):
            r1(0, part).wait_send()

    @pl.when(z < 3)
    def _():
        r1(0, 1).wait_recv()
        for part in range(2):
            r1(1, part).wait_send()

    @pl.when(z > 1)
    def _():
        r2(1).wait_recv()

    @pl.when(z < 2)
    def _():
        r2(0).wait_recv()

    @pl.when(is_mid)
    def _():
        r2(0).wait_send()
        r2(1).wait_send()

    for c in range(chunks):
        for kind in range(3):
            kv_copy(kind, c).wait_send()


def project(x, gain, w_k, w_v, w_q, w_o, cos_h, sin_h):
    rows, width = x.shape
    cols = w_k.shape[1]
    q_cols = w_q.shape[1]
    half = w_o.shape[0] // 16
    dma = pltpu.SemaphoreType.DMA
    out = jax.ShapeDtypeStruct
    hbm = pl.BlockSpec(memory_space=HBM)
    vmem = pl.BlockSpec(memory_space=VMEM)
    return pl.pallas_call(
        proj_kernel,
        in_specs=[hbm, vmem, hbm, hbm, hbm, hbm, vmem, vmem],
        out_specs=[hbm] * 8,
        out_shape=[out((rows, q_cols), BF16), out((4 * rows, 2 * cols), BF16)] + [out((half, w_o.shape[1]), BF16)] * 6,
        scratch_shapes=[
            VMEM((4, rows // 4, width), BF16),
            VMEM((rows, width), BF16),
            VMEM((rows // 4, HEAD), F32),
            VMEM((width, cols), BF16),
            VMEM((width, cols), BF16),
            VMEM((4, width, q_cols // 4), BF16),
            VMEM((rows, 2 * cols), BF16),
            VMEM((4, rows, q_cols // 4), BF16),
            dma((4,)), dma((2,)), dma((4,)), dma((4,)), dma((4,)),
            dma((3, 4)), dma((3, 4)), dma((2, 2)), dma((2, 2)), dma((2,)), dma((2,)),
        ],
        compiler_params=pltpu.CompilerParams(collective_id=0, has_side_effects=True, vmem_limit_bytes=48 << 20),
        cost_estimate=pl.CostEstimate(flops=2 * rows * width * (2 * cols + q_cols), bytes_accessed=24 << 20, transcendentals=0),
        name="proj",
    )(x, gain.reshape(1, width), w_k, w_v, w_q, w_o, cos_h, sin_h)


def attn_kernel(group, pos_smem, q_ref, pos_ref, kv_ref, o_ref):
    head, blk = pl.program_id(0), pl.program_id(1)
    half_blks = pl.num_programs(1) // 2
    piece = half_blks * Q_TILE
    cp = lax.axis_index("cp")
    q_rows = q_ref.shape[0]
    kv_cols = kv_ref.shape[1] // 2
    q = jnp.concatenate([q_ref[:, g * HEAD:(g + 1) * HEAD] for g in range(group)], axis=0)
    pieces = kv_ref.shape[0] // piece
    g0 = jnp.where(blk < half_blks, cp * piece + blk * Q_TILE, (pieces - 1 - cp) * piece + (blk - half_blks) * Q_TILE)
    low = (g0 - pos_smem[blk * Q_TILE]) // Q_TILE
    tok_1 = g0 + lax.broadcasted_iota(jnp.int32, (q_rows, 1), 0)
    tok = jnp.concatenate([tok_1] * group, axis=0)
    first = jnp.concatenate([tok_1 - pos_ref[...]] * group, axis=0)
    scale = HEAD ** -0.5
    k_at = pl.ds(pl.multiple_of(head * HEAD, HEAD), HEAD)
    v_at = pl.ds(pl.multiple_of(kv_cols + head * HEAD, HEAD), HEAD)

    def scores(start, width):
        keys = kv_ref[pl.ds(pl.multiple_of(start, Q_TILE), width), k_at]
        s = lax.dot_general(q, keys, (((1,), (1,)), ((), ())), preferred_element_type=F32) * scale
        u = start + lax.broadcasted_iota(jnp.int32, (1, width), 1)
        return jnp.where((u >= first) & (u <= tok), s, -1e30)

    def values(start, width):
        return kv_ref[pl.ds(pl.multiple_of(start, Q_TILE), width), v_at]

    near = jnp.maximum(g0 - Q_TILE, 0)
    s = scores(near, 2 * Q_TILE)
    m = jnp.max(s, axis=-1, keepdims=True)
    p = jnp.exp(s - m)
    total = jnp.sum(p, axis=-1, keepdims=True)
    acc = jnp.dot(p.astype(BF16), values(near, 2 * Q_TILE), preferred_element_type=F32)

    def far(i, carry):
        m, total, acc = carry
        start = i * Q_TILE
        s = scores(start, Q_TILE)
        m_new = jnp.maximum(m, jnp.max(s, axis=-1, keepdims=True))
        old = jnp.exp(m - m_new)
        p = jnp.exp(s - m_new)
        total = total * old + jnp.sum(p, axis=-1, keepdims=True)
        acc = acc * old + jnp.dot(p.astype(BF16), values(start, Q_TILE), preferred_element_type=F32)
        return m_new, total, acc

    m, total, acc = lax.fori_loop(low, near // Q_TILE, far, (m, total, acc))
    out = (acc / total).astype(BF16)
    for g in range(group):
        o_ref[:, g * HEAD:(g + 1) * HEAD] = out[g * q_rows:(g + 1) * q_rows]


def attention(q, kvg, pos):
    rows, q_cols = q.shape
    kv_cols = kvg.shape[1] // 2
    heads = kv_cols // HEAD
    group = q_cols // kv_cols
    q_map = lambda h, i, *_: (i, h)
    return pl.pallas_call(
        functools.partial(attn_kernel, group),
        grid_spec=pltpu.PrefetchScalarGridSpec(
            num_scalar_prefetch=1,
            grid=(heads, rows // Q_TILE),
            in_specs=[
                pl.BlockSpec((Q_TILE, group * HEAD), q_map),
                pl.BlockSpec((Q_TILE, 1), lambda h, i, *_: (i, 0)),
                pl.BlockSpec(kvg.shape, lambda h, i, *_: (0, 0)),
            ],
            out_specs=pl.BlockSpec((Q_TILE, group * HEAD), q_map),
        ),
        out_shape=jax.ShapeDtypeStruct((rows, q_cols), BF16),
        compiler_params=pltpu.CompilerParams(vmem_limit_bytes=32 << 20),
        cost_estimate=pl.CostEstimate(flops=5 << 30, bytes_accessed=8 << 20, transcendentals=0),
        name="attn",
    )(pos, q, pos[:, None], kvg)


def out_kernel(o_ref, fla_ref, flb_ref, fra_ref, frb_ref, fl2a_ref, fl2b_ref, fr2a_ref, fr2b_ref, wown_ref, x_ref, y_ref,
               wbuf, wtile, xtile, obuf, acc, ytile,
               load_sem, tile_sem, y_sem, wsend, wrecv, w3_send, w3_recv, own_send, fwd_send, o_recv):
    rows, kdim = o_ref.shape
    width = x_ref.shape[1]
    half = fla_ref.shape[0]
    slice_rows = 2 * half
    chunks = 4
    c_rows = rows // chunks
    n_tile = 512
    y_cols = ytile.shape[2]
    dp, z, cp = lax.axis_index("dp"), lax.axis_index("tp"), lax.axis_index("cp")
    is_end = (z == 0) | (z == 3)
    is_mid = (z == 1) | (z == 2)
    core = {"cp": cp + 1 - 2 * lax.rem(cp, 2)}
    ynb = {"cp": lax.rem(cp + 2, 4)}
    xnb = {"dp": 1 - dp}
    left = {"tp": jnp.maximum(z - 1, 0)}
    right = {"tp": jnp.minimum(z + 1, 3)}
    p_own = dp * 4 + cp
    p_x = (1 - dp) * 4 + cp
    p_y = dp * 4 + lax.rem(cp + 2, 4)
    p_d = (1 - dp) * 4 + lax.rem(cp + 2, 4)
    p_core = dp * 4 + cp + 1 - 2 * lax.rem(cp, 2)
    low_side = z < 2
    s1 = jnp.where(low_side, 1 - z, 5 - z)
    s2 = jnp.where(low_side, 2, 1)
    s3 = jnp.where(low_side, 3, 0)

    def remote(src, dst, ssem, rsem, dev):
        return pltpu.make_async_remote_copy(src_ref=src, dst_ref=dst, send_sem=ssem, recv_sem=rsem, device_id=dev, device_id_type=MESH)

    barrier = pltpu.get_barrier_semaphore()
    for dev in (core, ynb, xnb):
        pl.semaphore_signal(barrier, inc=1, device_id=dev, device_id_type=MESH)

    @pl.when(z > 0)
    def _():
        pl.semaphore_signal(barrier, inc=1, device_id=left, device_id_type=MESH)

    @pl.when(z < 3)
    def _():
        pl.semaphore_signal(barrier, inc=1, device_id=right, device_id_type=MESH)

    def w_at(j, p, start=0, n=None):
        n = slice_rows if n is None else n
        return wbuf.at[j, pl.ds(pl.multiple_of(p * slice_rows + start, half), n)]

    def load_w(src, j, part):
        return pltpu.make_async_copy(src, w_at(j, p_own, part * half, half), load_sem.at[j, part])

    fl, fr, fl2, fr2 = (fla_ref, flb_ref), (fra_ref, frb_ref), (fl2a_ref, fl2b_ref), (fr2a_ref, fr2b_ref)
    sources = ((fr, fr2, None), (fl, fr, fr2), (fr, fl, fl2), (fl, fl2, None))
    for zz in range(4):
        @pl.when(z == zz)
        def _(zz=zz):
            for j in range(3):
                if sources[zz][j] is not None:
                    for part in range(2):
                        load_w(sources[zz][j][part], j, part).start()

    @pl.when(is_end)
    def _():
        pl.semaphore_wait(barrier, 4)

    @pl.when(is_mid)
    def _():
        pl.semaphore_wait(barrier, 5)

    def w_copy(j, kind):
        dev = (xnb, ynb, core, ynb, xnb, core, core, core, core)[kind]
        src = (w_at(j, p_own), w_at(j, p_own), w_at(j, p_own), w_at(j, p_x, 0, half), w_at(j, p_y, half, half),
               w_at(j, p_x), w_at(j, p_y), w_at(j, p_d, 0, half), w_at(j, p_d, half, half))[kind]
        return remote(src, src, wsend.at[j, kind], wrecv.at[j, kind], dev)

    def core_p(p):
        return p + 1 - 2 * lax.rem(p, 2)

    def w_wait(j, kind):
        dst = (w_at(j, p_x), w_at(j, p_y), w_at(j, p_core), w_at(j, p_d, 0, half), w_at(j, p_d, half, half),
               w_at(j, core_p(p_x)), w_at(j, core_p(p_y)), w_at(j, core_p(p_d), 0, half), w_at(j, core_p(p_d), half, half))[kind]
        remote(dst, dst, wsend.at[j, kind], wrecv.at[j, kind], core).wait_recv()

    def spread_own(j):
        for kind in (0, 1, 2):
            w_copy(j, kind).start()

    def spread_relay(j):
        w_wait(j, 0)
        w_copy(j, 3).start()
        w_copy(j, 5).start()
        w_wait(j, 1)
        w_copy(j, 4).start()
        w_copy(j, 6).start()

    def spread_diag(j):
        w_wait(j, 3)
        w_copy(j, 7).start()
        w_wait(j, 4)
        w_copy(j, 8).start()

    def spread_done(j):
        for kind in (2, 5, 6, 7, 8):
            w_wait(j, kind)

    def slot_of(s, dev_z):
        return s - (s > dev_z).astype(jnp.int32)

    def o_at(s, c, dev_z=None):
        return obuf.at[slot_of(s, z if dev_z is None else dev_z), pl.ds(pl.multiple_of(c * c_rows, c_rows), c_rows)]

    def o_own(c, side):
        src = o_ref.at[pl.ds(c * c_rows, c_rows)]
        return remote(src, o_at(z, c, z + (-1, 1)[side]), own_send.at[side, c], o_recv.at[z, c], (left, right)[side])

    def o_fwd(s, c, side):
        return remote(o_at(s, c), o_at(s, c, z + (-1, 1)[side]), fwd_send.at[s, c], o_recv.at[s, c], (left, right)[side])

    def o_wait(s, c):
        remote(o_at(s, c), o_at(s, c), fwd_send.at[s, c], o_recv.at[s, c], left).wait_recv()

    def o_pass(s, c):
        o_wait(s, c)

        @pl.when(s < z)
        def _():
            o_fwd(s, c, 1).start()

        @pl.when(s > z)
        def _():
            o_fwd(s, c, 0).start()

    w3 = remote(w_at(2, p_own), w_at(2, p_own), w3_send, w3_recv, {"tp": jnp.where(z == 1, 0, 3)})

    @pl.when(is_mid)
    def _():
        for part in range(2):
            load_w(fla_ref, 2, part).wait()
        w3.start()

    for c in range(chunks):
        @pl.when(z > 0)
        def _(c=c):
            o_own(c, 0).start()

        @pl.when(z < 3)
        def _(c=c):
            o_own(c, 1).start()

    for j in range(2):
        for part in range(2):
            load_w(fla_ref, j, part).wait()
        spread_own(j)

    def tile_loads(n, slot):
        at = pl.ds(pl.multiple_of(n * n_tile, n_tile), n_tile)
        return (pltpu.make_async_copy(wown_ref.at[:, at], wtile.at[slot], tile_sem.at[0, slot]),
                pltpu.make_async_copy(x_ref.at[:, at], xtile.at[slot], tile_sem.at[1, slot]))

    n_steps = width // n_tile
    for cpy in tile_loads(0, 0):
        cpy.start()

    def own_step(n, _):
        slot = lax.rem(n, 2)

        @pl.when(n + 1 < n_steps)
        def _():
            for cpy in tile_loads(n + 1, 1 - slot):
                cpy.start()

        for cpy in tile_loads(n, slot):
            cpy.wait()
        at = pl.ds(pl.multiple_of(n * n_tile, n_tile), n_tile)
        acc[:, at] = xtile[slot].astype(F32) + jnp.dot(o_ref[...], wtile[slot], preferred_element_type=F32)
        return 0

    lax.fori_loop(0, n_steps, own_step, 0)

    def add_shard(j, s):
        def step(n, _):
            at = pl.ds(pl.multiple_of(n * n_tile, n_tile), n_tile)
            acc[:, at] += jnp.dot(obuf[slot_of(s, z)], wbuf[j, :, at], preferred_element_type=F32)
            return 0

        lax.fori_loop(0, n_steps, step, 0)

    spread_relay(0)
    spread_relay(1)

    @pl.when(is_end)
    def _():
        remote(w_at(2, p_own), w_at(2, p_own), w3_send, w3_recv, left).wait_recv()

    spread_own(2)

    @pl.when(is_mid)
    def _():
        for c in range(chunks):
            o_pass(s1, c)
            o_pass(s2, c)

    spread_diag(0)
    spread_done(0)

    @pl.when(is_end)
    def _():
        for c in range(chunks):
            o_wait(s1, c)

    add_shard(0, s1)
    spread_diag(1)
    spread_done(1)

    @pl.when(is_mid)
    def _():
        for c in range(chunks):
            o_pass(s3, c)

    spread_relay(2)

    @pl.when(is_end)
    def _():
        for c in range(chunks):
            o_wait(s2, c)

    add_shard(1, s2)
    spread_diag(2)
    spread_done(2)

    y_steps = width // y_cols

    def y_copy(i):
        slot = lax.rem(i, 2)
        r_at = pl.ds(pl.multiple_of((i // y_steps) * c_rows, c_rows), c_rows)
        n_at = pl.ds(pl.multiple_of(lax.rem(i, y_steps) * y_cols, y_cols), y_cols)
        return pltpu.make_async_copy(ytile.at[slot], y_ref.at[r_at, n_at], y_sem.at[slot])

    def last_step(i, _):
        c = i // y_steps

        @pl.when(is_end & (lax.rem(i, y_steps) == 0))
        def _():
            o_wait(s3, c)

        @pl.when(i >= 2)
        def _():
            y_copy(i - 2).wait()

        r_at = pl.ds(pl.multiple_of(c * c_rows, c_rows), c_rows)
        n_at = pl.ds(pl.multiple_of(lax.rem(i, y_steps) * y_cols, y_cols), y_cols)
        ytile[lax.rem(i, 2)] = (acc[r_at, n_at] + jnp.dot(obuf[slot_of(s3, z), r_at, :], wbuf[2, :, n_at], preferred_element_type=F32)).astype(BF16)
        y_copy(i).start()
        return 0

    total = chunks * y_steps
    lax.fori_loop(0, total, last_step, 0)
    y_copy(total - 2).wait()
    y_copy(total - 1).wait()

    for j in range(3):
        for kind in range(9):
            w_copy(j, kind).wait_send()
    for c in range(chunks):
        @pl.when(z > 0)
        def _(c=c):
            o_own(c, 0).wait_send()

        @pl.when(z < 3)
        def _(c=c):
            o_own(c, 1).wait_send()

    @pl.when(is_mid)
    def _():
        w3.wait_send()
        for c in range(chunks):
            for s in (s1, s2, s3):
                o_fwd(s, c, 0).wait_send()


def out_proj(o, slices, w_own, x):
    rows, kdim = o.shape
    width = x.shape[1]
    dma = pltpu.SemaphoreType.DMA
    return pl.pallas_call(
        out_kernel,
        in_specs=[pl.BlockSpec(memory_space=VMEM)] + [pl.BlockSpec(memory_space=HBM)] * 10,
        out_specs=pl.BlockSpec(memory_space=pl.ANY),
        out_shape=jax.ShapeDtypeStruct((rows, width), BF16),
        scratch_shapes=[
            VMEM((3, kdim, width), BF16),
            VMEM((2, kdim, 512), BF16),
            VMEM((2, rows, 512), BF16),
            VMEM((3, rows, kdim), BF16),
            VMEM((rows, width), F32),
            VMEM((2, rows // 4, 1024), BF16),
            dma((3, 2)), dma((2, 2)), dma((2,)), dma((3, 9)), dma((3, 9)), dma, dma,
            dma((2, 4)), dma((4, 4)), dma((4, 4)),
        ],
        compiler_params=pltpu.CompilerParams(collective_id=1, has_side_effects=True, vmem_limit_bytes=58 << 20),
        name="out_proj",
    )(o, *slices, w_own, x)


def solution(mesh):
    def local_step(x_in, doc_id, pos_in_doc, norm_gain, w_q, w_k, w_v, w_o, inv_freq):
        rows = x_in.shape[0]
        angle = pos_in_doc.astype(F32)[:, None] * inv_freq[None, :]
        q, kvg, fla, flb, fra, frb, fl2a, fr2a = project(x_in, norm_gain, w_k, w_v, w_q, w_o, jnp.cos(angle), jnp.sin(angle))
        fl2b = lax.ppermute(flb, "tp", [(1, 2), (2, 3)])
        fr2b = lax.ppermute(frb, "tp", [(1, 0), (2, 1)])
        o = attention(q, kvg, pos_in_doc)
        y = out_proj(o, (fla, flb, fra, frb, fl2a, fl2b, fr2a, fr2b), w_o, x_in)
        piece = rows // 2
        cp = lax.axis_index("cp")
        at = (cp * piece, (7 - cp) * piece)
        kv = jnp.concatenate([lax.dynamic_slice(kvg, (a, 0), (piece, kvg.shape[1])) for a in at])
        cols = w_k.shape[1]
        k_out = kv[:, :cols].reshape(rows, cols // HEAD, HEAD)
        v_out = kv[:, cols:].reshape(rows, cols // HEAD, HEAD)
        return y, k_out, v_out

    row_spec = P(("dp", "cp"))
    in_specs = (P(("dp", "cp"), None), row_spec, row_spec, P(), P(None, "tp"), P(None, "tp"), P(None, "tp"), P("tp", None), P())
    out_specs = (P(("dp", "cp"), None), P(("dp", "cp"), "tp", None), P(("dp", "cp"), "tp", None))
    return jax.shard_map(local_step, mesh=mesh, in_specs=in_specs, out_specs=out_specs, check_vma=False)
```

time: 270 us -> 250 us (0.926)
  waiting for transfers between devices: 17.7 us -> 0.01 us
  Pallas kernels: 208 us -> 222 us
  starting transfers between devices: 11.8 us -> 2.11 us
  local copies, waits for them, and re-layouts: 27.6 us -> 21.1 us
    ppermute x7 -> x2, waiting for transfers between devices: 17.7 us -> 0.01 us  [the longest x1 0.01 us: local_step(): fr2b = lax.ppermute(frb, 'tp', [(1, 0), (2, 1)])]
    pallas_call x4 -> x3, Pallas kernels: 208 us -> 222 us  [the longest x1 172 us: out_proj(): pl.pallas_call(out_kernel, in_specs=[pl.BlockSpec(memory_space=VMEM)] + [...]
    ppermute x7 -> x2, starting transfers between devices: 11.8 us -> 2.11 us  [the longest x1 1.29 us: local_step(): fr2b = lax.ppermute(frb, 'tp', [(1, 0), (2, 1)])]
    unnamed x15 -> x25, local copies, waits for them, and re-layouts: 19.9 us -> 17.7 us
  transfers between devices with their start and end apart: 7 -> 2, of which waited for: 3 -> 0; matrix products, arithmetic and copies ran while one was open for 3% -> 1% of each run, Pallas kernels for 9% -> 4%
where the time goes in v2:
time: 250 us; the launch traced here: 249 us
  Pallas kernels  222 us (89%)
  local copies, waits for them, and re-layouts  21.1 us (8%)
  other arithmetic  3.29 us (1%)
    pallas_call x1, Pallas kernels, out_proj(): pl.pallas_call(out_kernel, in_specs=[pl.BlockSpec(memory_space=VMEM)] + [...  172 us
    pallas_call x1, Pallas kernels, project(): pl.pallas_call(proj_kernel, in_specs=[hbm, vmem, hbm, hbm, hbm, hbm, vmem...  39.3 us
    unnamed x25, local copies, waits for them, and re-layouts  17.7 us
    pallas_call x1, Pallas kernels, attention(): pl.pallas_call(functools.partial(attn_kernel, group), grid_spec=pltpu.Pre...  10.6 us
  transfers between devices with their start and end apart: 2, of which 0 were waited for; matrix products, arithmetic and copies ran while one was open for 1% of the time, Pallas kernels for 4%

profile of v2, /device:TPU:0, one launch (start us, length us, event | category | flops | bytes accessed | tf_op | source)
XLA Modules:
  0.0 249.4 jit_solution(11231995538777648534)
XLA Ops:
  0.6 0.7 convert_element_type.3
  1.3 2.5 %multiply_sine_fusion = (f32[1024,64]{1,0:T(8,128)S(1)}, f32[1024,64]{1,0:T(8,128)S(1)}) fusion(f32[64]{0:T(128)} %param.16, f32[1024]{0:T(1024)S(1)} %convert_element_type.3), kind=kLoop, calls=%fused_computation.2 | loop fusion | flops 65536 | bytes 528640 | tf_op jit(solution)/shard_map/sin | solution.py:653
  3.9 0.0 copy-start.9
  3.9 0.7 copy-done.9
  4.6 39.3 %proj.1 = (bf16[1024,1024]{1,0:T(8,128)(2,1)}, bf16[4096,512]{1,0:T(8,128)(2,1)}, bf16[64,4096]{1,0:T(8,128)(2,1)S(1)}, bf16[64,4096]{1,0:T(8,128)(2,1)S(1)}, bf...) custom-call(bf16[1024,4096]{1,0:T(8,128)(2,1)} %x_ref.3, ...), custom_call_target="tpu_custom_call" | custom-call | flops 12884901888 | bytes 25165824 | tf_op jit(solution)/shard_map/proj/pallas_call | solution.py:246
  43.9 0.0 copy-start.1
  43.9 0.8 copy-done.1
  44.7 0.0 copy-start.3
  44.7 0.8 copy-done.3
  45.5 0.0 copy-start.5
  45.5 0.8 copy-done.5
  46.3 0.8 copy-done.6
  47.1 0.8 collective-permute-start
  47.9 1.3 collective-permute-start.1
  49.2 1.3 constant_dynamic-slice_fusion
  50.5 0.1 pad_maximum_fusion
  50.6 0.0 copy-done.8
  50.6 0.2 copy.11.pos_ref
  50.8 0.9 reshape.19
  51.8 0.9 reshape.18
  52.7 2.2 copy-done.7
  54.9 1.6 copy-done.10
  56.5 10.6 %attn.1.o_ref = bf16[1024,1024]{1,0:T(8,128)(2,1)S(1)} custom-call(s32[1024]{0:T(1024)S(1)} %copy-done.8, bf16[1024,1024]{1,0:T(8,128)(2,1)S(1)} %copy-done.10, s32[1024,1]{1,0:T(8,128)S(1)} %copy.11.pos_ref, bf16[4096,512]{1,0:T(8,128)(2,1)S(1)} %copy-done.7), custom_call_target="tpu_custom_call" | custom-call | flops 5368709120 | bytes 8388608 | tf_op jit(solution)/shard_map/attn/pallas_call | solution.py:326
  67.1 0.0 copy-done.2
  67.1 0.0 copy-done.4
  67.1 0.0 copy-start
  67.1 1.3 copy-done
  68.4 0.0 collective-permute-done.fl2b_ref
  68.4 0.0 collective-permute-done.1.fr2b_ref
  68.4 0.8 copy-done.11
  69.2 172.3 %out_proj.1 = bf16[1024,4096]{1,0:T(8,128)(2,1)} custom-call(bf16[1024,1024]{1,0:T(8,128)(2,1)} %copy-done, bf16[64,4096]{1,0:T(8,128)(2,1)} %copy-done.1, bf16[64,4096]{1,0:T(8,128)(2,1)} %copy-done.2, bf16[64,4096]{1,0:T(8,128)(2,1)} %copy-done.3, bf16[64,4096]{1,0:T(8,128)(2,1)} %copy-done.4, bf16[64,4096]{1,0:T(8,128)(2,1)} %copy-done.5, ...), custom_call_target="tpu_custom_call" | custom-call | tf_op jit(solution)/shard_map/out_proj/pallas_call | solution.py:629
  241.5 7.9 %copy.13 = bf16[1024,4096]{1,0:T(8,128)(2,1)} copy(bf16[1024,4096]{1,0:T(8,128)(2,1)} %out_proj.1) | data formatting | bytes 16777216
  (7 shorter events, 0.0 us)
Async XLA Ops:
  3.9 0.7 copy-start.9
  43.9 0.8 copy-start.1
  44.7 0.8 copy-start.3
  45.5 0.8 copy-start.5
  46.3 0.8 copy-start.6
  47.1 19.9 %copy-start.2 = (bf16[64,4096]{1,0:T(8,128)(2,1)}, bf16[64,4096]{1,0:T(8,128)(2,1)S(1)}, u32[]{:S(2)}) copy-start(bf16[64,4096]{1,0:T(8,128)(2,1)S(1)} %get-tuple-element.14.flb_ref) | copy-start | bytes 1572868
  47.1 20.0 %copy-start.4 = (bf16[64,4096]{1,0:T(8,128)(2,1)}, bf16[64,4096]{1,0:T(8,128)(2,1)S(1)}, u32[]{:S(2)}) copy-start(bf16[64,4096]{1,0:T(8,128)(2,1)S(1)} %get-tuple-element.16.frb_ref) | copy-start | bytes 1572868
  47.1 3.5 %copy-start.8 = (s32[1024]{0:T(1024)S(1)}, s32[1024]{0:T(1024)}, u32[]{:S(2)}) copy-start(s32[1024]{0:T(1024)} %pos_smem.1) | copy-start | bytes 12292
  47.1 21.3 %collective-permute-start = (bf16[64,4096]{1,0:T(8,128)(2,1)S(1)}, bf16[64,4096]{1,0:T(8,128)(2,1)S(1)}, u32[]{:S(2)}, u32[]{:S(2)}) collective-permute-start(bf16[64,4096]{1,0:T(8,128)(2,1)S(1)} %get-tuple-element.14.flb_ref), channel_id=1, source_target_pairs={{4,8},{8,12},{5,9},{9,13},{6,10},{10,14},{7,11},{11,15},{20,24},{2... | collective-permute-start | bytes 1572872 | tf_op jit(solution)/shard_map/ppermute | solution.py:654
  47.9 20.5 %collective-permute-start.1 = (bf16[64,4096]{1,0:T(8,128)(2,1)S(1)}, bf16[64,4096]{1,0:T(8,128)(2,1)}, u32[]{:S(2)}, u32[]{:S(2)}) collective-permute-start(bf16[64,4096]{1,0:T(8,128)(2,1)S(1)} %get-tuple-element.16.frb_ref), channel_id=1, source_target_pairs={{4,0},{8,4},{5,1},{9,5},{6,2},{10,6},{7,3},{11,7},{20,16},{24,20},... | collective-permute-start | bytes 1572872 | tf_op jit(solution)/shard_map/ppermute | solution.py:655
  52.7 2.2 copy-start.7
  54.9 1.6 copy-start.10
  67.1 1.3 copy-start
  68.4 0.8 copy-start.11

commit v3 on v2

--- a/solution.py
+++ b/solution.py
@@ -12,6 +12,7 @@
 VMEM = pltpu.VMEM
 HEAD = 128
 Q_TILE = 128
+VMEM_MAX = 67043328
 F32 = jnp.float32
 BF16 = jnp.bfloat16
 
@@ -21,10 +22,10 @@
     return (vec * cos_t + pltpu.roll(vec, HEAD // 2, 1) * sin_t).astype(BF16)
 
 
-def proj_kernel(x_ref, gain_ref, wk_ref, wv_ref, wq_ref, wo_ref, cos_ref, sin_ref,
-                q_ref, kvg_ref, fla_ref, flb_ref, fra_ref, frb_ref, fl2_ref, fr2_ref,
-                xbuf, hbuf, invbuf, wkbuf, wvbuf, wqbuf, kvbuf, qbuf,
-                x_sem, w_sem, wq_sem, kvl_sem, q_sem, kv_send, kv_recv, r1_send, r1_recv, r2_send, r2_recv):
+def proj_kernel(x_ref, gain_ref, wk_ref, wv_ref, wq_ref, wo_ref, pos_ref, freq_ref,
+                q_ref, kvg_ref, k_ref, v_ref, fla_ref, flb_ref, fra_ref, frb_ref, far_ref,
+                xbuf, hbuf, invbuf, gainbuf, posbuf, freqbuf, cosbuf, sinbuf, wkbuf, wvbuf, wqbuf, kvbuf, k3buf, v3buf, qbuf,
+                x_sem, w_sem, wq_sem, kvl_sem, kv3_sem, q_sem, kv_send, kv_recv, r1_send, r1_recv, r2_send, r2_recv):
     chunks, q_tiles = 4, 4
     rows, width = hbuf.shape
     c_rows = rows // chunks
@@ -64,6 +65,9 @@
 
     wk_load = pltpu.make_async_copy(wk_ref, wkbuf, w_sem.at[0])
     wv_load = pltpu.make_async_copy(wv_ref, wvbuf, w_sem.at[1])
+    small = [pltpu.make_async_copy(src, dst, w_sem.at[2 + i]) for i, (src, dst) in enumerate(((gain_ref, gainbuf), (pos_ref, posbuf), (freq_ref, freqbuf)))]
+    for cpy in small:
+        cpy.start()
     x_load(0).start()
     wk_load.start()
     wv_load.start()
@@ -89,8 +93,7 @@
 
     def r2(side):
         src = (fra_ref, fla_ref)[side]
-        dst = (fr2_ref, fl2_ref)[side]
-        return remote(src, dst, r2_send.at[side], r2_recv.at[side], (left, right)[side])
+        return remote(src, far_ref, r2_send.at[side], r2_recv, (left, right)[side])
 
     for part in range(2):
         @pl.when(z > 0)
@@ -121,14 +124,28 @@
         kv_copy(0, c).start()
         kv_copy(1, c).start()
 
+    def cache_out(c):
+        at = pl.ds(c * c_rows, c_rows)
+        return (pltpu.make_async_copy(k3buf.at[at], k_ref.at[at], kv3_sem.at[0, c]),
+                pltpu.make_async_copy(v3buf.at[at], v_ref.at[at], kv3_sem.at[1, c]))
+
     step = 16
 
-    def full(t):
-        return jnp.concatenate([t, t], axis=-1)
+    for cpy in small:
+        cpy.wait()
+
+    def angles(i, _):
+        at = pl.ds(pl.multiple_of(i * HEAD, HEAD), HEAD)
+        angle = posbuf[at, :].astype(F32) * freqbuf[...]
+        cos_h, sin_h = jnp.cos(angle), jnp.sin(angle)
+        cosbuf[at, :] = jnp.concatenate([cos_h, cos_h], axis=-1)
+        sinbuf[at, :] = jnp.concatenate([-sin_h, sin_h], axis=-1)
+        return 0
+
+    lax.fori_loop(0, rows // HEAD, angles, 0)
 
     def turn(vec, r_at):
-        cos_h, sin_h = cos_ref[r_at, :], sin_ref[r_at, :]
-        return rope(vec, full(cos_h), jnp.concatenate([-sin_h, sin_h], axis=-1))
+        return rope(vec, cosbuf[r_at, :], sinbuf[r_at, :])
 
     for c in range(chunks):
         x_load(c).wait()
@@ -144,7 +161,7 @@
             at = pl.ds(pl.multiple_of(i * step, step), step)
             to = pl.ds(pl.multiple_of(c * c_rows + i * step, step), step)
             inv = invbuf[at, 0:1]
-            hbuf[to, :] = (xbuf[c, at, :].astype(F32) * inv * gain_ref[...]).astype(BF16)
+            hbuf[to, :] = (xbuf[c, at, :].astype(F32) * inv * gainbuf[...]).astype(BF16)
             return 0
 
         lax.fori_loop(0, c_rows // step, square_rows, 0, unroll=4)
@@ -157,9 +174,15 @@
         k_new = jnp.dot(h, wkbuf[...], preferred_element_type=F32).astype(BF16)
         v_new = jnp.dot(h, wvbuf[...], preferred_element_type=F32).astype(BF16)
         for j in range(cols // HEAD):
-            kvbuf[r_at, j * HEAD:(j + 1) * HEAD] = turn(k_new[:, j * HEAD:(j + 1) * HEAD], r_at)
+            at = slice(j * HEAD, (j + 1) * HEAD)
+            k_head = turn(k_new[:, at], r_at)
+            kvbuf[r_at, at] = k_head
+            k3buf[r_at, j, :] = k_head
+            v3buf[r_at, j, :] = v_new[:, at]
         kvbuf[r_at, cols:] = v_new
         kv_local(c).start()
+        for cpy in cache_out(c):
+            cpy.start()
         if c > 0:
             kv_out(c - 1)
 
@@ -203,6 +226,9 @@
         kv_wait(2, c)
     for t in range(q_tiles):
         q_out(t).wait()
+    for c in range(chunks):
+        for cpy in cache_out(c):
+            cpy.wait()
 
     @pl.when(z > 0)
     def _():
@@ -216,13 +242,7 @@
         for part in range(2):
             r1(1, part).wait_send()
 
-    @pl.when(z > 1)
-    def _():
-        r2(1).wait_recv()
-
-    @pl.when(z < 2)
-    def _():
-        r2(0).wait_recv()
+    r2(0).wait_recv()
 
     @pl.when(is_mid)
     def _():
@@ -234,7 +254,7 @@
             kv_copy(kind, c).wait_send()
 
 
-def project(x, gain, w_k, w_v, w_q, w_o, cos_h, sin_h):
+def project(x, gain, w_k, w_v, w_q, w_o, pos, inv_freq):
     rows, width = x.shape
     cols = w_k.shape[1]
     q_cols = w_q.shape[1]
@@ -242,107 +262,149 @@
     dma = pltpu.SemaphoreType.DMA
     out = jax.ShapeDtypeStruct
     hbm = pl.BlockSpec(memory_space=HBM)
-    vmem = pl.BlockSpec(memory_space=VMEM)
     return pl.pallas_call(
         proj_kernel,
-        in_specs=[hbm, vmem, hbm, hbm, hbm, hbm, vmem, vmem],
-        out_specs=[hbm] * 8,
-        out_shape=[out((rows, q_cols), BF16), out((4 * rows, 2 * cols), BF16)] + [out((half, w_o.shape[1]), BF16)] * 6,
+        in_specs=[hbm] * 8,
+        out_specs=[hbm] * 9,
+        out_shape=[out((rows, q_cols), BF16), out((4 * rows, 2 * cols), BF16)] + [out((rows, cols // HEAD, HEAD), BF16)] * 2
+        + [out((half, w_o.shape[1]), BF16)] * 5,
         scratch_shapes=[
             VMEM((4, rows // 4, width), BF16),
             VMEM((rows, width), BF16),
             VMEM((rows // 4, HEAD), F32),
+            VMEM((1, width), F32),
+            VMEM((rows, 1), jnp.int32),
+            VMEM((1, HEAD // 2), F32),
+            VMEM((rows, HEAD), F32),
+            VMEM((rows, HEAD), F32),
             VMEM((width, cols), BF16),
             VMEM((width, cols), BF16),
             VMEM((4, width, q_cols // 4), BF16),
             VMEM((rows, 2 * cols), BF16),
+            VMEM((rows, cols // HEAD, HEAD), BF16),
+            VMEM((rows, cols // HEAD, HEAD), BF16),
             VMEM((4, rows, q_cols // 4), BF16),
-            dma((4,)), dma((2,)), dma((4,)), dma((4,)), dma((4,)),
-            dma((3, 4)), dma((3, 4)), dma((2, 2)), dma((2, 2)), dma((2,)), dma((2,)),
+            dma((4,)), dma((5,)), dma((4,)), dma((4,)), dma((2, 4)), dma((4,)),
+            dma((3, 4)), dma((3, 4)), dma((2, 2)), dma((2, 2)), dma((2,)), dma,
         ],
-        compiler_params=pltpu.CompilerParams(collective_id=0, has_side_effects=True, vmem_limit_bytes=48 << 20),
+        compiler_params=pltpu.CompilerParams(collective_id=0, has_side_effects=True, vmem_limit_bytes=VMEM_MAX),
         cost_estimate=pl.CostEstimate(flops=2 * rows * width * (2 * cols + q_cols), bytes_accessed=24 << 20, transcendentals=0),
         name="proj",
-    )(x, gain.reshape(1, width), w_k, w_v, w_q, w_o, cos_h, sin_h)
-
-
-def attn_kernel(group, pos_smem, q_ref, pos_ref, kv_ref, o_ref):
-    head, blk = pl.program_id(0), pl.program_id(1)
-    half_blks = pl.num_programs(1) // 2
+    )(x, gain.reshape(1, width), w_k, w_v, w_q, w_o, pos[:, None], inv_freq.reshape(1, HEAD // 2))
+
+
+def attn_kernel(pos_smem, q_ref, pos_ref, kv_ref, k_ref, v_ref, o_ref, k_out_ref, v_out_ref, kbuf, vbuf, in_sem, out_sem):
+    blk = pl.program_id(0)
+
+    cache = ((k_ref, kbuf, k_out_ref), (v_ref, vbuf, v_out_ref))
+    loads = [pltpu.make_async_copy(src, buf, in_sem.at[i]) for i, (src, buf, _) in enumerate(cache)]
+    stores = [pltpu.make_async_copy(buf, dst, out_sem.at[i]) for i, (_, buf, dst) in enumerate(cache)]
+
+    @pl.when(blk == 0)
+    def _():
+        for c in loads:
+            c.start()
+
+    @pl.when(blk == 2)
+    def _():
+        for c, d in zip(loads, stores):
+            c.wait()
+            d.start()
+
+    half_blks = pl.num_programs(0) // 2
     piece = half_blks * Q_TILE
     cp = lax.axis_index("cp")
     q_rows = q_ref.shape[0]
     kv_cols = kv_ref.shape[1] // 2
-    q = jnp.concatenate([q_ref[:, g * HEAD:(g + 1) * HEAD] for g in range(group)], axis=0)
+    heads = kv_cols // HEAD
+    group = q_ref.shape[1] // kv_cols
     pieces = kv_ref.shape[0] // piece
     g0 = jnp.where(blk < half_blks, cp * piece + blk * Q_TILE, (pieces - 1 - cp) * piece + (blk - half_blks) * Q_TILE)
     low = (g0 - pos_smem[blk * Q_TILE]) // Q_TILE
     tok_1 = g0 + lax.broadcasted_iota(jnp.int32, (q_rows, 1), 0)
     tok = jnp.concatenate([tok_1] * group, axis=0)
     first = jnp.concatenate([tok_1 - pos_ref[...]] * group, axis=0)
-    scale = HEAD ** -0.5
-    k_at = pl.ds(pl.multiple_of(head * HEAD, HEAD), HEAD)
-    v_at = pl.ds(pl.multiple_of(kv_cols + head * HEAD, HEAD), HEAD)
-
-    def scores(start, width):
-        keys = kv_ref[pl.ds(pl.multiple_of(start, Q_TILE), width), k_at]
-        s = lax.dot_general(q, keys, (((1,), (1,)), ((), ())), preferred_element_type=F32) * scale
+    factor = HEAD ** -0.5 * 1.4426950408889634
+
+    def head_q(n):
+        return jnp.concatenate([q_ref[:, (n * group + g) * HEAD:(n * group + g + 1) * HEAD] for g in range(group)], axis=0)
+
+    def scores(n, q, start, width):
+        keys = kv_ref[pl.ds(pl.multiple_of(start, Q_TILE), width), n * HEAD:(n + 1) * HEAD]
+        s = lax.dot_general(q, keys, (((1,), (1,)), ((), ())), preferred_element_type=F32)
         u = start + lax.broadcasted_iota(jnp.int32, (1, width), 1)
         return jnp.where((u >= first) & (u <= tok), s, -1e30)
 
-    def values(start, width):
-        return kv_ref[pl.ds(pl.multiple_of(start, Q_TILE), width), v_at]
+    def values(n, start, width):
+        return kv_ref[pl.ds(pl.multiple_of(start, Q_TILE), width), kv_cols + n * HEAD:kv_cols + (n + 1) * HEAD]
 
     near = jnp.maximum(g0 - Q_TILE, 0)
-    s = scores(near, 2 * Q_TILE)
-    m = jnp.max(s, axis=-1, keepdims=True)
-    p = jnp.exp(s - m)
-    total = jnp.sum(p, axis=-1, keepdims=True)
-    acc = jnp.dot(p.astype(BF16), values(near, 2 * Q_TILE), preferred_element_type=F32)
-
-    def far(i, carry):
+    states = []
+    for n in range(heads):
+        s = scores(n, head_q(n), near, 2 * Q_TILE)
+        m = jnp.max(s, axis=-1, keepdims=True)
+        p = jnp.exp2((s - m) * factor)
+        total = jnp.sum(p, axis=-1, keepdims=True)
+        acc = jnp.dot(p.astype(BF16), values(n, near, 2 * Q_TILE), preferred_element_type=F32)
+        states.append((m, total, acc))
+
+    def far(n, i, carry):
         m, total, acc = carry
         start = i * Q_TILE
-        s = scores(start, Q_TILE)
+        s = scores(n, head_q(n), start, Q_TILE)
         m_new = jnp.maximum(m, jnp.max(s, axis=-1, keepdims=True))
-        old = jnp.exp(m - m_new)
-        p = jnp.exp(s - m_new)
+        old = jnp.exp2((m - m_new) * factor)
+        p = jnp.exp2((s - m_new) * factor)
         total = total * old + jnp.sum(p, axis=-1, keepdims=True)
-        acc = acc * old + jnp.dot(p.astype(BF16), values(start, Q_TILE), preferred_element_type=F32)
+        acc = acc * old + jnp.dot(p.astype(BF16), values(n, start, Q_TILE), preferred_element_type=F32)
         return m_new, total, acc
 
-    m, total, acc = lax.fori_loop(low, near // Q_TILE, far, (m, total, acc))
-    out = (acc / total).astype(BF16)
-    for g in range(group):
-        o_ref[:, g * HEAD:(g + 1) * HEAD] = out[g * q_rows:(g + 1) * q_rows]
-
-
-def attention(q, kvg, pos):
+    def put(n, state):
+        out = (state[2] / state[1]).astype(BF16)
+        for g in range(group):
+            o_ref[:, (n * group + g) * HEAD:(n * group + g + 1) * HEAD] = out[g * q_rows:(g + 1) * q_rows]
+
+    for n in range(heads):
+        put(n, states[n])
+
+    @pl.when(low < near // Q_TILE)
+    def _():
+        for n in range(heads):
+            put(n, lax.fori_loop(low, near // Q_TILE, functools.partial(far, n), states[n]))
+
+    @pl.when(blk == pl.num_programs(0) - 1)
+    def _():
+        for d in stores:
+            d.wait()
+
+
+def attention(q, kvg, pos, k, v):
     rows, q_cols = q.shape
-    kv_cols = kvg.shape[1] // 2
-    heads = kv_cols // HEAD
-    group = q_cols // kv_cols
-    q_map = lambda h, i, *_: (i, h)
+    hbm = pl.BlockSpec(memory_space=HBM)
+    shape = jax.ShapeDtypeStruct
     return pl.pallas_call(
-        functools.partial(attn_kernel, group),
+        attn_kernel,
         grid_spec=pltpu.PrefetchScalarGridSpec(
             num_scalar_prefetch=1,
-            grid=(heads, rows // Q_TILE),
+            grid=(rows // Q_TILE,),
             in_specs=[
-                pl.BlockSpec((Q_TILE, group * HEAD), q_map),
-                pl.BlockSpec((Q_TILE, 1), lambda h, i, *_: (i, 0)),
-                pl.BlockSpec(kvg.shape, lambda h, i, *_: (0, 0)),
+                pl.BlockSpec((Q_TILE, q_cols), lambda i, *_: (i, 0)),
+                pl.BlockSpec((Q_TILE, 1), lambda i, *_: (i, 0)),
+                pl.BlockSpec(kvg.shape, lambda i, *_: (0, 0)),
+                hbm,
+                hbm,
             ],
-            out_specs=pl.BlockSpec((Q_TILE, group * HEAD), q_map),
+            out_specs=[pl.BlockSpec((Q_TILE, q_cols), lambda i, *_: (i, 0)), hbm, hbm],
+            scratch_shapes=[VMEM(k.shape, BF16), VMEM(v.shape, BF16), pltpu.SemaphoreType.DMA((2,)), pltpu.SemaphoreType.DMA((2,))],
         ),
-        out_shape=jax.ShapeDtypeStruct((rows, q_cols), BF16),
-        compiler_params=pltpu.CompilerParams(vmem_limit_bytes=32 << 20),
+        out_shape=[shape((rows, q_cols), BF16), shape(k.shape, BF16), shape(v.shape, BF16)],
+        compiler_params=pltpu.CompilerParams(vmem_limit_bytes=VMEM_MAX),
         cost_estimate=pl.CostEstimate(flops=5 << 30, bytes_accessed=8 << 20, transcendentals=0),
         name="attn",
-    )(pos, q, pos[:, None], kvg)
-
-
-def out_kernel(o_ref, fla_ref, flb_ref, fra_ref, frb_ref, fl2a_ref, fl2b_ref, fr2a_ref, fr2b_ref, wown_ref, x_ref, y_ref,
+    )(pos, q, pos[:, None], kvg, k, v)
+
+
+def out_kernel(o_ref, fla_ref, flb_ref, fra_ref, frb_ref, far_ref, fl2b_ref, fr2b_ref, third_ref, wown_ref, x_ref, y_ref,
                wbuf, wtile, xtile, obuf, acc, ytile,
                load_sem, tile_sem, y_sem, wsend, wrecv, w3_send, w3_recv, own_send, fwd_send, o_recv):
     rows, kdim = o_ref.shape
@@ -351,7 +413,7 @@
     slice_rows = 2 * half
     chunks = 4
     c_rows = rows // chunks
-    n_tile = 512
+    n_tile = xtile.shape[2]
     y_cols = ytile.shape[2]
     dp, z, cp = lax.axis_index("dp"), lax.axis_index("tp"), lax.axis_index("cp")
     is_end = (z == 0) | (z == 3)
@@ -393,15 +455,14 @@
     def load_w(src, j, part):
         return pltpu.make_async_copy(src, w_at(j, p_own, part * half, half), load_sem.at[j, part])
 
-    fl, fr, fl2, fr2 = (fla_ref, flb_ref), (fra_ref, frb_ref), (fl2a_ref, fl2b_ref), (fr2a_ref, fr2b_ref)
-    sources = ((fr, fr2, None), (fl, fr, fr2), (fr, fl, fl2), (fl, fl2, None))
+    fl, fr, fl2, fr2 = (fla_ref, flb_ref), (fra_ref, frb_ref), (far_ref, fl2b_ref), (far_ref, fr2b_ref)
+    sources = ((fr, fr2, (third_ref,)), (fl, fr, fr2), (fr, fl, fl2), (fl, fl2, (third_ref,)))
     for zz in range(4):
         @pl.when(z == zz)
         def _(zz=zz):
             for j in range(3):
-                if sources[zz][j] is not None:
-                    for part in range(2):
-                        load_w(sources[zz][j][part], j, part).start()
+                for part, src in enumerate(sources[zz][j]):
+                    load_w(src, j, part).start()
 
     @pl.when(is_end)
     def _():
@@ -474,12 +535,12 @@
         def _():
             o_fwd(s, c, 0).start()
 
-    w3 = remote(w_at(2, p_own), w_at(2, p_own), w3_send, w3_recv, {"tp": jnp.where(z == 1, 0, 3)})
+    w3_at = w_at(2, p_own, half, half)
+    w3 = remote(w3_at, w3_at, w3_send, w3_recv, {"tp": jnp.where(z == 1, 0, 3)})
 
     @pl.when(is_mid)
     def _():
-        for part in range(2):
-            load_w(fla_ref, 2, part).wait()
+        load_w(fla_ref, 2, 1).wait()
         w3.start()
 
     for c in range(chunks):
@@ -522,20 +583,23 @@
     lax.fori_loop(0, n_steps, own_step, 0)
 
     def add_shard(j, s):
+        wide = 512
+
         def step(n, _):
-            at = pl.ds(pl.multiple_of(n * n_tile, n_tile), n_tile)
+            at = pl.ds(pl.multiple_of(n * wide, wide), wide)
             acc[:, at] += jnp.dot(obuf[slot_of(s, z)], wbuf[j, :, at], preferred_element_type=F32)
             return 0
 
-        lax.fori_loop(0, n_steps, step, 0)
+        lax.fori_loop(0, width // wide, step, 0)
 
     spread_relay(0)
     spread_relay(1)
 
     @pl.when(is_end)
     def _():
-        remote(w_at(2, p_own), w_at(2, p_own), w3_send, w3_recv, left).wait_recv()
-
+        remote(w3_at, w3_at, w3_send, w3_recv, left).wait_recv()
+
+    load_w(fla_ref, 2, 0).wait()
     spread_own(2)
 
     @pl.when(is_mid)
@@ -628,40 +692,65 @@
     dma = pltpu.SemaphoreType.DMA
     return pl.pallas_call(
         out_kernel,
-        in_specs=[pl.BlockSpec(memory_space=VMEM)] + [pl.BlockSpec(memory_space=HBM)] * 10,
+        in_specs=[pl.BlockSpec(memory_space=VMEM)] + [pl.BlockSpec(memory_space=HBM)] * 5 + [pl.BlockSpec(memory_space=pl.ANY)] * 3 + [pl.BlockSpec(memory_space=HBM)] * 2,
         out_specs=pl.BlockSpec(memory_space=pl.ANY),
         out_shape=jax.ShapeDtypeStruct((rows, width), BF16),
         scratch_shapes=[
             VMEM((3, kdim, width), BF16),
-            VMEM((2, kdim, 512), BF16),
-            VMEM((2, rows, 512), BF16),
+            VMEM((2, kdim, 256), BF16),
+            VMEM((2, rows, 256), BF16),
             VMEM((3, rows, kdim), BF16),
             VMEM((rows, width), F32),
             VMEM((2, rows // 4, 1024), BF16),
             dma((3, 2)), dma((2, 2)), dma((2,)), dma((3, 9)), dma((3, 9)), dma, dma,
             dma((2, 4)), dma((4, 4)), dma((4, 4)),
         ],
-        compiler_params=pltpu.CompilerParams(collective_id=1, has_side_effects=True, vmem_limit_bytes=58 << 20),
+        compiler_params=pltpu.CompilerParams(collective_id=1, has_side_effects=True, vmem_limit_bytes=VMEM_MAX),
         name="out_proj",
     )(o, *slices, w_own, x)
+
+
+def settle_kernel(src_ref, dst_ref, buf, in_sem, out_sem):
+    parts, rows = buf.shape[0], buf.shape[1]
+
+    def load(i):
+        return pltpu.make_async_copy(src_ref.at[pl.ds(i * rows, rows)], buf.at[i], in_sem.at[i])
+
+    def store(i):
+        return pltpu.make_async_copy(buf.at[i], dst_ref.at[pl.ds(i * rows, rows)], out_sem.at[i])
+
+    for i in range(parts):
+        load(i).start()
+    for i in range(parts):
+        load(i).wait()
+        store(i).start()
+    for i in range(parts):
+        store(i).wait()
+
+
+def settle(y):
+    parts = 16
+    rows, width = y.shape
+    dma = pltpu.SemaphoreType.DMA
+    return pl.pallas_call(
+        settle_kernel,
+        in_specs=[pl.BlockSpec(memory_space=HBM)],
+        out_specs=pl.BlockSpec(memory_space=HBM),
+        out_shape=jax.ShapeDtypeStruct(y.shape, y.dtype),
+        scratch_shapes=[VMEM((parts, rows // parts, width), y.dtype), dma((parts,)), dma((parts,))],
+        name="settle",
+    )(y)
 
 
 def solution(mesh):
     def local_step(x_in, doc_id, pos_in_doc, norm_gain, w_q, w_k, w_v, w_o, inv_freq):
         rows = x_in.shape[0]
-        angle = pos_in_doc.astype(F32)[:, None] * inv_freq[None, :]
-        q, kvg, fla, flb, fra, frb, fl2a, fr2a = project(x_in, norm_gain, w_k, w_v, w_q, w_o, jnp.cos(angle), jnp.sin(angle))
+        q, kvg, k_new, v_new, fla, flb, fra, frb, far = project(x_in, norm_gain, w_k, w_v, w_q, w_o, pos_in_doc, inv_freq)
         fl2b = lax.ppermute(flb, "tp", [(1, 2), (2, 3)])
         fr2b = lax.ppermute(frb, "tp", [(1, 0), (2, 1)])
-        o = attention(q, kvg, pos_in_doc)
-        y = out_proj(o, (fla, flb, fra, frb, fl2a, fl2b, fr2a, fr2b), w_o, x_in)
-        piece = rows // 2
-        cp = lax.axis_index("cp")
-        at = (cp * piece, (7 - cp) * piece)
-        kv = jnp.concatenate([lax.dynamic_slice(kvg, (a, 0), (piece, kvg.shape[1])) for a in at])
-        cols = w_k.shape[1]
-        k_out = kv[:, :cols].reshape(rows, cols // HEAD, HEAD)
-        v_out = kv[:, cols:].reshape(rows, cols // HEAD, HEAD)
+        third = lax.ppermute(far, "tp", [(1, 0), (2, 3)])
+        o, k_out, v_out = attention(q, kvg, pos_in_doc, k_new, v_new)
+        y = settle(out_proj(o, (fla, flb, fra, frb, far, fl2b, fr2b, third), w_o, x_in))
         return y, k_out, v_out
 
     row_spec = P(("dp", "cp"))

time: 250 us -> 237 us (0.948)
  local copies, waits for them, and re-layouts: 21.1 us -> 1.73 us
  waiting for transfers between devices: 0.01 us -> 16.7 us
  Pallas kernels: 222 us -> 213 us
  other arithmetic: 3.29 us -> 0 us
    unnamed x25 -> x0, local copies, waits for them, and re-layouts: 17.7 us -> none
    pallas_call x1, Pallas kernels: 172 us -> 155 us  [out_proj(): pl.pallas_call(out_kernel, in_specs=[pl.BlockSpec(memory_space=VMEM)] + [...]
    ppermute x0 -> x1, waiting for transfers between devices: none -> 10.6 us  [local_step(): third = lax.ppermute(far, 'tp', [(1, 0), (2, 3)])]
    pallas_call x2 -> x3, Pallas kernels: 49.9 us -> 58.4 us  [the longest x1 41.5 us: project(): pl.pallas_call(proj_kernel, in_specs=[hbm] * 8, out_specs=[hbm] * 9, out_...]
    ppermute x1, waiting for transfers between devices: 0.01 us -> 6.08 us  [local_step(): fr2b = lax.ppermute(frb, 'tp', [(1, 0), (2, 1)])]
    sin x1 -> x0, other arithmetic: 2.53 us -> none  [local_step(): jnp.sin(angle)]
  transfers between devices with their start and end apart: 2 -> 3, of which waited for: 0 -> 2; matrix products, arithmetic and copies ran while one was open for 1% -> 0% of each run, Pallas kernels for 4% -> 4%
where the time goes in v3:
time: 237 us
  Pallas kernels  213 us (90%)
  waiting for transfers between devices  16.7 us (7%)
  starting transfers between devices  4.05 us (2%)
    pallas_call x1, Pallas kernels, out_proj(): pl.pallas_call(out_kernel, in_specs=[pl.BlockSpec(memory_space=VMEM)] + [...  155 us
    pallas_call x1, Pallas kernels, project(): pl.pallas_call(proj_kernel, in_specs=[hbm] * 8, out_specs=[hbm] * 9, out_...  41.5 us
    ppermute x1, waiting for transfers between devices, local_step(): third = lax.ppermute(far, 'tp', [(1, 0), (2, 3)])  10.6 us
    pallas_call x1, Pallas kernels, attention(): pl.pallas_call(attn_kernel, grid_spec=pltpu.PrefetchScalarGridSpec(num_sc...  10.4 us
    pallas_call x1, Pallas kernels, settle(): pl.pallas_call(settle_kernel, in_specs=[pl.BlockSpec(memory_space=HBM)],...  6.57 us
    ppermute x1, waiting for transfers between devices, local_step(): fr2b = lax.ppermute(frb, 'tp', [(1, 0), (2, 1)])  6.08 us
  transfers between devices with their start and end apart: 3, of which 2 were waited for; matrix products, arithmetic and copies ran while one was open for 0% of the time, Pallas kernels for 4%

profile of v3, /device:TPU:0, one launch (start us, length us, event | category | flops | bytes accessed | tf_op | source)
XLA Modules:
  0.0 236.6 jit_solution(11227919623655257345)
XLA Ops:
  0.6 1.7 copy.11.pos_ref
  2.4 41.5 %proj.1 = (bf16[1024,1024]{1,0:T(8,128)(2,1)}, bf16[4096,512]{1,0:T(8,128)(2,1)}, bf16[1024,2,128]{2,1,0:T(2,128)(2,1)}, bf16[1024,2,128]{2,1,0:T(2,128)(2,1)}, ...) custom-call(bf16[1024,4096]{1,0:T(8,128)(2,1)} %x_ref.3, ...), custom_call_target="tpu_custom_call" | custom-call | flops 12884901888 | bytes 25165824 | tf_op jit(solution)/shard_map/proj/pallas_call | solution.py:265
  43.9 1.5 collective-permute-start
  45.3 1.3 collective-permute-start.1
  46.6 1.3 collective-permute-start.2
  47.9 10.4 %attn.1 = (bf16[1024,1024]{1,0:T(8,128)(2,1)}, bf16[1024,2,128]{2,1,0:T(2,128)(2,1)}, bf16[1024,2,128]{2,1,0:T(2,128)(2,1)}) custom-call(s32[1024]{0:T(1024)} %pos_smem.1, bf16[1024,1024]{1,0:T(8,128)(2,1)} %get-tuple-element.15.q_ref, s32[1024,1]{1,0:T(8,128)} %copy.11.pos_ref, bf16[4096,512]{1,0:T(8,128)(2,1)} %get-tuple-element.16.kv_ref, ...), custom_call_target="tpu_custom_call" | custom-call | flops 5368709120 | bytes 8388608 | tf_op jit(solution)/shard_map/attn/pallas_call | solution.py:385
  58.3 0.0 collective-permute-done.fl2b_ref
  58.3 6.1 %collective-permute-done.1.fr2b_ref = bf16[64,4096]{1,0:T(8,128)(2,1)} collective-permute-done((bf16[64,4096]{1,0:T(8,128)(2,1)}, bf16[64,4096]{1,0:T(8,128)(2,1)}, u32[]{:S(2)}, u32[]{:S(2)}) %collective-permute-start.1) | collective-permute-done | bytes 524320 | tf_op jit(solution)/shard_map/ppermute | solution.py:750
  64.4 10.6 %collective-permute-done.2.third_ref = bf16[64,4096]{1,0:T(8,128)(2,1)} collective-permute-done((bf16[64,4096]{1,0:T(8,128)(2,1)}, bf16[64,4096]{1,0:T(8,128)(2,1)}, u32[]{:S(2)}, u32[]{:S(2)}) %collective-permute-start.2) | collective-permute-done | bytes 524320 | tf_op jit(solution)/shard_map/ppermute | solution.py:751
  75.0 154.8 %out_proj.1.src_ref = bf16[1024,4096]{1,0:T(8,128)(2,1)} custom-call(bf16[1024,1024]{1,0:T(8,128)(2,1)} %get-tuple-element.19.o_ref, bf16[64,4096]{1,0:T(8,128)(2,1)} %get-tuple-element.20.fla_ref, bf16[64,4096]{1,0:T(8,128)(2,1)} %get-tuple-element.21.flb_ref, bf16[64,4096]{1,0:T(8,128)(2,1)} %get-tuple-element.22.fra_ref, ...), custom_call_target="tpu_custom_call" | custom-call | tf_op jit(solution)/shard_map/out_proj/pallas_call | solution.py:693
  229.9 6.6 %settle.1 = bf16[1024,4096]{1,0:T(8,128)(2,1)} custom-call(bf16[1024,4096]{1,0:T(8,128)(2,1)} %out_proj.1.src_ref), custom_call_target="tpu_custom_call" | custom-call | tf_op jit(solution)/shard_map/settle/pallas_call | solution.py:735
Async XLA Ops:
  43.9 14.4 %collective-permute-start = (bf16[64,4096]{1,0:T(8,128)(2,1)}, bf16[64,4096]{1,0:T(8,128)(2,1)}, u32[]{:S(2)}, u32[]{:S(2)}) collective-permute-start(bf16[64,4096]{1,0:T(8,128)(2,1)} %get-tuple-element.21.flb_ref), channel_id=1, source_target_pairs={{4,8},{8,12},{5,9},{9,13},{6,10},{10,14},{7,11},{11,15},{20,24},{2... | collective-permute-start | bytes 1572872 | tf_op jit(solution)/shard_map/ppermute | solution.py:749
  45.3 19.1 %collective-permute-start.1 = (bf16[64,4096]{1,0:T(8,128)(2,1)}, bf16[64,4096]{1,0:T(8,128)(2,1)}, u32[]{:S(2)}, u32[]{:S(2)}) collective-permute-start(bf16[64,4096]{1,0:T(8,128)(2,1)} %get-tuple-element.23.frb_ref), channel_id=1, source_target_pairs={{4,0},{8,4},{5,1},{9,5},{6,2},{10,6},{7,3},{11,7},{20,16},{24,20},... | collective-permute-start | bytes 1572872 | tf_op jit(solution)/shard_map/ppermute | solution.py:750
  46.6 28.4 %collective-permute-start.2 = (bf16[64,4096]{1,0:T(8,128)(2,1)}, bf16[64,4096]{1,0:T(8,128)(2,1)}, u32[]{:S(2)}, u32[]{:S(2)}) collective-permute-start(bf16[64,4096]{1,0:T(8,128)(2,1)} %get-tuple-element.24.far_ref), channel_id=1, source_target_pairs={{4,0},{8,12},{5,1},{9,13},{6,2},{10,14},{7,3},{11,15},{20,16},{24,... | collective-permute-start | bytes 1572872 | tf_op jit(solution)/shard_map/ppermute | solution.py:751

commit v4 on v3

--- a/solution.py
+++ b/solution.py
@@ -17,13 +17,17 @@
 BF16 = jnp.bfloat16
 
 
+def in_vmem(arr):
+    return pltpu.with_memory_space_constraint(arr, VMEM)
+
+
 def rope(vec, cos_t, sin_t):
     vec = vec.astype(F32)
     return (vec * cos_t + pltpu.roll(vec, HEAD // 2, 1) * sin_t).astype(BF16)
 
 
 def proj_kernel(x_ref, gain_ref, wk_ref, wv_ref, wq_ref, wo_ref, pos_ref, freq_ref,
-                q_ref, kvg_ref, k_ref, v_ref, fla_ref, flb_ref, fra_ref, frb_ref, far_ref,
+                q_ref, kvg_ref, k_ref, v_ref, fl_ref, fr_ref, fara_ref, farb_ref,
                 xbuf, hbuf, invbuf, gainbuf, posbuf, freqbuf, cosbuf, sinbuf, wkbuf, wvbuf, wqbuf, kvbuf, k3buf, v3buf, qbuf,
                 x_sem, w_sem, wq_sem, kvl_sem, kv3_sem, q_sem, kv_send, kv_recv, r1_send, r1_recv, r2_send, r2_recv):
     chunks, q_tiles = 4, 4
@@ -32,7 +36,7 @@
     piece = rows // 2
     cols = wkbuf.shape[1]
     q_cols = wqbuf.shape[2]
-    half = fla_ref.shape[0]
+    half = fl_ref.shape[0] // 2
     n_cp = 4
     dp, z, cp = lax.axis_index("dp"), lax.axis_index("tp"), lax.axis_index("cp")
     core_cp = cp + 1 - 2 * lax.rem(cp, 2)
@@ -86,14 +90,31 @@
 
     p_own = dp * 4 + cp
 
+    def part_of(ref, part):
+        return ref.at[pl.ds(part * half, half)]
+
     def r1(side, part):
         src = wo_ref.at[pl.ds(pl.multiple_of((p_own * 2 + part) * half, half), half)]
-        dst = ((fra_ref, frb_ref), (fla_ref, flb_ref))[side][part]
+        dst = part_of((fr_ref, fl_ref)[side], part)
         return remote(src, dst, r1_send.at[side, part], r1_recv.at[side, part], (left, right)[side])
 
-    def r2(side):
-        src = (fra_ref, fla_ref)[side]
-        return remote(src, far_ref, r2_send.at[side], r2_recv, (left, right)[side])
+    def r2(side, part):
+        src = part_of((fr_ref, fl_ref)[side], part)
+        return remote(src, (fara_ref, farb_ref)[part], r2_send.at[side, part], r2_recv.at[part], (left, right)[side])
+
+    def second_hop(part):
+        @pl.when(z > 0)
+        def _():
+            r1(1, part).wait_recv()
+
+        @pl.when(z < 3)
+        def _():
+            r1(0, part).wait_recv()
+
+        @pl.when(is_mid)
+        def _():
+            r2(0, part).start()
+            r2(1, part).start()
 
     for part in range(2):
         @pl.when(z > 0)
@@ -134,15 +155,12 @@
     for cpy in small:
         cpy.wait()
 
-    def angles(i, _):
-        at = pl.ds(pl.multiple_of(i * HEAD, HEAD), HEAD)
-        angle = posbuf[at, :].astype(F32) * freqbuf[...]
+    pos_cols = jnp.transpose(posbuf[...].astype(F32))
+    for i in range(rows // HEAD):
+        angle = pos_cols[:, i:i + 1] * freqbuf[...]
         cos_h, sin_h = jnp.cos(angle), jnp.sin(angle)
-        cosbuf[at, :] = jnp.concatenate([cos_h, cos_h], axis=-1)
-        sinbuf[at, :] = jnp.concatenate([-sin_h, sin_h], axis=-1)
-        return 0
-
-    lax.fori_loop(0, rows // HEAD, angles, 0)
+        cosbuf[i * HEAD:(i + 1) * HEAD, :] = jnp.concatenate([cos_h, cos_h], axis=-1)
+        sinbuf[i * HEAD:(i + 1) * HEAD, :] = jnp.concatenate([-sin_h, sin_h], axis=-1)
 
     def turn(vec, r_at):
         return rope(vec, cosbuf[r_at, :], sinbuf[r_at, :])
@@ -186,18 +204,7 @@
         if c > 0:
             kv_out(c - 1)
 
-    @pl.when(z > 0)
-    def _():
-        r1(1, 0).wait_recv()
-
-    @pl.when(z < 3)
-    def _():
-        r1(0, 0).wait_recv()
-
-    @pl.when(is_mid)
-    def _():
-        r2(0).start()
-        r2(1).start()
+    second_hop(0)
 
     def q_out(t):
         return pltpu.make_async_copy(qbuf.at[t], q_ref.at[:, pl.ds(t * q_cols, q_cols)], q_sem.at[t])
@@ -217,6 +224,7 @@
         kv_wait(0, c)
         kv_copy(2, c).start()
     q_tile(2)
+    second_hop(1)
     q_tile(3)
     for c in range(2, chunks):
         kv_wait(0, c)
@@ -230,24 +238,21 @@
         for cpy in cache_out(c):
             cpy.wait()
 
-    @pl.when(z > 0)
-    def _():
-        r1(1, 1).wait_recv()
-        for part in range(2):
+    for part in range(2):
+        @pl.when(z > 0)
+        def _(part=part):
             r1(0, part).wait_send()
 
-    @pl.when(z < 3)
-    def _():
-        r1(0, 1).wait_recv()
-        for part in range(2):
+        @pl.when(z < 3)
+        def _(part=part):
             r1(1, part).wait_send()
 
-    r2(0).wait_recv()
-
-    @pl.when(is_mid)
-    def _():
-        r2(0).wait_send()
-        r2(1).wait_send()
+        r2(0, part).wait_recv()
+
+        @pl.when(is_mid)
+        def _(part=part):
+            r2(0, part).wait_send()
+            r2(1, part).wait_send()
 
     for c in range(chunks):
         for kind in range(3):
@@ -258,22 +263,21 @@
     rows, width = x.shape
     cols = w_k.shape[1]
     q_cols = w_q.shape[1]
-    half = w_o.shape[0] // 16
+    w_rows = w_o.shape[0] // 8
     dma = pltpu.SemaphoreType.DMA
-    out = jax.ShapeDtypeStruct
     hbm = pl.BlockSpec(memory_space=HBM)
     return pl.pallas_call(
         proj_kernel,
         in_specs=[hbm] * 8,
-        out_specs=[hbm] * 9,
-        out_shape=[out((rows, q_cols), BF16), out((4 * rows, 2 * cols), BF16)] + [out((rows, cols // HEAD, HEAD), BF16)] * 2
-        + [out((half, w_o.shape[1]), BF16)] * 5,
+        out_specs=[hbm] * 8,
+        out_shape=[HBM((rows, q_cols), BF16), HBM((4 * rows, 2 * cols), BF16)] + [HBM((rows, cols // HEAD, HEAD), BF16)] * 2
+        + [HBM((w_rows, w_o.shape[1]), BF16)] * 2 + [HBM((w_rows // 2, w_o.shape[1]), BF16)] * 2,
         scratch_shapes=[
             VMEM((4, rows // 4, width), BF16),
             VMEM((rows, width), BF16),
             VMEM((rows // 4, HEAD), F32),
             VMEM((1, width), F32),
-            VMEM((rows, 1), jnp.int32),
+            VMEM((rows // HEAD, HEAD), jnp.int32),
             VMEM((1, HEAD // 2), F32),
             VMEM((rows, HEAD), F32),
             VMEM((rows, HEAD), F32),
@@ -285,12 +289,12 @@
             VMEM((rows, cols // HEAD, HEAD), BF16),
             VMEM((4, rows, q_cols // 4), BF16),
             dma((4,)), dma((5,)), dma((4,)), dma((4,)), dma((2, 4)), dma((4,)),
-            dma((3, 4)), dma((3, 4)), dma((2, 2)), dma((2, 2)), dma((2,)), dma,
+            dma((3, 4)), dma((3, 4)), dma((2, 2)), dma((2, 2)), dma((2, 2)), dma((2,)),
         ],
         compiler_params=pltpu.CompilerParams(collective_id=0, has_side_effects=True, vmem_limit_bytes=VMEM_MAX),
         cost_estimate=pl.CostEstimate(flops=2 * rows * width * (2 * cols + q_cols), bytes_accessed=24 << 20, transcendentals=0),
         name="proj",
-    )(x, gain.reshape(1, width), w_k, w_v, w_q, w_o, pos[:, None], inv_freq.reshape(1, HEAD // 2))
+    )(x, gain.reshape(1, width), w_k, w_v, w_q, w_o, pos.reshape(rows // HEAD, HEAD), inv_freq.reshape(1, HEAD // 2))
 
 
 def attn_kernel(pos_smem, q_ref, pos_ref, kv_ref, k_ref, v_ref, o_ref, k_out_ref, v_out_ref, kbuf, vbuf, in_sem, out_sem):
@@ -314,7 +318,7 @@
     half_blks = pl.num_programs(0) // 2
     piece = half_blks * Q_TILE
     cp = lax.axis_index("cp")
-    q_rows = q_ref.shape[0]
+    q_rows = Q_TILE
     kv_cols = kv_ref.shape[1] // 2
     heads = kv_cols // HEAD
     group = q_ref.shape[1] // kv_cols
@@ -323,7 +327,10 @@
     low = (g0 - pos_smem[blk * Q_TILE]) // Q_TILE
     tok_1 = g0 + lax.broadcasted_iota(jnp.int32, (q_rows, 1), 0)
     tok = jnp.concatenate([tok_1] * group, axis=0)
-    first = jnp.concatenate([tok_1 - pos_ref[...]] * group, axis=0)
+    pos_cols = jnp.transpose(pos_ref[...].astype(F32))
+    mine = lax.broadcasted_iota(jnp.int32, pos_cols.shape, 1) == blk
+    pos_1 = jnp.sum(jnp.where(mine, pos_cols, 0.0), axis=1, keepdims=True).astype(jnp.int32)
+    first = jnp.concatenate([tok_1 - pos_1] * group, axis=0)
     factor = HEAD ** -0.5 * 1.4426950408889634
 
     def head_q(n):
@@ -380,41 +387,34 @@
 
 def attention(q, kvg, pos, k, v):
     rows, q_cols = q.shape
-    hbm = pl.BlockSpec(memory_space=HBM)
-    shape = jax.ShapeDtypeStruct
+    hbm, vmem = pl.BlockSpec(memory_space=HBM), pl.BlockSpec(memory_space=VMEM)
     return pl.pallas_call(
         attn_kernel,
         grid_spec=pltpu.PrefetchScalarGridSpec(
             num_scalar_prefetch=1,
             grid=(rows // Q_TILE,),
-            in_specs=[
-                pl.BlockSpec((Q_TILE, q_cols), lambda i, *_: (i, 0)),
-                pl.BlockSpec((Q_TILE, 1), lambda i, *_: (i, 0)),
-                pl.BlockSpec(kvg.shape, lambda i, *_: (0, 0)),
-                hbm,
-                hbm,
-            ],
+            in_specs=[pl.BlockSpec((Q_TILE, q_cols), lambda i, *_: (i, 0)), vmem, vmem, hbm, hbm],
             out_specs=[pl.BlockSpec((Q_TILE, q_cols), lambda i, *_: (i, 0)), hbm, hbm],
             scratch_shapes=[VMEM(k.shape, BF16), VMEM(v.shape, BF16), pltpu.SemaphoreType.DMA((2,)), pltpu.SemaphoreType.DMA((2,))],
         ),
-        out_shape=[shape((rows, q_cols), BF16), shape(k.shape, BF16), shape(v.shape, BF16)],
+        out_shape=[HBM((rows, q_cols), BF16), HBM(k.shape, BF16), HBM(v.shape, BF16)],
         compiler_params=pltpu.CompilerParams(vmem_limit_bytes=VMEM_MAX),
         cost_estimate=pl.CostEstimate(flops=5 << 30, bytes_accessed=8 << 20, transcendentals=0),
         name="attn",
-    )(pos, q, pos[:, None], kvg, k, v)
-
-
-def out_kernel(o_ref, fla_ref, flb_ref, fra_ref, frb_ref, far_ref, fl2b_ref, fr2b_ref, third_ref, wown_ref, x_ref, y_ref,
-               wbuf, wtile, xtile, obuf, acc, ytile,
-               load_sem, tile_sem, y_sem, wsend, wrecv, w3_send, w3_recv, own_send, fwd_send, o_recv):
+    )(pos, q, pos.reshape(rows // HEAD, HEAD), kvg, k, v)
+
+
+def out_kernel(o_ref, fl_ref, fr_ref, fara_ref, farb_ref, third_ref, wown_ref, x_ref, y_ref,
+               wbuf, wtile, xtile, obuf, own, acc,
+               load_sem, tile_sem, own_sem, wsend, wrecv, w3_send, w3_recv, own_send, fwd_send, o_recv):
     rows, kdim = o_ref.shape
     width = x_ref.shape[1]
-    half = fla_ref.shape[0]
-    slice_rows = 2 * half
+    slice_rows = fl_ref.shape[0]
+    half = slice_rows // 2
     chunks = 4
     c_rows = rows // chunks
     n_tile = xtile.shape[2]
-    y_cols = ytile.shape[2]
+    y_cols = 1024
     dp, z, cp = lax.axis_index("dp"), lax.axis_index("tp"), lax.axis_index("cp")
     is_end = (z == 0) | (z == 3)
     is_mid = (z == 1) | (z == 2)
@@ -448,6 +448,9 @@
     def _():
         pl.semaphore_signal(barrier, inc=1, device_id=right, device_id_type=MESH)
 
+    own_load = pltpu.make_async_copy(o_ref, own, own_sem)
+    own_load.start()
+
     def w_at(j, p, start=0, n=None):
         n = slice_rows if n is None else n
         return wbuf.at[j, pl.ds(pl.multiple_of(p * slice_rows + start, half), n)]
@@ -455,8 +458,11 @@
     def load_w(src, j, part):
         return pltpu.make_async_copy(src, w_at(j, p_own, part * half, half), load_sem.at[j, part])
 
-    fl, fr, fl2, fr2 = (fla_ref, flb_ref), (fra_ref, frb_ref), (far_ref, fl2b_ref), (far_ref, fr2b_ref)
-    sources = ((fr, fr2, (third_ref,)), (fl, fr, fr2), (fr, fl, fl2), (fl, fl2, (third_ref,)))
+    def parts_of(ref):
+        return ref.at[pl.ds(0, half)], ref.at[pl.ds(half, half)]
+
+    fl, fr, far, third = parts_of(fl_ref), parts_of(fr_ref), (fara_ref, farb_ref), (third_ref,)
+    sources = ((fr, far, third), (fl, fr, far), (fr, fl, far), (fl, far, third))
     for zz in range(4):
         @pl.when(z == zz)
         def _(zz=zz):
@@ -538,23 +544,28 @@
     w3_at = w_at(2, p_own, half, half)
     w3 = remote(w3_at, w3_at, w3_send, w3_recv, {"tp": jnp.where(z == 1, 0, 3)})
 
+    def send_own(c):
+        @pl.when(z > 0)
+        def _():
+            o_own(c, 0).start()
+
+        @pl.when(z < 3)
+        def _():
+            o_own(c, 1).start()
+
+    send_own(0)
+
     @pl.when(is_mid)
     def _():
-        load_w(fla_ref, 2, 1).wait()
+        load_w(third_ref, 2, 1).wait()
         w3.start()
 
-    for c in range(chunks):
-        @pl.when(z > 0)
-        def _(c=c):
-            o_own(c, 0).start()
-
-        @pl.when(z < 3)
-        def _(c=c):
-            o_own(c, 1).start()
+    for c in range(1, chunks):
+        send_own(c)
 
     for j in range(2):
         for part in range(2):
-            load_w(fla_ref, j, part).wait()
+            load_w(third_ref, j, part).wait()
         spread_own(j)
 
     def tile_loads(n, slot):
@@ -565,6 +576,7 @@
     n_steps = width // n_tile
     for cpy in tile_loads(0, 0):
         cpy.start()
+    own_load.wait()
 
     def own_step(n, _):
         slot = lax.rem(n, 2)
@@ -577,7 +589,7 @@
         for cpy in tile_loads(n, slot):
             cpy.wait()
         at = pl.ds(pl.multiple_of(n * n_tile, n_tile), n_tile)
-        acc[:, at] = xtile[slot].astype(F32) + jnp.dot(o_ref[...], wtile[slot], preferred_element_type=F32)
+        acc[:, at] = xtile[slot].astype(F32) + jnp.dot(own[...], wtile[slot], preferred_element_type=F32)
         return 0
 
     lax.fori_loop(0, n_steps, own_step, 0)
@@ -599,7 +611,7 @@
     def _():
         remote(w3_at, w3_at, w3_send, w3_recv, left).wait_recv()
 
-    load_w(fla_ref, 2, 0).wait()
+    load_w(third_ref, 2, 0).wait()
     spread_own(2)
 
     @pl.when(is_mid)
@@ -638,12 +650,6 @@
 
     y_steps = width // y_cols
 
-    def y_copy(i):
-        slot = lax.rem(i, 2)
-        r_at = pl.ds(pl.multiple_of((i // y_steps) * c_rows, c_rows), c_rows)
-        n_at = pl.ds(pl.multiple_of(lax.rem(i, y_steps) * y_cols, y_cols), y_cols)
-        return pltpu.make_async_copy(ytile.at[slot], y_ref.at[r_at, n_at], y_sem.at[slot])
-
     def last_step(i, _):
         c = i // y_steps
 
@@ -651,20 +657,12 @@
         def _():
             o_wait(s3, c)
 
-        @pl.when(i >= 2)
-        def _():
-            y_copy(i - 2).wait()
-
         r_at = pl.ds(pl.multiple_of(c * c_rows, c_rows), c_rows)
         n_at = pl.ds(pl.multiple_of(lax.rem(i, y_steps) * y_cols, y_cols), y_cols)
-        ytile[lax.rem(i, 2)] = (acc[r_at, n_at] + jnp.dot(obuf[slot_of(s3, z), r_at, :], wbuf[2, :, n_at], preferred_element_type=F32)).astype(BF16)
-        y_copy(i).start()
+        y_ref[r_at, n_at] = (acc[r_at, n_at] + jnp.dot(obuf[slot_of(s3, z), r_at, :], wbuf[2, :, n_at], preferred_element_type=F32)).astype(BF16)
         return 0
 
-    total = chunks * y_steps
-    lax.fori_loop(0, total, last_step, 0)
-    y_copy(total - 2).wait()
-    y_copy(total - 1).wait()
+    lax.fori_loop(0, chunks * y_steps, last_step, 0)
 
     for j in range(3):
         for kind in range(9):
@@ -692,52 +690,42 @@
     dma = pltpu.SemaphoreType.DMA
     return pl.pallas_call(
         out_kernel,
-        in_specs=[pl.BlockSpec(memory_space=VMEM)] + [pl.BlockSpec(memory_space=HBM)] * 5 + [pl.BlockSpec(memory_space=pl.ANY)] * 3 + [pl.BlockSpec(memory_space=HBM)] * 2,
-        out_specs=pl.BlockSpec(memory_space=pl.ANY),
-        out_shape=jax.ShapeDtypeStruct((rows, width), BF16),
+        in_specs=[pl.BlockSpec(memory_space=HBM)] * 8,
+        out_specs=pl.BlockSpec(memory_space=VMEM),
+        out_shape=VMEM((rows, width), BF16),
         scratch_shapes=[
             VMEM((3, kdim, width), BF16),
             VMEM((2, kdim, 256), BF16),
             VMEM((2, rows, 256), BF16),
             VMEM((3, rows, kdim), BF16),
+            VMEM((rows, kdim), BF16),
             VMEM((rows, width), F32),
-            VMEM((2, rows // 4, 1024), BF16),
-            dma((3, 2)), dma((2, 2)), dma((2,)), dma((3, 9)), dma((3, 9)), dma, dma,
+            dma((3, 2)), dma((2, 2)), dma, dma((3, 9)), dma((3, 9)), dma, dma,
             dma((2, 4)), dma((4, 4)), dma((4, 4)),
         ],
-        compiler_params=pltpu.CompilerParams(collective_id=1, has_side_effects=True, vmem_limit_bytes=VMEM_MAX),
+        compiler_params=pltpu.CompilerParams(collective_id=1, has_side_effects=True, vmem_limit_bytes=54 << 20),
         name="out_proj",
     )(o, *slices, w_own, x)
 
 
-def settle_kernel(src_ref, dst_ref, buf, in_sem, out_sem):
-    parts, rows = buf.shape[0], buf.shape[1]
-
-    def load(i):
-        return pltpu.make_async_copy(src_ref.at[pl.ds(i * rows, rows)], buf.at[i], in_sem.at[i])
-
-    def store(i):
-        return pltpu.make_async_copy(buf.at[i], dst_ref.at[pl.ds(i * rows, rows)], out_sem.at[i])
-
-    for i in range(parts):
-        load(i).start()
-    for i in range(parts):
-        load(i).wait()
-        store(i).start()
-    for i in range(parts):
-        store(i).wait()
+def settle_kernel(src_ref, dst_ref, sem):
+    parts = sem.shape[0]
+    rows = src_ref.shape[0] // parts
+    copies = [pltpu.make_async_copy(src_ref.at[pl.ds(i * rows, rows)], dst_ref.at[pl.ds(i * rows, rows)], sem.at[i]) for i in range(parts)]
+    for c in copies:
+        c.start()
+    for c in copies:
+        c.wait()
 
 
 def settle(y):
-    parts = 16
-    rows, width = y.shape
-    dma = pltpu.SemaphoreType.DMA
     return pl.pallas_call(
         settle_kernel,
-        in_specs=[pl.BlockSpec(memory_space=HBM)],
+        in_specs=[pl.BlockSpec(memory_space=VMEM)],
         out_specs=pl.BlockSpec(memory_space=HBM),
-        out_shape=jax.ShapeDtypeStruct(y.shape, y.dtype),
-        scratch_shapes=[VMEM((parts, rows // parts, width), y.dtype), dma((parts,)), dma((parts,))],
+        out_shape=HBM(y.shape, y.dtype),
+        scratch_shapes=[pltpu.SemaphoreType.DMA((8,))],
+        compiler_params=pltpu.CompilerParams(vmem_limit_bytes=16 << 20),
         name="settle",
     )(y)
 
@@ -745,12 +733,10 @@
 def solution(mesh):
     def local_step(x_in, doc_id, pos_in_doc, norm_gain, w_q, w_k, w_v, w_o, inv_freq):
         rows = x_in.shape[0]
-        q, kvg, k_new, v_new, fla, flb, fra, frb, far = project(x_in, norm_gain, w_k, w_v, w_q, w_o, pos_in_doc, inv_freq)
-        fl2b = lax.ppermute(flb, "tp", [(1, 2), (2, 3)])
-        fr2b = lax.ppermute(frb, "tp", [(1, 0), (2, 1)])
-        third = lax.ppermute(far, "tp", [(1, 0), (2, 3)])
+        q, kvg, k_new, v_new, fl, fr, fara, farb = project(x_in, norm_gain, w_k, w_v, w_q, w_o, pos_in_doc, inv_freq)
+        third = lax.ppermute(fara, "tp", [(1, 0), (2, 3)])
         o, k_out, v_out = attention(q, kvg, pos_in_doc, k_new, v_new)
-        y = settle(out_proj(o, (fla, flb, fra, frb, far, fl2b, fr2b, third), w_o, x_in))
+        y = settle(in_vmem(out_proj(o, (fl, fr, fara, farb, third), w_o, x_in)))
         return y, k_out, v_out
 
     row_spec = P(("dp", "cp"))

time: 237 us -> 222 us (0.937)
  waiting for transfers between devices: 16.7 us -> 2.89 us
  Pallas kernels: 213 us -> 217 us
  starting transfers between devices: 4.05 us -> 1.29 us
    ppermute x3 -> x1, waiting for transfers between devices: 16.7 us -> 2.89 us  [local_step(): third = lax.ppermute(fara, 'tp', [(1, 0), (2, 3)])]
    pallas_call x3, Pallas kernels: 203 us -> 206 us  [the longest x1 152 us: out_proj(): pl.pallas_call(out_kernel, in_specs=[pl.BlockSpec(memory_space=HBM)] * 8,...]
    ppermute x3 -> x1, starting transfers between devices: 4.05 us -> 1.29 us  [local_step(): third = lax.ppermute(fara, 'tp', [(1, 0), (2, 3)])]
  transfers between devices with their start and end apart: 3 -> 1, of which waited for: 2 -> 1; matrix products, arithmetic and copies ran while one was open for 0% -> 0% of each run, Pallas kernels for 4% -> 5%
where the time goes in v4:
time: 222 us
  Pallas kernels  217 us (98%)
  waiting for transfers between devices  2.89 us (1%)
    pallas_call x1, Pallas kernels, out_proj(): pl.pallas_call(out_kernel, in_specs=[pl.BlockSpec(memory_space=HBM)] * 8,...  152 us
    pallas_call x1, Pallas kernels, project(): pl.pallas_call(proj_kernel, in_specs=[hbm] * 8, out_specs=[hbm] * 8, out_...  50.7 us
    pallas_call x1, Pallas kernels, attention(): pl.pallas_call(attn_kernel, grid_spec=pltpu.PrefetchScalarGridSpec(num_sc...  10.8 us
  transfers between devices with their start and end apart: 1, of which 1 were waited for; matrix products, arithmetic and copies ran while one was open for 0% of the time, Pallas kernels for 5%

profile of v4, /device:TPU:0, one launch (start us, length us, event | category | flops | bytes accessed | tf_op | source)
XLA Modules:
  0.0 221.8 jit_solution(2788935411499508037)
XLA Ops:
  0.6 50.7 %proj.1 = (bf16[1024,1024]{1,0:T(8,128)(2,1)}, bf16[4096,512]{1,0:T(8,128)(2,1)}, bf16[1024,2,128]{2,1,0:T(2,128)(2,1)}, bf16[1024,2,128]{2,1,0:T(2,128)(2,1)}, ...) custom-call(bf16[1024,4096]{1,0:T(8,128)(2,1)} %x_ref.3, ...), custom_call_target="tpu_custom_call" | custom-call | flops 12884901888 | bytes 25165824 | tf_op jit(solution)/shard_map/proj/pallas_call | solution.py:269
  51.3 1.3 collective-permute-start
  52.6 10.8 %attn.1 = (bf16[1024,1024]{1,0:T(8,128)(2,1)}, bf16[1024,2,128]{2,1,0:T(2,128)(2,1)}, bf16[1024,2,128]{2,1,0:T(2,128)(2,1)}) custom-call(s32[1024]{0:T(1024)} %pos_smem.1, bf16[1024,1024]{1,0:T(8,128)(2,1)} %get-tuple-element.14.q_ref, s32[8,128]{1,0:T(8,128)} %bitcast.5, bf16[4096,512]{1,0:T(8,128)(2,1)} %get-tuple-element.15.kv_ref, ...), custom_call_target="tpu_custom_call" | custom-call | flops 5368709120 | bytes 8388608 | tf_op jit(solution)/shard_map/attn/pallas_call | solution.py:391
  63.5 2.9 %collective-permute-done.third_ref = bf16[64,4096]{1,0:T(8,128)(2,1)} collective-permute-done((bf16[64,4096]{1,0:T(8,128)(2,1)}, bf16[64,4096]{1,0:T(8,128)(2,1)}, u32[]{:S(2)}, u32[]{:S(2)}) %collective-permute-start) | collective-permute-done | bytes 524320 | tf_op jit(solution)/shard_map/ppermute | solution.py:737
  66.3 151.9 %out_proj.1.src_ref = bf16[1024,4096]{1,0:T(8,128)(2,1)S(1)} custom-call(bf16[1024,1024]{1,0:T(8,128)(2,1)} %get-tuple-element.18.o_ref, bf16[128,4096]{1,0:T(8,128)(2,1)} %get-tuple-element.19.fl_ref, bf16[128,4096]{1,0:T(8,128)(2,1)} %get-tuple-element.20.fr_ref, bf16[64,4096]{1,0:T(8,128)(2,1)} %get-tuple-element.21.fara_ref, ...), custom_call_target="tpu_custom_call" | custom-call | tf_op jit(solution)/shard_map/out_proj/pallas_call | solution.py:691
  218.3 3.4 %settle.1 = bf16[1024,4096]{1,0:T(8,128)(2,1)} custom-call(bf16[1024,4096]{1,0:T(8,128)(2,1)S(1)} %out_proj.1.src_ref), custom_call_target="tpu_custom_call" | custom-call | tf_op jit(solution)/shard_map/settle/pallas_call | solution.py:722
Async XLA Ops:
  51.3 15.0 %collective-permute-start = (bf16[64,4096]{1,0:T(8,128)(2,1)}, bf16[64,4096]{1,0:T(8,128)(2,1)}, u32[]{:S(2)}, u32[]{:S(2)}) collective-permute-start(bf16[64,4096]{1,0:T(8,128)(2,1)} %get-tuple-element.21.fara_ref), channel_id=1, source_target_pairs={{4,0},{8,12},{5,1},{9,13},{6,2},{10,14},{7,3},{11,15},{20,16},{24,... | collective-permute-start | bytes 1572872 | tf_op jit(solution)/shard_map/ppermute | solution.py:737

commit v5 on v4

--- a/solution.py
+++ b/solution.py
@@ -404,14 +404,14 @@
     )(pos, q, pos.reshape(rows // HEAD, HEAD), kvg, k, v)
 
 
-def out_kernel(o_ref, fl_ref, fr_ref, fara_ref, farb_ref, third_ref, wown_ref, x_ref, y_ref,
+def out_kernel(o_ref, fl_ref, fr_ref, fara_ref, farb_ref, third_ref, wown_ref, x_ref, y_ref, wlast, olast_ref, alast_ref,
                wbuf, wtile, xtile, obuf, own, acc,
                load_sem, tile_sem, own_sem, wsend, wrecv, w3_send, w3_recv, own_send, fwd_send, o_recv):
     rows, kdim = o_ref.shape
     width = x_ref.shape[1]
     slice_rows = fl_ref.shape[0]
     half = slice_rows // 2
-    chunks = 4
+    chunks = own_send.shape[1]
     c_rows = rows // chunks
     n_tile = xtile.shape[2]
     y_cols = 1024
@@ -453,7 +453,8 @@
 
     def w_at(j, p, start=0, n=None):
         n = slice_rows if n is None else n
-        return wbuf.at[j, pl.ds(pl.multiple_of(p * slice_rows + start, half), n)]
+        at = pl.ds(pl.multiple_of(p * slice_rows + start, half), n)
+        return wlast.at[at] if j == 2 else wbuf.at[j, at]
 
     def load_w(src, j, part):
         return pltpu.make_async_copy(src, w_at(j, p_own, part * half, half), load_sem.at[j, part])
@@ -659,10 +660,18 @@
 
         r_at = pl.ds(pl.multiple_of(c * c_rows, c_rows), c_rows)
         n_at = pl.ds(pl.multiple_of(lax.rem(i, y_steps) * y_cols, y_cols), y_cols)
-        y_ref[r_at, n_at] = (acc[r_at, n_at] + jnp.dot(obuf[slot_of(s3, z), r_at, :], wbuf[2, :, n_at], preferred_element_type=F32)).astype(BF16)
+        y_ref[r_at, n_at] = (acc[r_at, n_at] + jnp.dot(obuf[slot_of(s3, z), r_at, :], wlast[:, n_at], preferred_element_type=F32)).astype(BF16)
         return 0
 
-    lax.fori_loop(0, chunks * y_steps, last_step, 0)
+    rest = pl.ds((chunks - 1) * c_rows, c_rows)
+    alast_ref[...] = acc[rest, :]
+    lax.fori_loop(0, (chunks - 1) * y_steps, last_step, 0)
+
+    @pl.when(is_end)
+    def _():
+        o_wait(s3, chunks - 1)
+
+    olast_ref[...] = obuf[slot_of(s3, z), rest, :]
 
     for j in range(3):
         for kind in range(9):
@@ -686,48 +695,64 @@
 
 def out_proj(o, slices, w_own, x):
     rows, kdim = o.shape
+    chunks = 8
+    last = rows // chunks
     width = x.shape[1]
     dma = pltpu.SemaphoreType.DMA
     return pl.pallas_call(
         out_kernel,
         in_specs=[pl.BlockSpec(memory_space=HBM)] * 8,
-        out_specs=pl.BlockSpec(memory_space=VMEM),
-        out_shape=VMEM((rows, width), BF16),
+        out_specs=[pl.BlockSpec(memory_space=VMEM)] * 4,
+        out_shape=[
+            VMEM((rows - last, width), BF16),
+            VMEM((kdim, width), BF16),
+            VMEM((last, kdim), BF16),
+            VMEM((last, width), F32),
+        ],
         scratch_shapes=[
-            VMEM((3, kdim, width), BF16),
+            VMEM((2, kdim, width), BF16),
             VMEM((2, kdim, 256), BF16),
             VMEM((2, rows, 256), BF16),
             VMEM((3, rows, kdim), BF16),
             VMEM((rows, kdim), BF16),
             VMEM((rows, width), F32),
             dma((3, 2)), dma((2, 2)), dma, dma((3, 9)), dma((3, 9)), dma, dma,
-            dma((2, 4)), dma((4, 4)), dma((4, 4)),
+            dma((2, chunks)), dma((4, chunks)), dma((4, chunks)),
         ],
-        compiler_params=pltpu.CompilerParams(collective_id=1, has_side_effects=True, vmem_limit_bytes=54 << 20),
+        compiler_params=pltpu.CompilerParams(collective_id=1, has_side_effects=True, vmem_limit_bytes=45 << 20),
         name="out_proj",
     )(o, *slices, w_own, x)
 
 
-def settle_kernel(src_ref, dst_ref, sem):
-    parts = sem.shape[0]
+def settle_kernel(src_ref, w_ref, o_ref, acc_ref, y_ref, ytile, sem, last_sem):
+    parts, tiles = sem.shape[0], last_sem.shape[0]
     rows = src_ref.shape[0] // parts
-    copies = [pltpu.make_async_copy(src_ref.at[pl.ds(i * rows, rows)], dst_ref.at[pl.ds(i * rows, rows)], sem.at[i]) for i in range(parts)]
+    copies = [pltpu.make_async_copy(src_ref.at[pl.ds(i * rows, rows)], y_ref.at[pl.ds(i * rows, rows)], sem.at[i]) for i in range(parts)]
     for c in copies:
         c.start()
+    cols = w_ref.shape[1] // tiles
+    for t in range(tiles):
+        at = pl.ds(t * cols, cols)
+        ytile[:, at] = (acc_ref[:, at] + jnp.dot(o_ref[...], w_ref[:, at], preferred_element_type=F32)).astype(BF16)
+        copies.append(pltpu.make_async_copy(ytile.at[:, at], y_ref.at[pl.ds(src_ref.shape[0], ytile.shape[0]), at], last_sem.at[t]))
+        copies[-1].start()
     for c in copies:
         c.wait()
 
 
-def settle(y):
+def settle(y, w_last, o_last, acc_last):
+    rows, width = y.shape
+    last = o_last.shape[0]
+    dma = pltpu.SemaphoreType.DMA
     return pl.pallas_call(
         settle_kernel,
-        in_specs=[pl.BlockSpec(memory_space=VMEM)],
+        in_specs=[pl.BlockSpec(memory_space=VMEM)] * 4,
         out_specs=pl.BlockSpec(memory_space=HBM),
-        out_shape=HBM(y.shape, y.dtype),
-        scratch_shapes=[pltpu.SemaphoreType.DMA((8,))],
+        out_shape=HBM((rows + last, width), y.dtype),
+        scratch_shapes=[VMEM((last, width), BF16), dma((7,)), dma((4,))],
         compiler_params=pltpu.CompilerParams(vmem_limit_bytes=16 << 20),
         name="settle",
-    )(y)
+    )(in_vmem(y), in_vmem(w_last), in_vmem(o_last), in_vmem(acc_last))
 
 
 def solution(mesh):
@@ -736,7 +761,7 @@
         q, kvg, k_new, v_new, fl, fr, fara, farb = project(x_in, norm_gain, w_k, w_v, w_q, w_o, pos_in_doc, inv_freq)
         third = lax.ppermute(fara, "tp", [(1, 0), (2, 3)])
         o, k_out, v_out = attention(q, kvg, pos_in_doc, k_new, v_new)
-        y = settle(in_vmem(out_proj(o, (fl, fr, fara, farb, third), w_o, x_in)))
+        y = settle(*out_proj(o, (fl, fr, fara, farb, third), w_o, x_in))
         return y, k_out, v_out
 
     row_spec = P(("dp", "cp"))

time: 222 us -> 220 us (level)
  Pallas kernels: 217 us -> 214 us
    pallas_call x1, Pallas kernels: 152 us -> 149 us  [out_proj(): pl.pallas_call(out_kernel, in_specs=[pl.BlockSpec(memory_space=HBM)] * 8,...]
where the time goes in v5:
time: 220 us; the launch traced here: 219 us
  Pallas kernels  214 us (97%)
  waiting for transfers between devices  2.89 us (1%)
    pallas_call x1, Pallas kernels, out_proj(): pl.pallas_call(out_kernel, in_specs=[pl.BlockSpec(memory_space=HBM)] * 8,...  149 us
    pallas_call x1, Pallas kernels, project(): pl.pallas_call(proj_kernel, in_specs=[hbm] * 8, out_specs=[hbm] * 8, out_...  50.7 us
    pallas_call x1, Pallas kernels, attention(): pl.pallas_call(attn_kernel, grid_spec=pltpu.PrefetchScalarGridSpec(num_sc...  10.8 us
  transfers between devices with their start and end apart: 1, of which 1 were waited for; matrix products, arithmetic and copies ran while one was open for 0% of the time, Pallas kernels for 5%

profile of v5, /device:TPU:0, one launch (start us, length us, event | category | flops | bytes accessed | tf_op | source)
XLA Modules:
  0.0 219.4 jit_solution(3824933125550106469)
XLA Ops:
  0.6 50.7 %proj.1 = (bf16[1024,1024]{1,0:T(8,128)(2,1)}, bf16[4096,512]{1,0:T(8,128)(2,1)}, bf16[1024,2,128]{2,1,0:T(2,128)(2,1)}, bf16[1024,2,128]{2,1,0:T(2,128)(2,1)}, ...) custom-call(bf16[1024,4096]{1,0:T(8,128)(2,1)} %x_ref.3, ...), custom_call_target="tpu_custom_call" | custom-call | flops 12884901888 | bytes 25165824 | tf_op jit(solution)/shard_map/proj/pallas_call | solution.py:269
  51.3 1.3 collective-permute-start
  52.6 10.8 %attn.1 = (bf16[1024,1024]{1,0:T(8,128)(2,1)}, bf16[1024,2,128]{2,1,0:T(2,128)(2,1)}, bf16[1024,2,128]{2,1,0:T(2,128)(2,1)}) custom-call(s32[1024]{0:T(1024)} %pos_smem.1, bf16[1024,1024]{1,0:T(8,128)(2,1)} %get-tuple-element.18.q_ref, s32[8,128]{1,0:T(8,128)} %bitcast.5, bf16[4096,512]{1,0:T(8,128)(2,1)} %get-tuple-element.19.kv_ref, ...), custom_call_target="tpu_custom_call" | custom-call | flops 5368709120 | bytes 8388608 | tf_op jit(solution)/shard_map/attn/pallas_call | solution.py:391
  63.5 2.9 %collective-permute-done.third_ref = bf16[64,4096]{1,0:T(8,128)(2,1)} collective-permute-done((bf16[64,4096]{1,0:T(8,128)(2,1)}, bf16[64,4096]{1,0:T(8,128)(2,1)}, u32[]{:S(2)}, u32[]{:S(2)}) %collective-permute-start) | collective-permute-done | bytes 524320 | tf_op jit(solution)/shard_map/ppermute | solution.py:762
  66.3 149.4 %out_proj.1 = (bf16[896,4096]{1,0:T(8,128)(2,1)S(1)}, bf16[1024,4096]{1,0:T(8,128)(2,1)S(1)}, bf16[128,1024]{1,0:T(8,128)(2,1)S(1)}, f32[128,4096]{1,0:T(8,128)S(1)}) custom-call(bf16[1024,1024]{1,0:T(8,128)(2,1)} %get-tuple-element.22.o_ref, bf16[128,4096]{1,0:T(8,128)(2,1)} %get-tuple-element.23.fl_ref, bf16[128,4096]{1,0:T(8,128)(2,1)} %get-tuple-element.24.fr_ref, ...), custom_call_target="tpu_custom_call" | custom-call | tf_op jit(solution)/shard_map/out_proj/pallas_call | solution.py:702
  215.8 3.4 %settle.1 = bf16[1024,4096]{1,0:T(8,128)(2,1)} custom-call(bf16[896,4096]{1,0:T(8,128)(2,1)S(1)} %get-tuple-element.27.src_ref, bf16[1024,4096]{1,0:T(8,128)(2,1)S(1)} %get-tuple-element.28.w_ref, bf16[128,1024]{1,0:T(8,128)(2,1)S(1)} %get-tuple-element.29.o_ref, f32[128,4096]{1,0:T(8,128)S(1)} %get-tuple-element.30.acc_ref), custom_call_target="tpu_custom_call" | custom-call | tf_op jit(solution)/shard_map/settle/pallas_call | solution.py:747
Async XLA Ops:
  51.3 15.0 %collective-permute-start = (bf16[64,4096]{1,0:T(8,128)(2,1)}, bf16[64,4096]{1,0:T(8,128)(2,1)}, u32[]{:S(2)}, u32[]{:S(2)}) collective-permute-start(bf16[64,4096]{1,0:T(8,128)(2,1)} %get-tuple-element.25.fara_ref), channel_id=1, source_target_pairs={{4,0},{8,12},{5,1},{9,13},{6,2},{10,14},{7,3},{11,15},{20,16},{24,... | collective-permute-start | bytes 1572872 | tf_op jit(solution)/shard_map/ppermute | solution.py:762

commit v6 on v5

--- a/solution.py
+++ b/solution.py
@@ -346,38 +346,46 @@
         return kv_ref[pl.ds(pl.multiple_of(start, Q_TILE), width), kv_cols + n * HEAD:kv_cols + (n + 1) * HEAD]
 
     near = jnp.maximum(g0 - Q_TILE, 0)
+    wide = 2 * Q_TILE
+
+    def probs(s, m, inv):
+        return (jnp.exp2((s - m) * factor) * inv).astype(BF16)
+
+    def put(n, acc):
+        out = acc.astype(BF16)
+        for g in range(group):
+            o_ref[:, (n * group + g) * HEAD:(n * group + g + 1) * HEAD] = out[g * q_rows:(g + 1) * q_rows]
+
     states = []
     for n in range(heads):
-        s = scores(n, head_q(n), near, 2 * Q_TILE)
+        s = scores(n, head_q(n), near, wide)
         m = jnp.max(s, axis=-1, keepdims=True)
-        p = jnp.exp2((s - m) * factor)
-        total = jnp.sum(p, axis=-1, keepdims=True)
-        acc = jnp.dot(p.astype(BF16), values(n, near, 2 * Q_TILE), preferred_element_type=F32)
-        states.append((m, total, acc))
-
-    def far(n, i, carry):
-        m, total, acc = carry
-        start = i * Q_TILE
-        s = scores(n, head_q(n), start, Q_TILE)
-        m_new = jnp.maximum(m, jnp.max(s, axis=-1, keepdims=True))
-        old = jnp.exp2((m - m_new) * factor)
-        p = jnp.exp2((s - m_new) * factor)
-        total = total * old + jnp.sum(p, axis=-1, keepdims=True)
-        acc = acc * old + jnp.dot(p.astype(BF16), values(n, start, Q_TILE), preferred_element_type=F32)
-        return m_new, total, acc
-
-    def put(n, state):
-        out = (state[2] / state[1]).astype(BF16)
-        for g in range(group):
-            o_ref[:, (n * group + g) * HEAD:(n * group + g + 1) * HEAD] = out[g * q_rows:(g + 1) * q_rows]
-
-    for n in range(heads):
-        put(n, states[n])
+        e = jnp.exp2((s - m) * factor)
+        total = jnp.sum(e, axis=-1, keepdims=True)
+        p = (e * (1.0 / total)).astype(BF16)
+        put(n, jnp.dot(p, values(n, near, wide), preferred_element_type=F32))
+        states.append((m, total))
 
     @pl.when(low < near // Q_TILE)
     def _():
         for n in range(heads):
-            put(n, lax.fori_loop(low, near // Q_TILE, functools.partial(far, n), states[n]))
+            def far_sum(i, carry, n=n):
+                m, total = carry
+                s = scores(n, head_q(n), i * Q_TILE, Q_TILE)
+                m_new = jnp.maximum(m, jnp.max(s, axis=-1, keepdims=True))
+                part = jnp.sum(jnp.exp2((s - m_new) * factor), axis=-1, keepdims=True)
+                return m_new, total * jnp.exp2((m - m_new) * factor) + part
+
+            m, total = lax.fori_loop(low, near // Q_TILE, far_sum, states[n])
+            inv = 1.0 / total
+
+            def far_pv(i, acc, n=n, m=m, inv=inv):
+                p = probs(scores(n, head_q(n), i * Q_TILE, Q_TILE), m, inv)
+                return acc + jnp.dot(p, values(n, i * Q_TILE, Q_TILE), preferred_element_type=F32)
+
+            p = probs(scores(n, head_q(n), near, wide), m, inv)
+            acc = jnp.dot(p, values(n, near, wide), preferred_element_type=F32)
+            put(n, lax.fori_loop(low, near // Q_TILE, far_pv, acc))
 
     @pl.when(blk == pl.num_programs(0) - 1)
     def _():

time: 220 us -> 222 us (level)
  Pallas kernels: 214 us -> 217 us
  transfers between devices with their start and end apart: 1 -> 1, of which waited for: 1 -> 1; matrix products, arithmetic and copies ran while one was open for 0% -> 0% of each run, Pallas kernels for 5% -> 6%
where the time goes in v6:
time: 222 us; the launch traced here: 221 us
  Pallas kernels  217 us (98%)
    pallas_call x1, Pallas kernels, out_proj(): pl.pallas_call(out_kernel, in_specs=[pl.BlockSpec(memory_space=HBM)] * 8,...  151 us
    pallas_call x1, Pallas kernels, project(): pl.pallas_call(proj_kernel, in_specs=[hbm] * 8, out_specs=[hbm] * 8, out_...  50.7 us
    pallas_call x1, Pallas kernels, attention(): pl.pallas_call(attn_kernel, grid_spec=pltpu.PrefetchScalarGridSpec(num_sc...  12.4 us
  transfers between devices with their start and end apart: 1, of which 1 were waited for; matrix products, arithmetic and copies ran while one was open for 0% of the time, Pallas kernels for 6%

profile of v6, /device:TPU:0, one launch (start us, length us, event | category | flops | bytes accessed | tf_op | source)
XLA Modules:
  0.0 220.9 jit_solution(9945317674574221124)
XLA Ops:
  0.6 50.7 %proj.1 = (bf16[1024,1024]{1,0:T(8,128)(2,1)}, bf16[4096,512]{1,0:T(8,128)(2,1)}, bf16[1024,2,128]{2,1,0:T(2,128)(2,1)}, bf16[1024,2,128]{2,1,0:T(2,128)(2,1)}, ...) custom-call(bf16[1024,4096]{1,0:T(8,128)(2,1)} %x_ref.3, ...), custom_call_target="tpu_custom_call" | custom-call | flops 12884901888 | bytes 25165824 | tf_op jit(solution)/shard_map/proj/pallas_call | solution.py:269
  51.3 1.3 collective-permute-start
  52.6 12.4 %attn.1 = (bf16[1024,1024]{1,0:T(8,128)(2,1)}, bf16[1024,2,128]{2,1,0:T(2,128)(2,1)}, bf16[1024,2,128]{2,1,0:T(2,128)(2,1)}) custom-call(s32[1024]{0:T(1024)} %pos_smem.1, bf16[1024,1024]{1,0:T(8,128)(2,1)} %get-tuple-element.18.q_ref, s32[8,128]{1,0:T(8,128)} %bitcast.5, bf16[4096,512]{1,0:T(8,128)(2,1)} %get-tuple-element.19.kv_ref, ...), custom_call_target="tpu_custom_call" | custom-call | flops 5368709120 | bytes 8388608 | tf_op jit(solution)/shard_map/attn/pallas_call | solution.py:399
  65.0 1.4 collective-permute-done.third_ref
  66.3 151.0 %out_proj.1 = (bf16[896,4096]{1,0:T(8,128)(2,1)S(1)}, bf16[1024,4096]{1,0:T(8,128)(2,1)S(1)}, bf16[128,1024]{1,0:T(8,128)(2,1)S(1)}, f32[128,4096]{1,0:T(8,128)S(1)}) custom-call(bf16[1024,1024]{1,0:T(8,128)(2,1)} %get-tuple-element.22.o_ref, bf16[128,4096]{1,0:T(8,128)(2,1)} %get-tuple-element.23.fl_ref, bf16[128,4096]{1,0:T(8,128)(2,1)} %get-tuple-element.24.fr_ref, ...), custom_call_target="tpu_custom_call" | custom-call | tf_op jit(solution)/shard_map/out_proj/pallas_call | solution.py:710
  217.3 3.4 %settle.1 = bf16[1024,4096]{1,0:T(8,128)(2,1)} custom-call(bf16[896,4096]{1,0:T(8,128)(2,1)S(1)} %get-tuple-element.27.src_ref, bf16[1024,4096]{1,0:T(8,128)(2,1)S(1)} %get-tuple-element.28.w_ref, bf16[128,1024]{1,0:T(8,128)(2,1)S(1)} %get-tuple-element.29.o_ref, f32[128,4096]{1,0:T(8,128)S(1)} %get-tuple-element.30.acc_ref), custom_call_target="tpu_custom_call" | custom-call | tf_op jit(solution)/shard_map/settle/pallas_call | solution.py:755
Async XLA Ops:
  51.3 15.0 %collective-permute-start = (bf16[64,4096]{1,0:T(8,128)(2,1)}, bf16[64,4096]{1,0:T(8,128)(2,1)}, u32[]{:S(2)}, u32[]{:S(2)}) collective-permute-start(bf16[64,4096]{1,0:T(8,128)(2,1)} %get-tuple-element.25.fara_ref), channel_id=1, source_target_pairs={{4,0},{8,12},{5,1},{9,13},{6,2},{10,14},{7,3},{11,15},{20,16},{24,... | collective-permute-start | bytes 1572872 | tf_op jit(solution)/shard_map/ppermute | solution.py:770

commit v7 on v5

--- a/solution.py
+++ b/solution.py
@@ -297,89 +297,121 @@
     )(x, gain.reshape(1, width), w_k, w_v, w_q, w_o, pos.reshape(rows // HEAD, HEAD), inv_freq.reshape(1, HEAD // 2))
 
 
-def attn_kernel(pos_smem, q_ref, pos_ref, kv_ref, k_ref, v_ref, o_ref, k_out_ref, v_out_ref, kbuf, vbuf, in_sem, out_sem):
-    blk = pl.program_id(0)
+def attn_kernel(pos_smem, q_ref, pos_ref, kv_hbm, k_ref, v_ref, o_ref, k_out_ref, v_out_ref, kv_ref, kbuf, vbuf, kv_sem, in_sem, out_sem):
+    step, steps = pl.program_id(0), pl.num_programs(0)
+    cp = lax.axis_index("cp")
+    pieces = kv_sem.shape[0]
+    piece = kv_ref.shape[0] // pieces
+    per_step = q_ref.shape[0] // Q_TILE
+    half_blks = piece // Q_TILE
+    kv_cols = kv_ref.shape[1] // 2
+    heads = kv_cols // HEAD
+    group = q_ref.shape[1] // kv_cols
+
+    def kv_load(j):
+        at = pl.ds(j * piece, piece)
+        return pltpu.make_async_copy(kv_hbm.at[at], kv_ref.at[at], kv_sem.at[j])
 
     cache = ((k_ref, kbuf, k_out_ref), (v_ref, vbuf, v_out_ref))
     loads = [pltpu.make_async_copy(src, buf, in_sem.at[i]) for i, (src, buf, _) in enumerate(cache)]
     stores = [pltpu.make_async_copy(buf, dst, out_sem.at[i]) for i, (_, buf, dst) in enumerate(cache)]
 
-    @pl.when(blk == 0)
-    def _():
+    @pl.when(step == 0)
+    def _():
+        for j in range(pieces):
+            kv_load(j).start()
         for c in loads:
             c.start()
-
-    @pl.when(blk == 2)
-    def _():
+        for j in range(pieces):
+            @pl.when(j <= cp)
+            def _(j=j):
+                kv_load(j).wait()
+
+    @pl.when(step == steps // 2)
+    def _():
+        for j in range(pieces):
+            @pl.when(j > cp)
+            def _(j=j):
+                kv_load(j).wait()
         for c, d in zip(loads, stores):
             c.wait()
             d.start()
 
-    half_blks = pl.num_programs(0) // 2
-    piece = half_blks * Q_TILE
-    cp = lax.axis_index("cp")
-    q_rows = Q_TILE
-    kv_cols = kv_ref.shape[1] // 2
-    heads = kv_cols // HEAD
-    group = q_ref.shape[1] // kv_cols
-    pieces = kv_ref.shape[0] // piece
-    g0 = jnp.where(blk < half_blks, cp * piece + blk * Q_TILE, (pieces - 1 - cp) * piece + (blk - half_blks) * Q_TILE)
-    low = (g0 - pos_smem[blk * Q_TILE]) // Q_TILE
-    tok_1 = g0 + lax.broadcasted_iota(jnp.int32, (q_rows, 1), 0)
-    tok = jnp.concatenate([tok_1] * group, axis=0)
+    factor = HEAD ** -0.5 * 1.4426950408889634
+    wide = 2 * Q_TILE
     pos_cols = jnp.transpose(pos_ref[...].astype(F32))
-    mine = lax.broadcasted_iota(jnp.int32, pos_cols.shape, 1) == blk
-    pos_1 = jnp.sum(jnp.where(mine, pos_cols, 0.0), axis=1, keepdims=True).astype(jnp.int32)
-    first = jnp.concatenate([tok_1 - pos_1] * group, axis=0)
-    factor = HEAD ** -0.5 * 1.4426950408889634
-
-    def head_q(n):
-        return jnp.concatenate([q_ref[:, (n * group + g) * HEAD:(n * group + g + 1) * HEAD] for g in range(group)], axis=0)
-
-    def scores(n, q, start, width):
-        keys = kv_ref[pl.ds(pl.multiple_of(start, Q_TILE), width), n * HEAD:(n + 1) * HEAD]
-        s = lax.dot_general(q, keys, (((1,), (1,)), ((), ())), preferred_element_type=F32)
-        u = start + lax.broadcasted_iota(jnp.int32, (1, width), 1)
-        return jnp.where((u >= first) & (u <= tok), s, -1e30)
-
-    def values(n, start, width):
-        return kv_ref[pl.ds(pl.multiple_of(start, Q_TILE), width), kv_cols + n * HEAD:kv_cols + (n + 1) * HEAD]
-
-    near = jnp.maximum(g0 - Q_TILE, 0)
+
+    def make_block(sub):
+        blk = step * per_step + sub
+        g0 = jnp.where(blk < half_blks, cp * piece + blk * Q_TILE, (pieces - 1 - cp) * piece + (blk - half_blks) * Q_TILE)
+        low = (g0 - pos_smem[blk * Q_TILE]) // Q_TILE
+        tok = g0 + lax.broadcasted_iota(jnp.int32, (Q_TILE, 1), 0)
+        mine = lax.broadcasted_iota(jnp.int32, pos_cols.shape, 1) == blk
+        first = tok - jnp.sum(jnp.where(mine, pos_cols, 0.0), axis=1, keepdims=True).astype(jnp.int32)
+        rows_at = slice(sub * Q_TILE, (sub + 1) * Q_TILE)
+        near = jnp.maximum(g0 - Q_TILE, 0)
+
+        def limit(start, width):
+            u = start + lax.broadcasted_iota(jnp.int32, (1, width), 1)
+            return jnp.where((u >= first) & (u <= tok), 3e38, -1e30)
+
+        def scores(n, start, width, lim):
+            q = jnp.concatenate([q_ref[rows_at, (n * group + g) * HEAD:(n * group + g + 1) * HEAD] for g in range(group)], axis=0)
+            keys = kv_ref[pl.ds(pl.multiple_of(start, Q_TILE), width), n * HEAD:(n + 1) * HEAD]
+            s = lax.dot_general(q, keys, (((1,), (1,)), ((), ())), preferred_element_type=F32)
+            return jnp.minimum(s, jnp.concatenate([lim] * group, axis=0))
+
+        def values(n, start, width):
+            return kv_ref[pl.ds(pl.multiple_of(start, Q_TILE), width), kv_cols + n * HEAD:kv_cols + (n + 1) * HEAD]
+
+        def put(n, acc):
+            out = acc.astype(BF16)
+            for g in range(group):
+                o_ref[rows_at, (n * group + g) * HEAD:(n * group + g + 1) * HEAD] = out[g * Q_TILE:(g + 1) * Q_TILE]
+
+        return low, near, limit, scores, values, put
+
+    def probs(s, m, inv):
+        return (jnp.exp2((s - m) * factor) * inv).astype(BF16)
+
+    blocks = [make_block(sub) for sub in range(per_step)]
     states = []
-    for n in range(heads):
-        s = scores(n, head_q(n), near, 2 * Q_TILE)
-        m = jnp.max(s, axis=-1, keepdims=True)
-        p = jnp.exp2((s - m) * factor)
-        total = jnp.sum(p, axis=-1, keepdims=True)
-        acc = jnp.dot(p.astype(BF16), values(n, near, 2 * Q_TILE), preferred_element_type=F32)
-        states.append((m, total, acc))
-
-    def far(n, i, carry):
-        m, total, acc = carry
-        start = i * Q_TILE
-        s = scores(n, head_q(n), start, Q_TILE)
-        m_new = jnp.maximum(m, jnp.max(s, axis=-1, keepdims=True))
-        old = jnp.exp2((m - m_new) * factor)
-        p = jnp.exp2((s - m_new) * factor)
-        total = total * old + jnp.sum(p, axis=-1, keepdims=True)
-        acc = acc * old + jnp.dot(p.astype(BF16), values(n, start, Q_TILE), preferred_element_type=F32)
-        return m_new, total, acc
-
-    def put(n, state):
-        out = (state[2] / state[1]).astype(BF16)
-        for g in range(group):
-            o_ref[:, (n * group + g) * HEAD:(n * group + g + 1) * HEAD] = out[g * q_rows:(g + 1) * q_rows]
-
-    for n in range(heads):
-        put(n, states[n])
-
-    @pl.when(low < near // Q_TILE)
-    def _():
+    for low, near, limit, scores, values, put in blocks:
+        lim = limit(near, wide)
         for n in range(heads):
-            put(n, lax.fori_loop(low, near // Q_TILE, functools.partial(far, n), states[n]))
-
-    @pl.when(blk == pl.num_programs(0) - 1)
+            s = scores(n, near, wide, lim)
+            m = jnp.max(s, axis=-1, keepdims=True)
+            e = jnp.exp2((s - m) * factor)
+            total = jnp.sum(e, axis=-1, keepdims=True)
+            p = (e * (1.0 / total)).astype(BF16)
+            put(n, jnp.dot(p, values(n, near, wide), preferred_element_type=F32))
+            states.append((m, total))
+
+    for sub, (low, near, limit, scores, values, put) in enumerate(blocks):
+        @pl.when(low < near // Q_TILE)
+        def _(sub=sub, low=low, near=near, limit=limit, scores=scores, values=values, put=put):
+            for n in range(heads):
+                def far_scores(i, n=n):
+                    return scores(n, i * Q_TILE, Q_TILE, limit(i * Q_TILE, Q_TILE))
+
+                def far_sum(i, carry):
+                    m, total = carry
+                    s = far_scores(i)
+                    m_new = jnp.maximum(m, jnp.max(s, axis=-1, keepdims=True))
+                    part = jnp.sum(jnp.exp2((s - m_new) * factor), axis=-1, keepdims=True)
+                    return m_new, total * jnp.exp2((m - m_new) * factor) + part
+
+                m, total = lax.fori_loop(low, near // Q_TILE, far_sum, states[sub * heads + n])
+                inv = 1.0 / total
+
+                def far_pv(i, acc, n=n, m=m, inv=inv):
+                    return acc + jnp.dot(probs(far_scores(i), m, inv), values(n, i * Q_TILE, Q_TILE), preferred_element_type=F32)
+
+                p = probs(scores(n, near, wide, limit(near, wide)), m, inv)
+                acc = jnp.dot(p, values(n, near, wide), preferred_element_type=F32)
+                put(n, lax.fori_loop(low, near // Q_TILE, far_pv, acc))
+
+    @pl.when(step == steps - 1)
     def _():
         for d in stores:
             d.wait()
@@ -388,14 +420,17 @@
 def attention(q, kvg, pos, k, v):
     rows, q_cols = q.shape
     hbm, vmem = pl.BlockSpec(memory_space=HBM), pl.BlockSpec(memory_space=VMEM)
+    dma = pltpu.SemaphoreType.DMA
+    tile = 2 * Q_TILE
+    block = pl.BlockSpec((tile, q_cols), lambda i, *_: (i, 0))
     return pl.pallas_call(
         attn_kernel,
         grid_spec=pltpu.PrefetchScalarGridSpec(
             num_scalar_prefetch=1,
-            grid=(rows // Q_TILE,),
-            in_specs=[pl.BlockSpec((Q_TILE, q_cols), lambda i, *_: (i, 0)), vmem, vmem, hbm, hbm],
-            out_specs=[pl.BlockSpec((Q_TILE, q_cols), lambda i, *_: (i, 0)), hbm, hbm],
-            scratch_shapes=[VMEM(k.shape, BF16), VMEM(v.shape, BF16), pltpu.SemaphoreType.DMA((2,)), pltpu.SemaphoreType.DMA((2,))],
+            grid=(rows // tile,),
+            in_specs=[block, vmem, hbm, hbm, hbm],
+            out_specs=[block, hbm, hbm],
+            scratch_shapes=[VMEM(kvg.shape, BF16), VMEM(k.shape, BF16), VMEM(v.shape, BF16), dma((8,)), dma((2,)), dma((2,))],
         ),
         out_shape=[HBM((rows, q_cols), BF16), HBM(k.shape, BF16), HBM(v.shape, BF16)],
         compiler_params=pltpu.CompilerParams(vmem_limit_bytes=VMEM_MAX),

time: 220 us -> 219 us (level)
  transfers between devices with their start and end apart: 1 -> 1, of which waited for: 1 -> 1; matrix products, arithmetic and copies ran while one was open for 0% -> 0% of each run, Pallas kernels for 5% -> 4%
where the time goes in v7:
time: 219 us
  Pallas kernels  212 us (97%)
  waiting for transfers between devices  4.49 us (2%)
    pallas_call x1, Pallas kernels, out_proj(): pl.pallas_call(out_kernel, in_specs=[pl.BlockSpec(memory_space=HBM)] * 8,...  149 us
    pallas_call x1, Pallas kernels, project(): pl.pallas_call(proj_kernel, in_specs=[hbm] * 8, out_specs=[hbm] * 8, out_...  50.7 us
    pallas_call x1, Pallas kernels, attention(): pl.pallas_call(attn_kernel, grid_spec=pltpu.PrefetchScalarGridSpec(num_sc...  9.23 us
    ppermute x1, waiting for transfers between devices, local_step(): third = lax.ppermute(fara, 'tp', [(1, 0), (2, 3)])  4.49 us
  transfers between devices with their start and end apart: 1, of which 1 were waited for; matrix products, arithmetic and copies ran while one was open for 0% of the time, Pallas kernels for 4%

profile of v7, /device:TPU:0, one launch (start us, length us, event | category | flops | bytes accessed | tf_op | source)
XLA Modules:
  0.0 218.5 jit_solution(6505131528066456776)
XLA Ops:
  0.6 50.7 %proj.1 = (bf16[1024,1024]{1,0:T(8,128)(2,1)}, bf16[4096,512]{1,0:T(8,128)(2,1)}, bf16[1024,2,128]{2,1,0:T(2,128)(2,1)}, bf16[1024,2,128]{2,1,0:T(2,128)(2,1)}, ...) custom-call(bf16[1024,4096]{1,0:T(8,128)(2,1)} %x_ref.3, ...), custom_call_target="tpu_custom_call" | custom-call | flops 12884901888 | bytes 25165824 | tf_op jit(solution)/shard_map/proj/pallas_call | solution.py:269
  51.3 1.3 collective-permute-start
  52.6 9.2 %attn.1 = (bf16[1024,1024]{1,0:T(8,128)(2,1)}, bf16[1024,2,128]{2,1,0:T(2,128)(2,1)}, bf16[1024,2,128]{2,1,0:T(2,128)(2,1)}) custom-call(s32[1024]{0:T(1024)} %pos_smem.1, bf16[1024,1024]{1,0:T(8,128)(2,1)} %get-tuple-element.18.q_ref, s32[8,128]{1,0:T(8,128)} %bitcast.5, bf16[4096,512]{1,0:T(8,128)(2,1)} %get-tuple-element.19.kv_hbm, ...), custom_call_target="tpu_custom_call" | custom-call | flops 5368709120 | bytes 8388608 | tf_op jit(solution)/shard_map/attn/pallas_call | solution.py:426
  61.9 4.5 %collective-permute-done.third_ref = bf16[64,4096]{1,0:T(8,128)(2,1)} collective-permute-done((bf16[64,4096]{1,0:T(8,128)(2,1)}, bf16[64,4096]{1,0:T(8,128)(2,1)}, u32[]{:S(2)}, u32[]{:S(2)}) %collective-permute-start) | collective-permute-done | bytes 524320 | tf_op jit(solution)/shard_map/ppermute | solution.py:797
  66.3 148.6 %out_proj.1 = (bf16[896,4096]{1,0:T(8,128)(2,1)S(1)}, bf16[1024,4096]{1,0:T(8,128)(2,1)S(1)}, bf16[128,1024]{1,0:T(8,128)(2,1)S(1)}, f32[128,4096]{1,0:T(8,128)S(1)}) custom-call(bf16[1024,1024]{1,0:T(8,128)(2,1)} %get-tuple-element.22.o_ref, bf16[128,4096]{1,0:T(8,128)(2,1)} %get-tuple-element.23.fl_ref, bf16[128,4096]{1,0:T(8,128)(2,1)} %get-tuple-element.24.fr_ref, ...), custom_call_target="tpu_custom_call" | custom-call | tf_op jit(solution)/shard_map/out_proj/pallas_call | solution.py:737
  215.0 3.4 %settle.1 = bf16[1024,4096]{1,0:T(8,128)(2,1)} custom-call(bf16[896,4096]{1,0:T(8,128)(2,1)S(1)} %get-tuple-element.27.src_ref, bf16[1024,4096]{1,0:T(8,128)(2,1)S(1)} %get-tuple-element.28.w_ref, bf16[128,1024]{1,0:T(8,128)(2,1)S(1)} %get-tuple-element.29.o_ref, f32[128,4096]{1,0:T(8,128)S(1)} %get-tuple-element.30.acc_ref), custom_call_target="tpu_custom_call" | custom-call | tf_op jit(solution)/shard_map/settle/pallas_call | solution.py:782
Async XLA Ops:
  51.3 15.0 %collective-permute-start = (bf16[64,4096]{1,0:T(8,128)(2,1)}, bf16[64,4096]{1,0:T(8,128)(2,1)}, u32[]{:S(2)}, u32[]{:S(2)}) collective-permute-start(bf16[64,4096]{1,0:T(8,128)(2,1)} %get-tuple-element.25.fara_ref), channel_id=1, source_target_pairs={{4,0},{8,12},{5,1},{9,13},{6,2},{10,14},{7,3},{11,15},{20,16},{24,... | collective-permute-start | bytes 1572872 | tf_op jit(solution)/shard_map/ppermute | solution.py:797
